TPU v7x, 32 devices: a whole 2x2x4 slice. The times are simulated.
32 devices in a mesh: seq: 8 (over z, x), kvh: 4 (over y, core).
Axes of the slice: x: 2, y: 2, z: 4, core: 2. Of those that a mesh axis runs over, the one named last changes fastest.
Arguments:
- queries: bfloat16 [1024, 28, 128], P('seq', 'kvh'), may hold values from -80 to 80
- new_keys: bfloat16 [1024, 4, 128], P('seq', 'kvh'), may hold values from -8 to 8
- cache_keys: bfloat16 [512, 4, 128], P('seq', 'kvh'), may hold values from -1.1953125 to 1.1953125
- window_start: int32 [8], replicated, may hold values from 0 to 512, as said below
- owner_slot: int32 [8], replicated, may hold values from 0 to 511, as said below
Outputs:
- relevance: bfloat16 [1024, 28, 512], P('seq', 'kvh')
- rep_bank: bfloat16 [512, 4, 128], P('seq', 'kvh')
Inputs may be any that keep to these rules, and one draw needn't show every extreme that they name: `window_start`: each window lies inside the new tokens; some window begins at the first new token and some ends at the last. `owner_slot`: the slots are distinct; the first and the last memory block are always among them.
All inputs are finite; a program needn't handle non-finite values.
Results may differ from a plain program's by a relative error of at most 0.0018.
Values may be sent and summed in bfloat16 or wider, within the bound.
No kernel may reach another device: no remote copies, remote signals or barrier semaphores. Data moves between devices by JAX's collectives and lax.ppermute only.
A program may use at most 64 MiB of HBM per device.

v0:
```python
import math

import jax
import jax.numpy as jnp
from jax import lax
from jax.sharding import PartitionSpec as P

BLK = 128
WIN = 512


def row_scores(query_rows, key_rows):
    return lax.dot_general(
        query_rows, key_rows, (((1,), (1,)), ((), ())), preferred_element_type=jnp.float32
    )


def per_device(queries, new_keys, cache_keys, window_start, owner_slot):
    tok_count, group_size, head_dim = queries.shape
    score_scale = 1.0 / math.sqrt(head_dim)
    query_rows = queries.reshape(tok_count * group_size, head_dim)
    device_index = lax.axis_index("seq")
    keys_all = lax.all_gather(new_keys, "seq", axis=0, tiled=True)
    key_flat = keys_all[:, 0, :]
    total_tokens = key_flat.shape[0]
    block_count = total_tokens // BLK
    group_blocks = math.gcd(block_count, 8)
    position = device_index * tok_count + jnp.arange(tok_count, dtype=jnp.int32)
    row_position = jnp.repeat(position, group_size)
    inside = (row_position[:, None] >= window_start[None, :]) & (
        row_position[:, None] < window_start[None, :] + WIN
    )
    inside = inside.astype(jnp.float32)
    key_groups = key_flat.reshape(block_count // group_blocks, group_blocks * BLK, head_dim)
    inside_groups = inside.reshape(
        query_rows.shape[0], block_count // group_blocks, group_blocks
    ).transpose(1, 0, 2)

    def group_sums(members):
        key_part, mask_part = members
        scores = row_scores(query_rows, key_part) * score_scale
        scores = scores.reshape(query_rows.shape[0], group_blocks, BLK)
        softmax_weights = jax.nn.softmax(scores, axis=-1)
        return jnp.einsum("rgk,rg->gk", softmax_weights, mask_part)

    colsum = lax.map(group_sums, (key_groups, inside_groups)).reshape(block_count, BLK)
    colsum = lax.psum(colsum, "seq")
    weights = colsum / (group_size * WIN)
    representative = jnp.einsum(
        "nr,nrz->nz",
        weights,
        key_flat.reshape(block_count, BLK, head_dim).astype(jnp.float32),
        precision=lax.Precision.HIGHEST,
    ).astype(jnp.bfloat16)
    rep_float = representative.astype(jnp.float32)
    local_blocks = cache_keys.shape[0]
    slot_ids = device_index * local_blocks + jnp.arange(local_blocks, dtype=jnp.int32)
    matches = (owner_slot[:, None] == slot_ids[None, :]).astype(jnp.float32)
    placed = jnp.dot(matches.T, rep_float, precision=lax.Precision.HIGHEST)
    slot_taken = jnp.sum(matches, axis=0) > 0.5
    new_shard = jnp.where(slot_taken[:, None], placed.astype(jnp.bfloat16), cache_keys[:, 0, :])
    totals = (
        row_scores(query_rows, lax.all_gather(new_shard, "seq", axis=0, tiled=True)) * score_scale
    )
    relevance = totals.astype(jnp.bfloat16).reshape(tok_count, group_size, totals.shape[1])
    return (relevance, new_shard[:, None, :])


def solution(mesh):
    return jax.shard_map(
        per_device,
        mesh=mesh,
        in_specs=(P("seq", "kvh", None), P("seq", "kvh", None), P("seq", "kvh", None), P(), P()),
        out_specs=(P("seq", "kvh", None), P("seq", "kvh", None)),
        check_vma=False,
    )
```

profile of v0, /device:TPU:0, one launch (start us, length us, event | category | flops | bytes accessed | tf_op | source)
XLA Modules:
  0.0 238.6 jit_solution(1154057495097289812)
XLA Ops:
  0.6 1.1 copy.14
  1.7 0.1 reshape.33
  1.8 32.8 %all_gather.6 = bf16[1024,1,128]{2,0,1:T(8,128)(2,1)S(1)} all-gather(bf16[128,1,128]{2,0,1:T(8,128)(2,1)} %param.6), channel_id=1, replica_groups=mesh['seq'=8,'kvh'=4] {'seq'}, dimensions={0}, use_global_device_ids=true | all-gather | bytes 294912 | tf_op jit(solution)/shard_map/all_gather | solution.py:23
  34.6 0.6 multiply_bitcast_fusion
  35.2 0.9 copy.22
  36.1 145.2 %fusion.12 = (f32[896,8]{1,0:T(8,128)S(1)}, f32[896,8,128]{2,1,0:T(8,128)S(1)}) fusion(f32[896,8,128]{2,1,0:T(8,128)S(1)} %bitcast.27), kind=kOutput, calls=%fused_computation.24 | output fusion | flops 1835135 | bytes 7368704 | tf_op jit(solution)/shard_map/while/body/eval_jaxpr/sub | solution.py:43
  181.3 0.0 copy-start.1
  181.3 0.0 copy-start.3
  181.3 0.0 copy-start.2
  181.4 1.2 broadcast_divide_fusion
  182.6 0.1 broadcast_in_dim.28
  182.7 0.2 ge.15
  182.9 0.1 and_bitcast_fusion
  183.0 0.5 fusion.1
  183.5 21.4 %psum.7 = f32[8,128]{1,0:T(8,128)S(1)} all-reduce(f32[8,128]{1,0:T(8,128)S(1)} %bitcast.32), channel_id=1, replica_groups=mesh['seq'=8,'kvh'=4] {'seq'}, use_global_device_ids=true, to_apply=%region_3.4 | all-reduce | flops 1024 | bytes 8192 | tf_op jit(solution)/shard_map/psum | solution.py:47
  204.9 0.3 fusion.13
  205.2 0.1 fusion.8
  205.3 0.3 fusion.4
  205.6 0.0 copy-start
  205.6 30.5 %all_gather.7 = bf16[512,128]{1,0:T(8,128)(2,1)S(1)} all-gather(bf16[64,128]{1,0:T(8,128)(2,1)S(1)} %fusion.4), channel_id=1, replica_groups=mesh['seq'=8,'kvh'=4] {'seq'}, dimensions={0}, use_global_device_ids=true | all-gather | bytes 147456 | tf_op jit(solution)/shard_map/all_gather | solution.py:63
  236.1 0.4 fusion.3
  236.5 0.5 copy.15
  237.0 0.3 reshape.35
  237.3 1.2 copy.16
  (9 shorter events, 0.0 us)
Async XLA Ops:
  181.3 1.6 copy-start.1
  181.3 23.9 %copy-start.3 = (s32[8]{0:T(128)S(1)}, s32[8]{0:T(128)}, u32[]{:S(2)}) copy-start(s32[8]{0:T(128)} %param.9) | copy-start | bytes 100
  181.3 24.0 %copy-start.2 = (bf16[64,1,128]{2,0,1:T(8,128)(2,1)S(1)}, bf16[64,1,128]{2,0,1:T(8,128)(2,1)}, u32[]{:S(2)}) copy-start(bf16[64,1,128]{2,0,1:T(8,128)(2,1)} %param.7) | copy-start | bytes 49156
  205.6 33.0 %copy-start = (bf16[64,128]{1,0:T(8,128)(2,1)}, bf16[64,128]{1,0:T(8,128)(2,1)S(1)}, u32[]{:S(2)}) copy-start(bf16[64,128]{1,0:T(8,128)(2,1)S(1)} %fusion.4) | copy-start | bytes 49156
where the time goes:
time: 239 us
  other arithmetic  147 us (62%)
  blocking collectives  84.7 us (35%)
  local copies, waits for them, and re-layouts  4.46 us (2%)
    sub x1, other arithmetic, group_sums(): softmax_weights = jax.nn.softmax(scores, axis=-1)  145 us
    all_gather x1, blocking collectives, per_device(): keys_all = lax.all_gather(new_keys, 'seq', axis=0, tiled=True)  32.8 us
    all_gather x1, blocking collectives, per_device(): lax.all_gather(new_shard, 'seq', axis=0, tiled=True)  30.5 us
    psum x1, blocking collectives, per_device(): colsum = lax.psum(colsum, 'seq')  21.4 us

commit v1 on v0

v1 whole, which is shorter than its diff:
```python
import functools
import math

import jax
import jax.numpy as jnp
from jax import lax
from jax.experimental import pallas as pl
from jax.experimental.pallas import tpu as pltpu
from jax.sharding import PartitionSpec as P

BLK = 128
WIN = 512
PACK = 16

VMEM = pl.BlockSpec(memory_space=pltpu.VMEM)
SMEM = pl.BlockSpec(memory_space=pltpu.SMEM)


def nt_dot(left, right):
    return lax.dot_general(
        left, right, (((1,), (1,)), ((), ())), preferred_element_type=jnp.float32
    )


def lead_rows(parts):
    return PACK * pl.cdiv(parts, PACK)


def score_kernel(parts, scale, own_ref, mate_ref, mask_ref, *refs):
    key_refs = refs[:parts]
    rep_ref, load_ref = refs[parts:]
    group, tok, _ = own_ref.shape
    bank_rows = key_refs[0].shape[0] - BLK
    here = lax.axis_index("seq") // 2
    lead = lead_rows(parts)
    rep_ref[...] = jnp.zeros_like(rep_ref)
    load_ref[pl.ds(0, lead), :] = jnp.zeros((lead, load_ref.shape[1]), load_ref.dtype)
    for part in range(parts):
        slot = here ^ part
        keys = key_refs[part][pl.ds(0, BLK), :]
        total = jnp.zeros((BLK, tok), jnp.float32)
        for side, query_ref in enumerate((own_ref, mate_ref)):
            inside = mask_ref[side, pl.ds(slot, 1), :]
            for head in range(group):
                scores = nt_dot(keys, query_ref[head])
                top = jnp.max(scores, axis=0, keepdims=True)
                grown = jnp.exp2((scores - top) * scale)
                total += grown * (inside / jnp.sum(grown, axis=0, keepdims=True))
        column = jnp.sum(total, axis=1, keepdims=True)
        rep_ref[pl.ds(slot, 1), :] = jnp.sum(
            column * keys.astype(jnp.float32), axis=0, keepdims=True
        )
        start = pl.multiple_of(lead + slot * bank_rows, PACK)
        load_ref[pl.ds(start, bank_rows), :] = key_refs[part][pl.ds(BLK, bank_rows), :]


def bank_kernel(parts, scale, query_ref, own_ref, mate_ref, slot_ref, rel_ref, bank_ref, work_ref, full_ref):
    rows = bank_ref.shape[0]
    lead = lead_rows(parts)
    me = lax.axis_index("seq")

    @pl.when(pl.program_id(0) == 0)
    def _():
        for side, ref in enumerate((own_ref, mate_ref)):
            lane = (me % 2) ^ side
            for part in range(parts):
                start = pl.multiple_of((2 * part + lane) * rows, rows)
                work_ref[pl.ds(start, rows), :] = ref[pl.ds(lead + part * rows, rows), :].astype(
                    jnp.float32
                )
        for side, ref in enumerate((own_ref, mate_ref)):
            lane = (me % 2) ^ side
            fresh = ref[pl.ds(0, lead), :].astype(jnp.float32)
            for part in range(parts):
                work_ref[pl.ds(slot_ref[2 * part + lane], 1), :] = fresh[part : part + 1]
        full_ref[...] = work_ref[...].astype(jnp.bfloat16)
        bank_ref[...] = full_ref[pl.ds(pl.multiple_of(me * rows, rows), rows), :]

    rel_ref[0] = (nt_dot(query_ref[0], full_ref[...]) * scale).astype(jnp.bfloat16)


def per_device(count, queries, new_keys, cache_keys, window_start, owner_slot):
    tok, group, head_dim = queries.shape
    rows = cache_keys.shape[0]
    parts = count // 2
    assert tok == BLK and count == 1 << (count.bit_length() - 1)
    score_scale = 1.0 / math.sqrt(head_dim)

    def swap(value, mask):
        return lax.ppermute(value, "seq", [(i, i ^ mask) for i in range(count)])

    own = queries.transpose(1, 0, 2)
    mate = swap(own, 1)
    packed = jnp.concatenate([new_keys[:, 0, :], cache_keys[:, 0, :]], axis=0)
    pieces = [packed] + [swap(packed, 2 * k) for k in range(1, parts)]

    me = lax.axis_index("seq")
    sides = jnp.stack([me, me ^ 1])
    position = sides[:, None] * tok + jnp.arange(tok, dtype=jnp.int32)
    starts = window_start.reshape(parts, 2)
    starts = jnp.where(me % 2 == 0, starts[:, 0], starts[:, 1])
    inside = (position[:, None, :] >= starts[None, :, None]) & (
        position[:, None, :] < starts[None, :, None] + WIN
    )
    inside = inside.astype(jnp.float32)

    partial, load = pl.pallas_call(
        functools.partial(score_kernel, parts, score_scale * math.log2(math.e)),
        out_shape=(
            jax.ShapeDtypeStruct((8 * pl.cdiv(parts, 8), head_dim), jnp.float32),
            jax.ShapeDtypeStruct((lead_rows(parts) + parts * rows, head_dim), jnp.bfloat16),
        ),
        in_specs=[VMEM] * (3 + parts),
        out_specs=(VMEM, VMEM),
        name="scores",
    )(own, mate, inside, *pieces)

    step = 2
    while step < count:
        partial = partial + swap(partial, step)
        step *= 2
    fresh = (partial[:parts] * (1.0 / (group * WIN))).astype(jnp.bfloat16)
    load = lax.dynamic_update_slice(load, fresh, (0, 0))
    other = swap(load, 1)

    relevance, bank = pl.pallas_call(
        functools.partial(bank_kernel, parts, score_scale),
        grid=(group,),
        out_shape=(
            jax.ShapeDtypeStruct((group, tok, count * rows), jnp.bfloat16),
            jax.ShapeDtypeStruct((rows, head_dim), jnp.bfloat16),
        ),
        in_specs=[
            pl.BlockSpec((1, tok, head_dim), lambda h: (h, 0, 0)),
            VMEM,
            VMEM,
            SMEM,
        ],
        out_specs=(
            pl.BlockSpec((1, tok, count * rows), lambda h: (h, 0, 0)),
            pl.BlockSpec((rows, head_dim), lambda h: (0, 0)),
        ),
        scratch_shapes=[
            pltpu.VMEM((count * rows, head_dim), jnp.float32),
            pltpu.VMEM((count * rows, head_dim), jnp.bfloat16),
        ],
        name="bank",
    )(own, load, other, owner_slot)
    return (relevance.transpose(1, 0, 2), bank[:, None, :])


def solution(mesh):
    return jax.shard_map(
        functools.partial(per_device, mesh.shape["seq"]),
        mesh=mesh,
        in_specs=(P("seq", "kvh", None), P("seq", "kvh", None), P("seq", "kvh", None), P(), P()),
        out_specs=(P("seq", "kvh", None), P("seq", "kvh", None)),
        check_vma=False,
    )
```

time: 239 us -> 38.6 us (0.16)
  other arithmetic: 147 us -> 3.02 us
  blocking collectives: 84.7 us -> 0 us
  starting transfers between devices: 0 us -> 12.5 us
  waiting for transfers between devices: 0 us -> 11.3 us
  Pallas kernels: 0 us -> 8.4 us
  local copies, waits for them, and re-layouts: 4.46 us -> 2.01 us
    sub x1 -> x0, other arithmetic: 145 us -> none  [group_sums(): softmax_weights = jax.nn.softmax(scores, axis=-1)]
    all_gather x2 -> x0, blocking collectives: 63.3 us -> none  [the longest x1 32.8 us: per_device(): keys_all = lax.all_gather(new_keys, 'seq', axis=0, tiled=True)]
    psum x1 -> x0, blocking collectives: 21.4 us -> none  [per_device(): colsum = lax.psum(colsum, 'seq')]
    ppermute x0 -> x7, starting transfers between devices: none -> 12.5 us  [swap(): return lax.ppermute(value, 'seq', [(i, i ^ mask) for i in range(count)])]
    ppermute x0 -> x7, waiting for transfers between devices: none -> 11.3 us  [swap(): return lax.ppermute(value, 'seq', [(i, i ^ mask) for i in range(count)])]
    pallas_call x0 -> x2, Pallas kernels: none -> 8.4 us  [the longest x1 5.1 us: per_device(): pl.pallas_call(functools.partial(bank_kernel, parts, score_scale), grid=(...]
  transfers between devices with their start and end apart: 0 -> 7, of which waited for: 0 -> 5; matrix products, arithmetic and copies ran while one was open for 0% -> 3% of each run, Pallas kernels for 0% -> 0%
where the time goes in v1:
time: 38.6 us; the launch traced here: 37.9 us
  starting transfers between devices  12.5 us (32%)
  waiting for transfers between devices  11.3 us (29%)
  Pallas kernels  8.4 us (22%)
  other arithmetic  3.02 us (8%)
  local copies, waits for them, and re-layouts  2.01 us (5%)
  between operations  0.67 us (2%)
    ppermute x7, starting transfers between devices, swap(): return lax.ppermute(value, 'seq', [(i, i ^ mask) for i in range(count)])  12.5 us
    ppermute x7, waiting for transfers between devices, swap(): return lax.ppermute(value, 'seq', [(i, i ^ mask) for i in range(count)])  11.3 us
    pallas_call x1, Pallas kernels, per_device(): pl.pallas_call(functools.partial(bank_kernel, parts, score_scale), grid=(...  5.1 us
    pallas_call x1, Pallas kernels, per_device(): pl.pallas_call(functools.partial(score_kernel, parts, score_scale * math....  3.3 us
    unnamed x14, local copies, waits for them, and re-layouts  1.93 us
    concatenate x1, other arithmetic, per_device(): packed = jnp.concatenate([new_keys[:, 0, :], cache_keys[:, 0, :]], axis=0)  0.78 us
  transfers between devices with their start and end apart: 7, of which 5 were waited for; matrix products, arithmetic and copies ran while one was open for 3% of the time, Pallas kernels for 0%

profile of v1, /device:TPU:0, one launch (start us, length us, event | category | flops | bytes accessed | tf_op | source)
XLA Modules:
  0.0 37.9 jit_solution(11117399018598931291)
XLA Ops:
  0.6 0.8 %pad_maximum_fusion.refs_0_ = bf16[192,128]{1,0:T(8,128)(2,1)S(1)} fusion(bf16[64,128]{1,0:T(8,128)(2,1)} %bitcast.11, bf16[128,128]{1,0:T(8,128)(2,1)} %bitcast.10), kind=kLoop, calls=%fused_computation | loop fusion | flops 98304 | bytes 98304 | tf_op jit(solution)/shard_map/concatenate | solution.py:94
  1.4 5.1 %collective-permute-start.3 = (bf16[192,128]{1,0:T(8,128)(2,1)S(1)}, bf16[192,128]{1,0:T(8,128)(2,1)S(1)}, u32[]{:S(2)}, u32[]{:S(2)}) collective-permute-start(bf16[192,128]{1,0:T(8,128)(2,1)S(1)} %pad_maximum_fusion.refs_0_), channel_id=1, source_target_pairs={{0,24},{4,28},{8,16},{12,20},{16,8},{20,12},{24,0},{28,4},{1,25},{... | collective-permute-start | bytes 147464 | tf_op jit(solution)/shard_map/ppermute | solution.py:90
  6.5 0.6 %collective-permute-start.1 = (bf16[192,128]{1,0:T(8,128)(2,1)S(1)}, bf16[192,128]{1,0:T(8,128)(2,1)S(1)}, u32[]{:S(2)}, u32[]{:S(2)}) collective-permute-start(bf16[192,128]{1,0:T(8,128)(2,1)S(1)} %pad_maximum_fusion.refs_0_), channel_id=1, source_target_pairs={{0,8},{4,12},{8,0},{12,4},{16,24},{20,28},{24,16},{28,20},{1,9},{5... | collective-permute-start | bytes 147464 | tf_op jit(solution)/shard_map/ppermute | solution.py:90
  7.1 1.6 %collective-permute-start = (bf16[7,128,128]{2,1,0:T(8,128)(2,1)}, bf16[7,128,128]{2,1,0:T(8,128)(2,1)S(1)}, u32[]{:S(2)}, u32[]{:S(2)}) collective-permute-start(bf16[7,128,128]{2,1,0:T(8,128)(2,1)} %bitcast.7), channel_id=1, source_target_pairs={{0,4},{4,0},{8,12},{12,8},{16,20},{20,16},{24,28},{28,24},{1,5},{5... | collective-permute-start | bytes 688136 | tf_op jit(solution)/shard_map/ppermute | solution.py:90
  8.8 0.1 add_multiply_fusion
  8.8 0.1 iota_add_fusion
  8.9 0.6 %copy-done.6 = s32[8]{0:T(128)S(1)} copy-done((s32[8]{0:T(128)S(1)}, s32[8]{0:T(128)}, u32[]{:S(2)}) %copy-start.6) | copy-done | bytes 56
  9.5 0.1 reshape.61
  9.6 0.2 select_reduce_fusion
  9.8 0.7 %and_convert_fusion.mask_ref = f32[2,4,128]{2,1,0:T(4,128)} fusion(s32[2,128]{1,0:T(2,128)S(1)} %iota_add_fusion, s32[4]{0:T(128)S(1)} %broadcast_add_fusion, s32[4]{0:T(128)S(1)} %select_reduce_fusion), kind=kLoop, calls=%fused_computation.1 | loop fusion | flops 4096 | bytes 5152 | tf_op jit(solution)/shard_map/convert_element_type | solution.py:105
  10.5 1.0 %collective-permute-done.2.refs_2_ = bf16[192,128]{1,0:T(8,128)(2,1)S(1)} collective-permute-done((bf16[192,128]{1,0:T(8,128)(2,1)S(1)}, bf16[192,128]{1,0:T(8,128)(2,1)S(1)}, u32[]{:S(2)}, u32[]{:S(2)}) %collective-permute-start.2) | collective-permute-done | bytes 49184 | tf_op jit(solution)/shard_map/ppermute | solution.py:90
  11.5 2.6 %collective-permute-done.mate_ref = bf16[7,128,128]{2,1,0:T(8,128)(2,1)S(1)} collective-permute-done((bf16[7,128,128]{2,1,0:T(8,128)(2,1)}, bf16[7,128,128]{2,1,0:T(8,128)(2,1)S(1)}, u32[]{:S(2)}, u32[]{:S(2)}) %collective-permute-start) | collective-permute-done | bytes 229408 | tf_op jit(solution)/shard_map/ppermute | solution.py:90
  14.2 0.7 %copy-done = bf16[7,128,128]{2,1,0:T(8,128)(2,1)} copy-done((bf16[7,128,128]{2,1,0:T(8,128)(2,1)}, bf16[7,128,128]{2,1,0:T(8,128)(2,1)S(1)}, u32[]{:S(2)}) %copy-start) | copy-done | bytes 229400
  14.8 3.3 %scores.1 = (f32[8,128]{1,0:T(8,128)}, bf16[272,128]{1,0:T(8,128)(2,1)}) custom-call(bf16[7,128,128]{2,1,0:T(8,128)(2,1)} %bitcast.8, bf16[7,128,128]{2,1,0:T(8,128)(2,1)} %copy-done, f32[2,4,128]{2,1,0:T(4,128)} %and_convert_fusion.mask_ref, bf16[192,128]{1,0:T(8,128)(2,1)} %copy-done.1, bf16[192,128]{1,0:T(8,128)(2,1)} %copy-done.5, ...), custom_call_target="tpu_custom_call" | custom-call | tf_op jit(solution)/shard_map/scores/pallas_call | solution.py:107
  18.1 1.4 %collective-permute-start.4 = (f32[8,128]{1,0:T(8,128)}, f32[8,128]{1,0:T(8,128)S(1)}, u32[]{:S(2)}, u32[]{:S(2)}) collective-permute-start(f32[8,128]{1,0:T(8,128)} %get-tuple-element.7), channel_id=1, source_target_pairs={{0,8},{4,12},{8,0},{12,4},{16,24},{20,28},{24,16},{28,20},{1,9},{5... | collective-permute-start | bytes 12296 | tf_op jit(solution)/shard_map/ppermute | solution.py:90
  19.5 2.4 %collective-permute-done.4 = f32[8,128]{1,0:T(8,128)S(1)} collective-permute-done((f32[8,128]{1,0:T(8,128)}, f32[8,128]{1,0:T(8,128)S(1)}, u32[]{:S(2)}, u32[]{:S(2)}) %collective-permute-start.4) | collective-permute-done | bytes 4128 | tf_op jit(solution)/shard_map/ppermute | solution.py:90
  21.9 0.7 %add.40 = f32[8,128]{1,0:T(8,128)S(1)} add(f32[8,128]{1,0:T(8,128)} %get-tuple-element.7, f32[8,128]{1,0:T(8,128)S(1)} %collective-permute-done.4) | non-fusion elementwise | flops 1024 | bytes 12288 | tf_op jit(solution)/shard_map/add | solution.py:120
  22.6 2.3 %collective-permute-start.5 = (f32[8,128]{1,0:T(8,128)S(1)}, f32[8,128]{1,0:T(8,128)S(1)}, u32[]{:S(2)}, u32[]{:S(2)}) collective-permute-start(f32[8,128]{1,0:T(8,128)S(1)} %add.40), channel_id=1, source_target_pairs={{0,16},{4,20},{8,24},{12,28},{16,0},{20,4},{24,8},{28,12},{1,17},{... | collective-permute-start | bytes 12296 | tf_op jit(solution)/shard_map/ppermute | solution.py:90
  24.9 2.2 %collective-permute-done.5 = f32[8,128]{1,0:T(8,128)S(1)} collective-permute-done((f32[8,128]{1,0:T(8,128)S(1)}, f32[8,128]{1,0:T(8,128)S(1)}, u32[]{:S(2)}, u32[]{:S(2)}) %collective-permute-start.5) | collective-permute-done | bytes 4128 | tf_op jit(solution)/shard_map/ppermute | solution.py:90
  27.1 0.5 %fusion.own_ref = bf16[272,128]{1,0:T(8,128)(2,1)} fusion(bf16[272,128]{1,0:T(8,128)(2,1)} %get-tuple-element.6, f32[8,128]{1,0:T(8,128)S(1)} %add.41), kind=kLoop, calls=%fused_computation.4 | loop fusion | flops 1024 | bytes 3072 | tf_op jit(solution)/shard_map/dynamic_update_slice | solution.py:123
  27.7 1.5 %collective-permute-start.6 = (bf16[272,128]{1,0:T(8,128)(2,1)}, bf16[272,128]{1,0:T(8,128)(2,1)S(1)}, u32[]{:S(2)}, u32[]{:S(2)}) collective-permute-start(bf16[272,128]{1,0:T(8,128)(2,1)} %fusion.own_ref), channel_id=1, source_target_pairs={{0,4},{4,0},{8,12},{12,8},{16,20},{20,16},{24,28},{28,24},{1,5},{5... | collective-permute-start | bytes 208904 | tf_op jit(solution)/shard_map/ppermute | solution.py:90
  29.2 3.0 %collective-permute-done.6.mate_ref = bf16[272,128]{1,0:T(8,128)(2,1)S(1)} collective-permute-done((bf16[272,128]{1,0:T(8,128)(2,1)}, bf16[272,128]{1,0:T(8,128)(2,1)S(1)}, u32[]{:S(2)}, u32[]{:S(2)}) %collective-permute-start.6) | collective-permute-done | bytes 69664 | tf_op jit(solution)/shard_map/ppermute | solution.py:90
  32.2 0.6 %copy-done.2 = bf16[272,128]{1,0:T(8,128)(2,1)} copy-done((bf16[272,128]{1,0:T(8,128)(2,1)}, bf16[272,128]{1,0:T(8,128)(2,1)S(1)}, u32[]{:S(2)}) %copy-start.2) | copy-done | bytes 69656
  32.8 5.1 %bank.1 = (bf16[7,128,512]{2,1,0:T(8,128)(2,1)}, bf16[64,128]{1,0:T(8,128)(2,1)}) custom-call(bf16[7,128,128]{2,1,0:T(8,128)(2,1)} %bitcast.9, bf16[272,128]{1,0:T(8,128)(2,1)} %fusion.own_ref, bf16[272,128]{1,0:T(8,128)(2,1)} %copy-done.2, s32[8]{0:T(128)} %slot_ref.1), custom_call_target="tpu_custom_call" | custom-call | tf_op jit(solution)/shard_map/bank/pallas_call | solution.py:126
  (16 shorter events, 0.0 us)
Async XLA Ops:
  1.4 12.7 %copy-start.1 = (bf16[192,128]{1,0:T(8,128)(2,1)}, bf16[192,128]{1,0:T(8,128)(2,1)S(1)}, u32[]{:S(2)}) copy-start(bf16[192,128]{1,0:T(8,128)(2,1)S(1)} %pad_maximum_fusion.refs_0_) | copy-start | bytes 147460
  1.4 9.0 %collective-permute-start.3 = (bf16[192,128]{1,0:T(8,128)(2,1)S(1)}, bf16[192,128]{1,0:T(8,128)(2,1)S(1)}, u32[]{:S(2)}, u32[]{:S(2)}) collective-permute-start(bf16[192,128]{1,0:T(8,128)(2,1)S(1)} %pad_maximum_fusion.refs_0_), channel_id=1, source_target_pairs={{0,24},{4,28},{8,16},{12,20},{16,8},{20,12},{24,0},{28,4},{1,25},{... | collective-permute-start | bytes 147464 | tf_op jit(solution)/shard_map/ppermute | solution.py:90
  6.5 5.0 %collective-permute-start.2 = (bf16[192,128]{1,0:T(8,128)(2,1)S(1)}, bf16[192,128]{1,0:T(8,128)(2,1)S(1)}, u32[]{:S(2)}, u32[]{:S(2)}) collective-permute-start(bf16[192,128]{1,0:T(8,128)(2,1)S(1)} %pad_maximum_fusion.refs_0_), channel_id=1, source_target_pairs={{0,16},{4,20},{8,24},{12,28},{16,0},{20,4},{24,8},{28,12},{1,17},{... | collective-permute-start | bytes 147464 | tf_op jit(solution)/shard_map/ppermute | solution.py:90
  6.5 5.0 %collective-permute-start.1 = (bf16[192,128]{1,0:T(8,128)(2,1)S(1)}, bf16[192,128]{1,0:T(8,128)(2,1)S(1)}, u32[]{:S(2)}, u32[]{:S(2)}) collective-permute-start(bf16[192,128]{1,0:T(8,128)(2,1)S(1)} %pad_maximum_fusion.refs_0_), channel_id=1, source_target_pairs={{0,8},{4,12},{8,0},{12,4},{16,24},{20,28},{24,16},{28,20},{1,9},{5... | collective-permute-start | bytes 147464 | tf_op jit(solution)/shard_map/ppermute | solution.py:90
  7.1 7.0 %collective-permute-start = (bf16[7,128,128]{2,1,0:T(8,128)(2,1)}, bf16[7,128,128]{2,1,0:T(8,128)(2,1)S(1)}, u32[]{:S(2)}, u32[]{:S(2)}) collective-permute-start(bf16[7,128,128]{2,1,0:T(8,128)(2,1)} %bitcast.7), channel_id=1, source_target_pairs={{0,4},{4,0},{8,12},{12,8},{16,20},{20,16},{24,28},{28,24},{1,5},{5... | collective-permute-start | bytes 688136 | tf_op jit(solution)/shard_map/ppermute | solution.py:90
  8.8 0.7 %copy-start.6 = (s32[8]{0:T(128)S(1)}, s32[8]{0:T(128)}, u32[]{:S(2)}) copy-start(s32[8]{0:T(128)} %param.8) | copy-start | bytes 100
  10.5 3.7 %copy-start.3 = (bf16[192,128]{1,0:T(8,128)(2,1)}, bf16[192,128]{1,0:T(8,128)(2,1)S(1)}, u32[]{:S(2)}) copy-start(bf16[192,128]{1,0:T(8,128)(2,1)S(1)} %collective-permute-done.3.refs_3_) | copy-start | bytes 147460
  11.5 2.6 %copy-start.4 = (bf16[192,128]{1,0:T(8,128)(2,1)}, bf16[192,128]{1,0:T(8,128)(2,1)S(1)}, u32[]{:S(2)}) copy-start(bf16[192,128]{1,0:T(8,128)(2,1)S(1)} %collective-permute-done.2.refs_2_) | copy-start | bytes 147460
  11.5 2.6 %copy-start.5 = (bf16[192,128]{1,0:T(8,128)(2,1)}, bf16[192,128]{1,0:T(8,128)(2,1)S(1)}, u32[]{:S(2)}) copy-start(bf16[192,128]{1,0:T(8,128)(2,1)S(1)} %collective-permute-done.1.refs_1_) | copy-start | bytes 147460
  14.1 0.7 %copy-start = (bf16[7,128,128]{2,1,0:T(8,128)(2,1)}, bf16[7,128,128]{2,1,0:T(8,128)(2,1)S(1)}, u32[]{:S(2)}) copy-start(bf16[7,128,128]{2,1,0:T(8,128)(2,1)S(1)} %collective-permute-done.mate_ref) | copy-start | bytes 688132
  18.1 3.8 %collective-permute-start.4 = (f32[8,128]{1,0:T(8,128)}, f32[8,128]{1,0:T(8,128)S(1)}, u32[]{:S(2)}, u32[]{:S(2)}) collective-permute-start(f32[8,128]{1,0:T(8,128)} %get-tuple-element.7), channel_id=1, source_target_pairs={{0,8},{4,12},{8,0},{12,4},{16,24},{20,28},{24,16},{28,20},{1,9},{5... | collective-permute-start | bytes 12296 | tf_op jit(solution)/shard_map/ppermute | solution.py:90
  22.6 4.5 %collective-permute-start.5 = (f32[8,128]{1,0:T(8,128)S(1)}, f32[8,128]{1,0:T(8,128)S(1)}, u32[]{:S(2)}, u32[]{:S(2)}) collective-permute-start(f32[8,128]{1,0:T(8,128)S(1)} %add.40), channel_id=1, source_target_pairs={{0,16},{4,20},{8,24},{12,28},{16,0},{20,4},{24,8},{28,12},{1,17},{... | collective-permute-start | bytes 12296 | tf_op jit(solution)/shard_map/ppermute | solution.py:90
  27.7 4.5 %collective-permute-start.6 = (bf16[272,128]{1,0:T(8,128)(2,1)}, bf16[272,128]{1,0:T(8,128)(2,1)S(1)}, u32[]{:S(2)}, u32[]{:S(2)}) collective-permute-start(bf16[272,128]{1,0:T(8,128)(2,1)} %fusion.own_ref), channel_id=1, source_target_pairs={{0,4},{4,0},{8,12},{12,8},{16,20},{20,16},{24,28},{28,24},{1,5},{5... | collective-permute-start | bytes 208904 | tf_op jit(solution)/shard_map/ppermute | solution.py:90
  32.2 0.6 %copy-start.2 = (bf16[272,128]{1,0:T(8,128)(2,1)}, bf16[272,128]{1,0:T(8,128)(2,1)S(1)}, u32[]{:S(2)}) copy-start(bf16[272,128]{1,0:T(8,128)(2,1)S(1)} %collective-permute-done.6.mate_ref) | copy-start | bytes 208900

commit v2 on v1

v2 whole, which is shorter than its diff:
```python
import functools
import math

import jax
import jax.numpy as jnp
from jax import lax
from jax.experimental import pallas as pl
from jax.experimental.pallas import tpu as pltpu
from jax.sharding import PartitionSpec as P

BLK = 128
WIN = 512
PACK = 16
MIB = 1 << 20

VMEM = pl.BlockSpec(memory_space=pltpu.VMEM)
SMEM = pl.BlockSpec(memory_space=pltpu.SMEM)
HBM = pl.BlockSpec(memory_space=pl.ANY)


def nt_dot(left, right):
    return lax.dot_general(
        left, right, (((1,), (1,)), ((), ())), preferred_element_type=jnp.float32
    )


def lead_rows(parts):
    return PACK * pl.cdiv(parts, PACK)


def partial_rep(scale, own_ref, mate_ref, mask_ref, slot, keys):
    group, tok, _ = own_ref.shape
    total = jnp.zeros((BLK, tok), jnp.float32)
    for side, query_ref in enumerate((own_ref, mate_ref)):
        inside = mask_ref[side, pl.ds(slot, 1), :]
        for head in range(group):
            scores = nt_dot(keys, query_ref[head])
            top = jnp.max(scores, axis=0, keepdims=True)
            grown = jnp.exp2((scores - top) * scale)
            total += grown * (inside / jnp.sum(grown, axis=0, keepdims=True))
    column = jnp.sum(total, axis=1, keepdims=True)
    return jnp.sum(column * keys.astype(jnp.float32), axis=0, keepdims=True)


def early_kernel(parts, ahead, scale, start_ref, slot_ref, own_ref, mate_ref, *refs):
    key_refs = refs[:ahead]
    rep_ref, mask_ref, pick_ref = refs[ahead:]
    tok = own_ref.shape[1]
    me = lax.axis_index("seq")
    here, lane = me // 2, me % 2
    lead = lead_rows(parts)
    token = lax.broadcasted_iota(jnp.int32, (1, tok), 1)
    column = lax.broadcasted_iota(jnp.int32, (1, 2 * lead), 1)
    slots = jnp.full((1, 2 * lead), -1, jnp.int32)
    for part in range(parts):
        for side in range(2):
            where = (me ^ side) * tok + token - start_ref[2 * part + lane]
            mask_ref[side, pl.ds(part, 1), :] = ((where >= 0) & (where < WIN)).astype(jnp.float32)
            slots = jnp.where(
                column == side * lead + part, slot_ref[2 * part + (lane ^ side)], slots
            )
    row = lax.broadcasted_iota(jnp.int32, pick_ref.shape, 0)
    pick_ref[...] = (row == slots).astype(jnp.float32).astype(jnp.bfloat16)
    rep_ref[...] = jnp.zeros_like(rep_ref)
    for part in range(ahead):
        slot = here ^ part
        rep_ref[pl.ds(slot, 1), :] = partial_rep(
            scale, own_ref, mate_ref, mask_ref, slot, key_refs[part][pl.ds(0, BLK), :]
        )


def late_kernel(parts, ahead, scale, own_ref, mate_ref, mask_ref, early_ref, *refs):
    key_refs, rep_ref = refs[:-1], refs[-1]
    here = lax.axis_index("seq") // 2
    rep_ref[...] = early_ref[...]
    for part in range(ahead, parts):
        slot = here ^ part
        rep_ref[pl.ds(slot, 1), :] = partial_rep(
            scale, own_ref, mate_ref, mask_ref, slot, key_refs[part - ahead][pl.ds(0, BLK), :]
        )


def load_kernel(parts, share, *refs):
    rep_refs, key_refs, load_ref = refs[:parts], refs[parts:-1], refs[-1]
    rows = key_refs[0].shape[0] - BLK
    here = lax.axis_index("seq") // 2
    lead = lead_rows(parts)
    sums = [ref[...] for ref in rep_refs]
    while len(sums) > 1:
        sums = [left + right for left, right in zip(sums[::2], sums[1::2])]
    load_ref[pl.ds(0, lead), :] = (sums[0] * share).astype(jnp.bfloat16)
    for part in range(parts):
        start = pl.multiple_of(lead + (here ^ part) * rows, PACK)
        load_ref[pl.ds(start, rows), :] = key_refs[part][pl.ds(BLK, rows), :]


def bank_kernel(parts, scale, query_ref, own_ref, mate_ref, pick_ref, rel_ref, bank_ref, base_ref, rel_work, bank_work, sems):
    group = query_ref.shape[0]
    rows = bank_ref.shape[0]
    lead = lead_rows(parts)
    me = lax.axis_index("seq")
    for side, ref in enumerate((own_ref, mate_ref)):
        lane = (me % 2) ^ side
        for part in range(parts):
            start = pl.multiple_of((2 * part + lane) * rows, PACK)
            base_ref[pl.ds(start, rows), :] = ref[pl.ds(lead + part * rows, rows), :]
    fresh = jnp.concatenate([own_ref[pl.ds(0, lead), :], mate_ref[pl.ds(0, lead), :]], axis=0)
    pick = pick_ref[...]
    placed = jnp.dot(pick, fresh, preferred_element_type=jnp.float32)
    taken = jnp.dot(pick, jnp.ones_like(fresh), preferred_element_type=jnp.float32)
    bank = jnp.where(taken > 0.5, placed, base_ref[...].astype(jnp.float32)).astype(jnp.bfloat16)
    base_ref[...] = bank
    bank_work[...] = base_ref[pl.ds(pl.multiple_of(me * rows, PACK), rows), :]
    copies = [pltpu.make_async_copy(bank_work, bank_ref, sems.at[group])]
    copies[0].start()
    for head in range(group):
        rel_work[head] = (nt_dot(query_ref[head], bank) * scale).astype(jnp.bfloat16)
        copies.append(pltpu.make_async_copy(rel_work.at[head], rel_ref.at[head], sems.at[head]))
        copies[-1].start()
    for copy in copies:
        copy.wait()


def per_device(count, queries, new_keys, cache_keys, window_start, owner_slot):
    tok, group, head_dim = queries.shape
    rows = cache_keys.shape[0]
    parts = count // 2
    ahead = max(parts - 1, 1)
    lead = lead_rows(parts)
    assert tok == BLK and count == 1 << (count.bit_length() - 1)
    score_scale = 1.0 / math.sqrt(head_dim)
    exp_scale = score_scale * math.log2(math.e)

    def swap(value, mask):
        return lax.ppermute(value, "seq", [(i, i ^ mask) for i in range(count)])

    def params(mib):
        return pltpu.CompilerParams(vmem_limit_bytes=mib * MIB)

    own = queries.transpose(1, 0, 2)
    mate = swap(own, 1)
    packed = jnp.concatenate([new_keys[:, 0, :], cache_keys[:, 0, :]], axis=0)
    pieces = [packed] + [swap(packed, 2 * k) for k in range(1, parts)]

    sums = jax.ShapeDtypeStruct((lead, head_dim), jnp.float32)
    small = 8 + parts // 2
    partial, inside, pick = pl.pallas_call(
        functools.partial(early_kernel, parts, ahead, exp_scale),
        out_shape=(
            sums,
            jax.ShapeDtypeStruct((2, parts, tok), jnp.float32),
            jax.ShapeDtypeStruct((count * rows, 2 * lead), jnp.bfloat16),
        ),
        in_specs=[SMEM, SMEM] + [VMEM] * (2 + ahead),
        out_specs=(VMEM, VMEM, VMEM),
        compiler_params=params(small),
        name="early",
    )(window_start, owner_slot, own, mate, *pieces[:ahead])
    partial = pl.pallas_call(
        functools.partial(late_kernel, parts, ahead, exp_scale),
        out_shape=sums,
        in_specs=[VMEM] * (4 + parts - ahead),
        out_specs=VMEM,
        compiler_params=params(small),
        name="late",
    )(own, mate, inside, partial, *pieces[ahead:])

    load = pl.pallas_call(
        functools.partial(load_kernel, parts, 1.0 / (group * WIN)),
        out_shape=jax.ShapeDtypeStruct((lead + parts * rows, head_dim), jnp.bfloat16),
        in_specs=[VMEM] * (2 * parts),
        out_specs=VMEM,
        compiler_params=params(small),
        name="load",
    )(partial, *[swap(partial, 2 * k) for k in range(1, parts)], *pieces)
    other = swap(load, 1)

    relevance, bank = pl.pallas_call(
        functools.partial(bank_kernel, parts, score_scale),
        out_shape=(
            jax.ShapeDtypeStruct((group, tok, count * rows), jnp.bfloat16),
            jax.ShapeDtypeStruct((rows, head_dim), jnp.bfloat16),
        ),
        in_specs=[VMEM] * 4,
        out_specs=(HBM, HBM),
        scratch_shapes=[
            pltpu.VMEM((count * rows, head_dim), jnp.bfloat16),
            pltpu.VMEM((group, tok, count * rows), jnp.bfloat16),
            pltpu.VMEM((rows, head_dim), jnp.bfloat16),
            pltpu.SemaphoreType.DMA((group + 1,)),
        ],
        compiler_params=params(8 + parts),
        name="bank",
    )(own, load, other, pick)
    return (relevance.transpose(1, 0, 2), bank[:, None, :])


def solution(mesh):
    return jax.shard_map(
        functools.partial(per_device, mesh.shape["seq"]),
        mesh=mesh,
        in_specs=(P("seq", "kvh", None), P("seq", "kvh", None), P("seq", "kvh", None), P(), P()),
        out_specs=(P("seq", "kvh", None), P("seq", "kvh", None)),
        check_vma=False,
    )
```

time: 38.6 us -> 28.2 us (0.73); the launches traced: 37.9 us -> 28 us
  Pallas kernels: 8.4 us -> 3.83 us
  other arithmetic: 3.02 us -> 0.81 us
  waiting for transfers between devices: 11.3 us -> 9.18 us
  local copies, waits for them, and re-layouts: 2.01 us -> 0.94 us
    pallas_call x2 -> x4, Pallas kernels: 8.4 us -> 3.83 us  [the longest x1 1.85 us: per_device(): pl.pallas_call(functools.partial(early_kernel, parts, ahead, exp_scale),...]
    ppermute x7 -> x8, waiting for transfers between devices: 11.3 us -> 9.18 us  [swap(): return lax.ppermute(value, 'seq', [(i, i ^ mask) for i in range(count)])]
    unnamed x14 -> x8, local copies, waits for them, and re-layouts: 1.93 us -> 0.94 us
    add x4 -> x0, other arithmetic: 0.76 us -> none  [the longest x2 0.68 us: per_device(): partial = partial + swap(partial, step)]
    convert_element_type x1 -> x0, other arithmetic: 0.67 us -> none  [per_device(): inside = inside.astype(jnp.float32)]
    dynamic_update_slice x1 -> x0, other arithmetic: 0.55 us -> none  [per_device(): load = lax.dynamic_update_slice(load, fresh, (0, 0))]
    ppermute x7 -> x8, starting transfers between devices: 12.5 us -> 12.6 us  [swap(): return lax.ppermute(value, 'seq', [(i, i ^ mask) for i in range(count)])]
  transfers between devices with their start and end apart: 7 -> 8, of which waited for: 5 -> 6; matrix products, arithmetic and copies ran while one was open for 3% -> 3% of each run, Pallas kernels for 0% -> 7%
where the time goes in v2:
time: 28.2 us; the launch traced here: 28 us
  starting transfers between devices  12.6 us (45%)
  waiting for transfers between devices  9.18 us (33%)
  Pallas kernels  3.83 us (14%)
  local copies, waits for them, and re-layouts  0.94 us (3%)
  other arithmetic  0.81 us (3%)
  between operations  0.67 us (2%)
    ppermute x8, starting transfers between devices, swap(): return lax.ppermute(value, 'seq', [(i, i ^ mask) for i in range(count)])  12.6 us
    ppermute x8, waiting for transfers between devices, swap(): return lax.ppermute(value, 'seq', [(i, i ^ mask) for i in range(count)])  9.18 us
    pallas_call x1, Pallas kernels, per_device(): pl.pallas_call(functools.partial(early_kernel, parts, ahead, exp_scale),...  1.85 us
    pallas_call x1, Pallas kernels, per_device(): pl.pallas_call(functools.partial(bank_kernel, parts, score_scale), out_sh...  1.36 us
    unnamed x8, local copies, waits for them, and re-layouts  0.94 us
    concatenate x1, other arithmetic, per_device(): packed = jnp.concatenate([new_keys[:, 0, :], cache_keys[:, 0, :]], axis=0)  0.81 us
    pallas_call x1, Pallas kernels, per_device(): pl.pallas_call(functools.partial(late_kernel, parts, ahead, exp_scale), o...  0.6 us
  transfers between devices with their start and end apart: 8, of which 6 were waited for; matrix products, arithmetic and copies ran while one was open for 3% of the time, Pallas kernels for 7%

profile of v2, /device:TPU:0, one launch (start us, length us, event | category | flops | bytes accessed | tf_op | source)
XLA Modules:
  0.0 28.0 jit_solution(1138099295431130049)
XLA Ops:
  0.6 3.0 %collective-permute-start = (bf16[7,128,128]{2,1,0:T(8,128)(2,1)}, bf16[7,128,128]{2,1,0:T(8,128)(2,1)S(1)}, u32[]{:S(2)}, u32[]{:S(2)}) collective-permute-start(bf16[7,128,128]{2,1,0:T(8,128)(2,1)} %bitcast.5), channel_id=1, source_target_pairs={{0,4},{4,0},{8,12},{12,8},{16,20},{20,16},{24,28},{28,24},{1,5},{5... | collective-permute-start | bytes 688136 | tf_op jit(solution)/shard_map/ppermute | solution.py:135
  3.7 0.8 %pad_maximum_fusion.refs_0_.refs_4_ = bf16[192,128]{1,0:T(8,128)(2,1)S(1)} fusion(bf16[64,128]{1,0:T(8,128)(2,1)} %bitcast.10, bf16[128,128]{1,0:T(8,128)(2,1)} %bitcast.9), kind=kLoop, calls=%fused_computation | loop fusion | flops 98304 | bytes 98304 | tf_op jit(solution)/shard_map/concatenate | solution.py:142
  4.5 2.6 %collective-permute-start.2 = (bf16[192,128]{1,0:T(8,128)(2,1)S(1)}, bf16[192,128]{1,0:T(8,128)(2,1)S(1)}, u32[]{:S(2)}, u32[]{:S(2)}) collective-permute-start(bf16[192,128]{1,0:T(8,128)(2,1)S(1)} %pad_maximum_fusion.refs_0_.refs_4_), channel_id=1, source_target_pairs={{0,16},{4,20},{8,24},{12,28},{16,0},{20,4},{24,8},{28,12},{1,17},{... | collective-permute-start | bytes 147464 | tf_op jit(solution)/shard_map/ppermute | solution.py:135
  7.1 1.6 %collective-permute-start.1 = (bf16[192,128]{1,0:T(8,128)(2,1)S(1)}, bf16[192,128]{1,0:T(8,128)(2,1)S(1)}, u32[]{:S(2)}, u32[]{:S(2)}) collective-permute-start(bf16[192,128]{1,0:T(8,128)(2,1)S(1)} %pad_maximum_fusion.refs_0_.refs_4_), channel_id=1, source_target_pairs={{0,8},{4,12},{8,0},{12,4},{16,24},{20,28},{24,16},{28,20},{1,9},{5... | collective-permute-start | bytes 147464 | tf_op jit(solution)/shard_map/ppermute | solution.py:135
  8.6 0.2 collective-permute-start.3
  8.9 0.8 %collective-permute-done.2.refs_2_.refs_6_ = bf16[192,128]{1,0:T(8,128)(2,1)S(1)} collective-permute-done((bf16[192,128]{1,0:T(8,128)(2,1)S(1)}, bf16[192,128]{1,0:T(8,128)(2,1)S(1)}, u32[]{:S(2)}, u32[]{:S(2)}) %collective-permute-start.2) | collective-permute-done | bytes 49184 | tf_op jit(solution)/shard_map/ppermute | solution.py:135
  9.7 1.5 %collective-permute-done.1.refs_1_.refs_5_ = bf16[192,128]{1,0:T(8,128)(2,1)S(1)} collective-permute-done((bf16[192,128]{1,0:T(8,128)(2,1)S(1)}, bf16[192,128]{1,0:T(8,128)(2,1)S(1)}, u32[]{:S(2)}, u32[]{:S(2)}) %collective-permute-start.1) | collective-permute-done | bytes 49184 | tf_op jit(solution)/shard_map/ppermute | solution.py:135
  11.2 0.0 collective-permute-done.mate_ref
  11.2 0.0 copy-done.2
  11.2 0.0 copy-done.3
  11.2 0.0 copy-start
  11.2 0.9 %copy-done = bf16[128,7,128]{2,0,1:T(8,128)(2,1)S(1)} copy-done((bf16[128,7,128]{2,0,1:T(8,128)(2,1)S(1)}, bf16[128,7,128]{2,0,1:T(8,128)(2,1)}, u32[]{:S(2)}) %copy-start) | copy-done | bytes 229400
  12.1 1.8 %early.1 = (f32[16,128]{1,0:T(8,128)S(1)}, f32[2,4,128]{2,1,0:T(4,128)S(1)}, bf16[512,32]{1,0:T(8,128)(2,1)S(1)}) custom-call(s32[8]{0:T(128)S(1)} %copy-done.2, s32[8]{0:T(128)S(1)} %copy-done.3, bf16[7,128,128]{2,1,0:T(8,128)(2,1)S(1)} %bitcast.6, bf16[7,128,128]{2,1,0:T(8,128)(2,1)S(1)} %collective-permute-done.mate_ref, ...), custom_call_target="tpu_custom_call" | custom-call | tf_op jit(solution)/shard_map/early/pallas_call | solution.py:147
  14.0 0.6 %collective-permute-done.3.refs_0_.refs_7_ = bf16[192,128]{1,0:T(8,128)(2,1)S(1)} collective-permute-done((bf16[192,128]{1,0:T(8,128)(2,1)S(1)}, bf16[192,128]{1,0:T(8,128)(2,1)S(1)}, u32[]{:S(2)}, u32[]{:S(2)}) %collective-permute-start.3) | collective-permute-done | bytes 49184 | tf_op jit(solution)/shard_map/ppermute | solution.py:135
  14.5 0.6 %late.1.refs_0_ = f32[16,128]{1,0:T(8,128)S(1)} custom-call(bf16[7,128,128]{2,1,0:T(8,128)(2,1)S(1)} %bitcast.7, bf16[7,128,128]{2,1,0:T(8,128)(2,1)S(1)} %collective-permute-done.mate_ref, f32[2,4,128]{2,1,0:T(4,128)S(1)} %get-tuple-element.7.mask_ref, f32[16,128]{1,0:T(8,128)S(1)} %get-tuple-element.8.early_ref, ...), custom_call_target="tpu_custom_call" | custom-call | tf_op jit(solution)/shard_map/late/pallas_call | solution.py:159
  15.1 2.5 %collective-permute-start.6 = (f32[16,128]{1,0:T(8,128)S(1)}, f32[16,128]{1,0:T(8,128)S(1)}, u32[]{:S(2)}, u32[]{:S(2)}) collective-permute-start(f32[16,128]{1,0:T(8,128)S(1)} %late.1.refs_0_), channel_id=1, source_target_pairs={{0,24},{4,28},{8,16},{12,20},{16,8},{20,12},{24,0},{28,4},{1,25},{... | collective-permute-start | bytes 24584 | tf_op jit(solution)/shard_map/ppermute | solution.py:135
  17.7 0.0 collective-permute-start.5
  17.7 1.9 %collective-permute-start.4 = (f32[16,128]{1,0:T(8,128)S(1)}, f32[16,128]{1,0:T(8,128)S(1)}, u32[]{:S(2)}, u32[]{:S(2)}) collective-permute-start(f32[16,128]{1,0:T(8,128)S(1)} %late.1.refs_0_), channel_id=1, source_target_pairs={{0,8},{4,12},{8,0},{12,4},{16,24},{20,28},{24,16},{28,20},{1,9},{5... | collective-permute-start | bytes 24584 | tf_op jit(solution)/shard_map/ppermute | solution.py:135
  19.6 1.1 %collective-permute-done.6.refs_3_ = f32[16,128]{1,0:T(8,128)S(1)} collective-permute-done((f32[16,128]{1,0:T(8,128)S(1)}, f32[16,128]{1,0:T(8,128)S(1)}, u32[]{:S(2)}, u32[]{:S(2)}) %collective-permute-start.6) | collective-permute-done | bytes 8224 | tf_op jit(solution)/shard_map/ppermute | solution.py:135
  20.7 1.6 %collective-permute-done.5.refs_2_ = f32[16,128]{1,0:T(8,128)S(1)} collective-permute-done((f32[16,128]{1,0:T(8,128)S(1)}, f32[16,128]{1,0:T(8,128)S(1)}, u32[]{:S(2)}, u32[]{:S(2)}) %collective-permute-start.5) | collective-permute-done | bytes 8224 | tf_op jit(solution)/shard_map/ppermute | solution.py:135
  22.2 0.0 collective-permute-done.4.refs_1_
  22.3 0.7 %collective-permute-start.7 = (bf16[272,128]{1,0:T(8,128)(2,1)S(1)}, bf16[272,128]{1,0:T(8,128)(2,1)S(1)}, u32[]{:S(2)}, u32[]{:S(2)}) collective-permute-start(bf16[272,128]{1,0:T(8,128)(2,1)S(1)} %load.1.own_ref), channel_id=1, source_target_pairs={{0,4},{4,0},{8,12},{12,8},{16,20},{20,16},{24,28},{28,24},{1,5},{5... | collective-permute-start | bytes 208904 | tf_op jit(solution)/shard_map/ppermute | solution.py:135
  23.0 3.7 %collective-permute-done.7.mate_ref = bf16[272,128]{1,0:T(8,128)(2,1)S(1)} collective-permute-done((bf16[272,128]{1,0:T(8,128)(2,1)S(1)}, bf16[272,128]{1,0:T(8,128)(2,1)S(1)}, u32[]{:S(2)}, u32[]{:S(2)}) %collective-permute-start.7) | collective-permute-done | bytes 69664 | tf_op jit(solution)/shard_map/ppermute | solution.py:135
  26.6 1.4 %bank.1 = (bf16[7,128,512]{2,1,0:T(8,128)(2,1)}, bf16[64,128]{1,0:T(8,128)(2,1)}) custom-call(bf16[7,128,128]{2,1,0:T(8,128)(2,1)S(1)} %bitcast.8, bf16[272,128]{1,0:T(8,128)(2,1)S(1)} %load.1.own_ref, bf16[272,128]{1,0:T(8,128)(2,1)S(1)} %collective-permute-done.7.mate_ref, bf16[512,32]{1,0:T(8,128)(2,1)S(1)} %get-tuple-element.9.pick_ref), custom_call_target="tpu_custom_call" | custom-call | tf_op jit(solution)/shard_map/bank/pallas_call | solution.py:178
  (5 shorter events, 0.0 us)
Async XLA Ops:
  0.6 10.5 %collective-permute-start = (bf16[7,128,128]{2,1,0:T(8,128)(2,1)}, bf16[7,128,128]{2,1,0:T(8,128)(2,1)S(1)}, u32[]{:S(2)}, u32[]{:S(2)}) collective-permute-start(bf16[7,128,128]{2,1,0:T(8,128)(2,1)} %bitcast.5), channel_id=1, source_target_pairs={{0,4},{4,0},{8,12},{12,8},{16,20},{20,16},{24,28},{28,24},{1,5},{5... | collective-permute-start | bytes 688136 | tf_op jit(solution)/shard_map/ppermute | solution.py:135
  3.7 7.5 %copy-start.2 = (s32[8]{0:T(128)S(1)}, s32[8]{0:T(128)}, u32[]{:S(2)}) copy-start(s32[8]{0:T(128)} %start_ref.1) | copy-start | bytes 100
  3.7 7.5 %copy-start.3 = (s32[8]{0:T(128)S(1)}, s32[8]{0:T(128)}, u32[]{:S(2)}) copy-start(s32[8]{0:T(128)} %slot_ref.1) | copy-start | bytes 100
  4.5 5.2 %collective-permute-start.2 = (bf16[192,128]{1,0:T(8,128)(2,1)S(1)}, bf16[192,128]{1,0:T(8,128)(2,1)S(1)}, u32[]{:S(2)}, u32[]{:S(2)}) collective-permute-start(bf16[192,128]{1,0:T(8,128)(2,1)S(1)} %pad_maximum_fusion.refs_0_.refs_4_), channel_id=1, source_target_pairs={{0,16},{4,20},{8,24},{12,28},{16,0},{20,4},{24,8},{28,12},{1,17},{... | collective-permute-start | bytes 147464 | tf_op jit(solution)/shard_map/ppermute | solution.py:135
  7.1 4.1 %collective-permute-start.1 = (bf16[192,128]{1,0:T(8,128)(2,1)S(1)}, bf16[192,128]{1,0:T(8,128)(2,1)S(1)}, u32[]{:S(2)}, u32[]{:S(2)}) collective-permute-start(bf16[192,128]{1,0:T(8,128)(2,1)S(1)} %pad_maximum_fusion.refs_0_.refs_4_), channel_id=1, source_target_pairs={{0,8},{4,12},{8,0},{12,4},{16,24},{20,28},{24,16},{28,20},{1,9},{5... | collective-permute-start | bytes 147464 | tf_op jit(solution)/shard_map/ppermute | solution.py:135
  8.6 5.9 %collective-permute-start.3 = (bf16[192,128]{1,0:T(8,128)(2,1)S(1)}, bf16[192,128]{1,0:T(8,128)(2,1)S(1)}, u32[]{:S(2)}, u32[]{:S(2)}) collective-permute-start(bf16[192,128]{1,0:T(8,128)(2,1)S(1)} %pad_maximum_fusion.refs_0_.refs_4_), channel_id=1, source_target_pairs={{0,24},{4,28},{8,16},{12,20},{16,8},{20,12},{24,0},{28,4},{1,25},{... | collective-permute-start | bytes 147464 | tf_op jit(solution)/shard_map/ppermute | solution.py:135
  11.2 0.9 %copy-start = (bf16[128,7,128]{2,0,1:T(8,128)(2,1)S(1)}, bf16[128,7,128]{2,0,1:T(8,128)(2,1)}, u32[]{:S(2)}) copy-start(bf16[128,7,128]{2,0,1:T(8,128)(2,1)} %param.5) | copy-start | bytes 688132
  12.1 2.4 %copy-start.1 = (bf16[128,7,128]{2,0,1:T(8,128)(2,1)S(1)}, bf16[128,7,128]{2,0,1:T(8,128)(2,1)}, u32[]{:S(2)}) copy-start(bf16[128,7,128]{2,0,1:T(8,128)(2,1)} %param.5) | copy-start | bytes 688132
  15.1 5.5 %collective-permute-start.6 = (f32[16,128]{1,0:T(8,128)S(1)}, f32[16,128]{1,0:T(8,128)S(1)}, u32[]{:S(2)}, u32[]{:S(2)}) collective-permute-start(f32[16,128]{1,0:T(8,128)S(1)} %late.1.refs_0_), channel_id=1, source_target_pairs={{0,24},{4,28},{8,16},{12,20},{16,8},{20,12},{24,0},{28,4},{1,25},{... | collective-permute-start | bytes 24584 | tf_op jit(solution)/shard_map/ppermute | solution.py:135
  17.7 4.5 %collective-permute-start.5 = (f32[16,128]{1,0:T(8,128)S(1)}, f32[16,128]{1,0:T(8,128)S(1)}, u32[]{:S(2)}, u32[]{:S(2)}) collective-permute-start(f32[16,128]{1,0:T(8,128)S(1)} %late.1.refs_0_), channel_id=1, source_target_pairs={{0,16},{4,20},{8,24},{12,28},{16,0},{20,4},{24,8},{28,12},{1,17},{... | collective-permute-start | bytes 24584 | tf_op jit(solution)/shard_map/ppermute | solution.py:135
  17.7 4.5 %collective-permute-start.4 = (f32[16,128]{1,0:T(8,128)S(1)}, f32[16,128]{1,0:T(8,128)S(1)}, u32[]{:S(2)}, u32[]{:S(2)}) collective-permute-start(f32[16,128]{1,0:T(8,128)S(1)} %late.1.refs_0_), channel_id=1, source_target_pairs={{0,8},{4,12},{8,0},{12,4},{16,24},{20,28},{24,16},{28,20},{1,9},{5... | collective-permute-start | bytes 24584 | tf_op jit(solution)/shard_map/ppermute | solution.py:135
  22.3 4.4 %collective-permute-start.7 = (bf16[272,128]{1,0:T(8,128)(2,1)S(1)}, bf16[272,128]{1,0:T(8,128)(2,1)S(1)}, u32[]{:S(2)}, u32[]{:S(2)}) collective-permute-start(bf16[272,128]{1,0:T(8,128)(2,1)S(1)} %load.1.own_ref), channel_id=1, source_target_pairs={{0,4},{4,0},{8,12},{12,8},{16,20},{20,16},{24,28},{28,24},{1,5},{5... | collective-permute-start | bytes 208904 | tf_op jit(solution)/shard_map/ppermute | solution.py:135

commit v3 on v2

v3 whole, which is shorter than its diff:
```python
import functools
import math

import jax
import jax.numpy as jnp
from jax import lax
from jax.experimental import pallas as pl
from jax.experimental.pallas import tpu as pltpu
from jax.sharding import PartitionSpec as P

BLK = 128
WIN = 512
PACK = 16
MIB = 1 << 20

VMEM = pl.BlockSpec(memory_space=pltpu.VMEM)
SMEM = pl.BlockSpec(memory_space=pltpu.SMEM)
HBM = pl.BlockSpec(memory_space=pltpu.HBM)


def nt_dot(left, right):
    return lax.dot_general(
        left, right, (((1,), (1,)), ((), ())), preferred_element_type=jnp.float32
    )


def padded(rows, unit):
    return unit * pl.cdiv(rows, unit)


def lead_rows(parts):
    return padded(parts, PACK)


def term_rows(parts):
    return padded(3 * parts, PACK)


def column_sums(scale, query_ref, inside, keys):
    group, tok, _ = query_ref.shape

    def one_head(head, total):
        scores = nt_dot(keys, query_ref[head])
        top = jnp.max(scores, axis=0, keepdims=True)
        grown = jnp.exp2((scores - top) * scale)
        return total + grown * (inside / jnp.sum(grown, axis=0, keepdims=True))

    total = jnp.zeros((BLK, tok), jnp.float32)
    return lax.fori_loop(0, group, one_head, total, unroll=True)


def partial_rep(scale, query_refs, mask_refs, keys):
    total = 0.0
    for query_ref, inside in zip(query_refs, mask_refs):
        total += column_sums(scale, query_ref, inside, keys)
    column = jnp.sum(total, axis=1, keepdims=True)
    return jnp.sum(column * keys.astype(jnp.float32), axis=0, keepdims=True)


def first_kernel(parts, scale, start_ref, slot_ref, query_hbm, key_hbm, rep_ref, mask_ref, pick_ref, query_ref, key_ref, sems):
    tok = query_ref.shape[1]
    copies = [
        pltpu.make_async_copy(key_hbm, key_ref, sems.at[0]),
        pltpu.make_async_copy(query_hbm, query_ref, sems.at[1]),
    ]
    for copy in copies:
        copy.start()
    me = lax.axis_index("seq")
    here, lane = me // 2, me % 2
    lead = lead_rows(parts)
    token = lax.broadcasted_iota(jnp.int32, (1, tok), 1)
    column = lax.broadcasted_iota(jnp.int32, (1, 2 * lead), 1)
    slots = jnp.full((1, 2 * lead), -1, jnp.int32)
    for part in range(parts):
        for side in range(2):
            where = (me ^ side) * tok + token - start_ref[2 * part + lane]
            mask_ref[side, pl.ds(part, 1), :] = ((where >= 0) & (where < WIN)).astype(jnp.float32)
            slots = jnp.where(
                column == side * lead + part, slot_ref[2 * part + (lane ^ side)], slots
            )
    row = lax.broadcasted_iota(jnp.int32, pick_ref.shape, 0)
    pick_ref[...] = (row == slots).astype(jnp.float32).astype(jnp.bfloat16)
    rep_ref[...] = jnp.zeros_like(rep_ref)
    for copy in copies:
        copy.wait()
    inside = mask_ref[0, pl.ds(here, 1), :]
    rep_ref[pl.ds(here, 1), :] = partial_rep(scale, [query_ref], [inside], key_ref[...])


def step_kernel(sides, members, scale, mask_ref, prior_ref, *refs):
    query_refs, key_refs, rep_ref = refs[: len(sides)], refs[len(sides) : -1], refs[-1]
    here = lax.axis_index("seq") // 2
    rep_ref[...] = prior_ref[...]
    for part, key_ref in zip(members, key_refs):
        slot = here ^ part
        inside = [mask_ref[side, pl.ds(slot, 1), :] for side in sides]
        rep_ref[pl.ds(slot, 1), :] += partial_rep(scale, query_refs, inside, key_ref[...])


def last_kernel(parts, scale, mask_ref, prior_ref, own_ref, mate_ref, key_ref, cache_ref, sum_ref, rep_ref):
    slot = (lax.axis_index("seq") // 2) ^ (parts - 1)
    rep_ref[...] = prior_ref[...]
    inside = [mask_ref[side, pl.ds(slot, 1), :] for side in range(2)]
    rep_ref[pl.ds(slot, 1), :] += partial_rep(scale, [own_ref, mate_ref], inside, key_ref[...])
    rest = rep_ref[pl.ds(0, parts), :]
    terms = []
    for _ in range(3):
        terms.append(rest.astype(jnp.bfloat16).astype(jnp.float32))
        rest = rest - terms[-1]
    spare = term_rows(parts) - 3 * parts
    if spare:
        terms.append(jnp.zeros((spare, rest.shape[1]), jnp.float32))
    sum_ref[pl.ds(0, term_rows(parts)), :] = jnp.concatenate(terms, axis=0).astype(jnp.bfloat16)
    sum_ref[pl.ds(term_rows(parts), cache_ref.shape[0]), :] = cache_ref[...]


def load_kernel(parts, share, *refs):
    sum_refs, load_ref = refs[:-1], refs[-1]
    terms = term_rows(parts)
    rows = sum_refs[0].shape[0] - terms
    here = lax.axis_index("seq") // 2
    lead = lead_rows(parts)
    sums = []
    for ref in sum_refs:
        wide = ref[pl.ds(0, terms), :].astype(jnp.float32)
        sums.append(wide[:parts] + (wide[parts : 2 * parts] + wide[2 * parts : 3 * parts]))
    while len(sums) > 1:
        sums = [left + right for left, right in zip(sums[::2], sums[1::2])]
    fresh = [sums[0] * share]
    if lead > parts:
        fresh.append(jnp.zeros((lead - parts, fresh[0].shape[1]), jnp.float32))
    load_ref[pl.ds(0, lead), :] = jnp.concatenate(fresh, axis=0).astype(jnp.bfloat16)
    for part in range(parts):
        start = pl.multiple_of(lead + (here ^ part) * rows, PACK)
        load_ref[pl.ds(start, rows), :] = sum_refs[part][pl.ds(terms, rows), :]


def bank_kernel(parts, scale, query_ref, own_ref, mate_ref, pick_ref, rel_ref, bank_ref, base_ref, rel_work, bank_work, sems):
    group = query_ref.shape[0]
    rows = bank_ref.shape[0]
    lead = lead_rows(parts)
    me = lax.axis_index("seq")
    for side, ref in enumerate((own_ref, mate_ref)):
        lane = (me % 2) ^ side
        for part in range(parts):
            start = pl.multiple_of((2 * part + lane) * rows, PACK)
            base_ref[pl.ds(start, rows), :] = ref[pl.ds(lead + part * rows, rows), :]
    fresh = jnp.concatenate([own_ref[pl.ds(0, lead), :], mate_ref[pl.ds(0, lead), :]], axis=0)
    pick = pick_ref[...]
    placed = jnp.dot(pick, fresh, preferred_element_type=jnp.float32)
    taken = jnp.dot(pick, jnp.ones_like(fresh), preferred_element_type=jnp.float32)
    bank = jnp.where(taken > 0.5, placed, base_ref[...].astype(jnp.float32)).astype(jnp.bfloat16)
    base_ref[...] = bank
    bank_work[...] = base_ref[pl.ds(pl.multiple_of(me * rows, PACK), rows), :]
    copies = [pltpu.make_async_copy(bank_work, bank_ref, sems.at[group])]
    copies[0].start()
    for head in range(group):
        rel_work[head] = (nt_dot(query_ref[head], bank) * scale).astype(jnp.bfloat16)
        copies.append(pltpu.make_async_copy(rel_work.at[head], rel_ref.at[head], sems.at[head]))
        copies[-1].start()
    for copy in copies:
        copy.wait()


def per_device(count, queries, new_keys, cache_keys, window_start, owner_slot):
    tok, group, head_dim = queries.shape
    rows = cache_keys.shape[0]
    parts = count // 2
    lead = lead_rows(parts)
    assert tok == BLK and count == 1 << (count.bit_length() - 1) and count > 2
    score_scale = 1.0 / math.sqrt(head_dim)
    exp_scale = score_scale * math.log2(math.e)

    def swap(value, mask):
        return lax.ppermute(value, "seq", [(i, i ^ mask) for i in range(count)])

    def shape(rows_of, dtype):
        return jax.ShapeDtypeStruct((rows_of, head_dim), dtype)

    params = pltpu.CompilerParams(vmem_limit_bytes=(8 + parts) * MIB)
    asked = queries.transpose(1, 0, 2)
    mate = swap(asked, 1)
    keys = new_keys[:, 0, :]
    pieces = [keys] + [swap(keys, 2 * k) for k in range(1, parts)]

    sums = shape(padded(parts, 8), jnp.float32)
    partial, inside, pick, own, held = pl.pallas_call(
        functools.partial(first_kernel, parts, exp_scale),
        out_shape=(
            sums,
            jax.ShapeDtypeStruct((2, parts, tok), jnp.float32),
            jax.ShapeDtypeStruct((count * rows, 2 * lead), jnp.bfloat16),
            jax.ShapeDtypeStruct(asked.shape, jnp.bfloat16),
            jax.ShapeDtypeStruct(keys.shape, jnp.bfloat16),
        ),
        in_specs=[SMEM, SMEM, HBM, HBM],
        out_specs=(VMEM,) * 5,
        scratch_shapes=[pltpu.SemaphoreType.DMA((2,))],
        compiler_params=params,
        name="first",
    )(window_start, owner_slot, asked, keys)
    pieces[0] = held

    def step(partial, sides, members, label):
        asking = [(own, mate)[side] for side in sides]
        return pl.pallas_call(
            functools.partial(step_kernel, sides, members, exp_scale),
            out_shape=sums,
            in_specs=[VMEM] * (2 + len(sides) + len(members)),
            out_specs=VMEM,
            compiler_params=params,
            name=label,
        )(inside, partial, *asking, *[pieces[part] for part in members])

    for part in reversed(range(1, parts - 1)):
        partial = step(partial, (0,), (part,), "own_step")
    partial = step(partial, (1,), tuple(range(parts - 1)), "mate_step")
    partial = pl.pallas_call(
        functools.partial(last_kernel, parts, exp_scale),
        out_shape=shape(term_rows(parts) + rows, jnp.bfloat16),
        in_specs=[VMEM] * 6,
        out_specs=VMEM,
        scratch_shapes=[pltpu.VMEM(sums.shape, sums.dtype)],
        compiler_params=params,
        name="last",
    )(inside, partial, own, mate, pieces[-1], cache_keys[:, 0, :])

    load = pl.pallas_call(
        functools.partial(load_kernel, parts, 1.0 / (group * WIN)),
        out_shape=shape(lead + parts * rows, jnp.bfloat16),
        in_specs=[VMEM] * parts,
        out_specs=VMEM,
        compiler_params=params,
        name="load",
    )(partial, *[swap(partial, 2 * k) for k in range(1, parts)])
    other = swap(load, 1)

    relevance, bank = pl.pallas_call(
        functools.partial(bank_kernel, parts, score_scale),
        out_shape=(
            jax.ShapeDtypeStruct((group, tok, count * rows), jnp.bfloat16),
            jax.ShapeDtypeStruct((rows, head_dim), jnp.bfloat16),
        ),
        in_specs=[VMEM] * 4,
        out_specs=(HBM, HBM),
        scratch_shapes=[
            pltpu.VMEM((count * rows, head_dim), jnp.bfloat16),
            pltpu.VMEM((group, tok, count * rows), jnp.bfloat16),
            pltpu.VMEM((rows, head_dim), jnp.bfloat16),
            pltpu.SemaphoreType.DMA((group + 1,)),
        ],
        compiler_params=params,
        name="bank",
    )(own, load, other, pick)
    return (relevance.transpose(1, 0, 2), bank[:, None, :])


def solution(mesh):
    return jax.shard_map(
        functools.partial(per_device, mesh.shape["seq"]),
        mesh=mesh,
        in_specs=(P("seq", "kvh", None), P("seq", "kvh", None), P("seq", "kvh", None), P(), P()),
        out_specs=(P("seq", "kvh", None), P("seq", "kvh", None)),
        check_vma=False,
    )
```

time: 28.2 us -> 27.9 us (0.989)
  waiting for transfers between devices: 9.18 us -> 7.71 us
  Pallas kernels: 3.83 us -> 5.05 us
  other arithmetic: 0.81 us -> 0 us
  local copies, waits for them, and re-layouts: 0.94 us -> 1.71 us
    ppermute x8, waiting for transfers between devices: 9.18 us -> 7.71 us  [swap(): return lax.ppermute(value, 'seq', [(i, i ^ mask) for i in range(count)])]
    pallas_call x2 -> x5, Pallas kernels: 2.45 us -> 3.67 us  [the longest x3 1.65 us: step(): pl.pallas_call(functools.partial(step_kernel, sides, members, exp_scale),...]
    concatenate x1 -> x0, other arithmetic: 0.81 us -> none  [per_device(): packed = jnp.concatenate([new_keys[:, 0, :], cache_keys[:, 0, :]], axis=0)]
    unnamed x8 -> x10, local copies, waits for them, and re-layouts: 0.94 us -> 1.71 us
  transfers between devices with their start and end apart: 8 -> 8, of which waited for: 6 -> 4; matrix products, arithmetic and copies ran while one was open for 3% -> 0% of each run, Pallas kernels for 7% -> 11%
where the time goes in v3:
time: 27.9 us; the launch traced here: 27.7 us
  starting transfers between devices  12.5 us (45%)
  waiting for transfers between devices  7.71 us (28%)
  Pallas kernels  5.05 us (18%)
  local copies, waits for them, and re-layouts  1.71 us (6%)
  between operations  0.72 us (3%)
    ppermute x8, starting transfers between devices, swap(): return lax.ppermute(value, 'seq', [(i, i ^ mask) for i in range(count)])  12.5 us
    ppermute x8, waiting for transfers between devices, swap(): return lax.ppermute(value, 'seq', [(i, i ^ mask) for i in range(count)])  7.71 us
    unnamed x10, local copies, waits for them, and re-layouts  1.71 us
    pallas_call x3, Pallas kernels, step(): pl.pallas_call(functools.partial(step_kernel, sides, members, exp_scale),...  1.65 us
    pallas_call x1, Pallas kernels, per_device(): pl.pallas_call(functools.partial(first_kernel, parts, exp_scale), out_sha...  1.4 us
    pallas_call x1, Pallas kernels, per_device(): pl.pallas_call(functools.partial(bank_kernel, parts, score_scale), out_sh...  1.36 us
    pallas_call x1, Pallas kernels, per_device(): pl.pallas_call(functools.partial(last_kernel, parts, exp_scale), out_shap...  0.62 us
  transfers between devices with their start and end apart: 8, of which 4 were waited for; matrix products, arithmetic and copies ran while one was open for 0% of the time, Pallas kernels for 11%

profile of v3, /device:TPU:0, one launch (start us, length us, event | category | flops | bytes accessed | tf_op | source)
XLA Modules:
  0.0 27.7 jit_solution(3097181607706047288)
XLA Ops:
  0.7 3.0 %collective-permute-start.2 = (bf16[7,128,128]{2,1,0:T(8,128)(2,1)}, bf16[7,128,128]{2,1,0:T(8,128)(2,1)S(1)}, u32[]{:S(2)}, u32[]{:S(2)}) collective-permute-start(bf16[7,128,128]{2,1,0:T(8,128)(2,1)} %bitcast.5), channel_id=1, source_target_pairs={{0,4},{4,0},{8,12},{12,8},{16,20},{20,16},{24,28},{28,24},{1,5},{5... | collective-permute-start | bytes 688136 | tf_op jit(solution)/shard_map/ppermute | solution.py:175
  3.7 2.6 %collective-permute-start = (bf16[128,128]{1,0:T(8,128)(2,1)}, bf16[128,128]{1,0:T(8,128)(2,1)S(1)}, u32[]{:S(2)}, u32[]{:S(2)}) collective-permute-start(bf16[128,128]{1,0:T(8,128)(2,1)} %bitcast.7), channel_id=1, source_target_pairs={{0,16},{4,20},{8,24},{12,28},{16,0},{20,4},{24,8},{28,12},{1,17},{... | collective-permute-start | bytes 98312 | tf_op jit(solution)/shard_map/ppermute | solution.py:175
  6.3 1.6 %collective-permute-start.1 = (bf16[128,128]{1,0:T(8,128)(2,1)}, bf16[128,128]{1,0:T(8,128)(2,1)S(1)}, u32[]{:S(2)}, u32[]{:S(2)}) collective-permute-start(bf16[128,128]{1,0:T(8,128)(2,1)} %bitcast.8), channel_id=1, source_target_pairs={{0,8},{4,12},{8,0},{12,4},{16,24},{20,28},{24,16},{28,20},{1,9},{5... | collective-permute-start | bytes 98312 | tf_op jit(solution)/shard_map/ppermute | solution.py:175
  7.8 0.2 collective-permute-start.3
  8.1 0.9 %copy-done = bf16[128,7,128]{2,0,1:T(8,128)(2,1)S(1)} copy-done((bf16[128,7,128]{2,0,1:T(8,128)(2,1)S(1)}, bf16[128,7,128]{2,0,1:T(8,128)(2,1)}, u32[]{:S(2)}) %copy-start) | copy-done | bytes 229400
  9.0 0.8 %copy-done.1 = bf16[128,1,128]{2,0,1:T(8,128)(2,1)S(1)} copy-done((bf16[128,1,128]{2,0,1:T(8,128)(2,1)S(1)}, bf16[128,1,128]{2,0,1:T(8,128)(2,1)}, u32[]{:S(2)}) %copy-start.1) | copy-done | bytes 32792
  9.8 1.4 %first.1 = (f32[8,128]{1,0:T(8,128)S(1)}, f32[2,4,128]{2,1,0:T(4,128)S(1)}, bf16[512,32]{1,0:T(8,128)(2,1)S(1)}, bf16[7,128,128]{2,1,0:T(8,128)(2,1)S(1)}, bf16[128,128]{1,0:T(8,128)(2,1)S(1)}) custom-call(s32[8]{0:T(128)S(1)} %copy-done.3, s32[8]{0:T(128)S(1)} %copy-done.4, bf16[7,128,128]{2,1,0:T(8,128)(2,1)S(1)} %bitcast.6, bf16[128,128]{1,0:T(8,128)(2,1)S(1)} %bitcast.10), custom_call_target="tpu_custom_call" | custom-call | tf_op jit(solution)/shard_map/first/pallas_call | solution.py:187
  11.2 0.0 collective-permute-done.refs_1_.refs_3_
  11.2 0.4 %own_step.2.prior_ref = f32[8,128]{1,0:T(8,128)S(1)} custom-call(f32[2,4,128]{2,1,0:T(4,128)S(1)} %get-tuple-element.10.mask_ref, f32[8,128]{1,0:T(8,128)S(1)} %get-tuple-element.11.prior_ref, bf16[7,128,128]{2,1,0:T(8,128)(2,1)S(1)} %get-tuple-element.9.refs_0_.own_ref.query_ref, bf16[128,128]{1,0:T(8,128)(2,1)S(1)} %collective-permute-done.refs_1_.refs_3_), custom_call_target="tpu_custom_call" | custom-call | tf_op jit(solution)/shard_map/own_step/pallas_call | solution.py:206
  11.6 0.0 collective-permute-done.1.refs_1_.refs_2_
  11.6 0.4 %own_step.3.prior_ref = f32[8,128]{1,0:T(8,128)S(1)} custom-call(f32[2,4,128]{2,1,0:T(4,128)S(1)} %get-tuple-element.10.mask_ref, f32[8,128]{1,0:T(8,128)S(1)} %own_step.2.prior_ref, bf16[7,128,128]{2,1,0:T(8,128)(2,1)S(1)} %get-tuple-element.9.refs_0_.own_ref.query_ref, bf16[128,128]{1,0:T(8,128)(2,1)S(1)} %collective-permute-done.1.refs_1_.refs_2_), custom_call_target="tpu_custom_call" | custom-call | tf_op jit(solution)/shard_map/own_step/pallas_call | solution.py:206
  12.1 0.0 copy-start.2
  12.1 0.8 %mate_step.1.prior_ref = f32[8,128]{1,0:T(8,128)S(1)} custom-call(f32[2,4,128]{2,1,0:T(4,128)S(1)} %get-tuple-element.10.mask_ref, f32[8,128]{1,0:T(8,128)S(1)} %own_step.3.prior_ref, bf16[7,128,128]{2,1,0:T(8,128)(2,1)S(1)} %collective-permute-done.2.refs_0_.mate_ref, bf16[128,128]{1,0:T(8,128)(2,1)S(1)} %get-tuple-element.12.refs_1_, ...), custom_call_target="tpu_custom_call" | custom-call | tf_op jit(solution)/shard_map/mate_step/pallas_call | solution.py:206
  12.9 0.9 %collective-permute-done.3.key_ref = bf16[128,128]{1,0:T(8,128)(2,1)S(1)} collective-permute-done((bf16[128,128]{1,0:T(8,128)(2,1)}, bf16[128,128]{1,0:T(8,128)(2,1)S(1)}, u32[]{:S(2)}, u32[]{:S(2)}) %collective-permute-start.3) | collective-permute-done | bytes 32800 | tf_op jit(solution)/shard_map/ppermute | solution.py:175
  13.8 0.6 %last.1.refs_0_ = bf16[80,128]{1,0:T(8,128)(2,1)S(1)} custom-call(f32[2,4,128]{2,1,0:T(4,128)S(1)} %get-tuple-element.10.mask_ref, f32[8,128]{1,0:T(8,128)S(1)} %mate_step.1.prior_ref, bf16[7,128,128]{2,1,0:T(8,128)(2,1)S(1)} %get-tuple-element.9.refs_0_.own_ref.query_ref, bf16[7,128,128]{2,1,0:T(8,128)(2,1)S(1)} %collective-permute-done.2.refs_0_.mate_ref, ...), custom_call_target="tpu_custom_call" | custom-call | tf_op jit(solution)/shard_map/last/pallas_call | solution.py:218
  14.4 2.8 %collective-permute-start.6 = (bf16[80,128]{1,0:T(8,128)(2,1)S(1)}, bf16[80,128]{1,0:T(8,128)(2,1)S(1)}, u32[]{:S(2)}, u32[]{:S(2)}) collective-permute-start(bf16[80,128]{1,0:T(8,128)(2,1)S(1)} %last.1.refs_0_), channel_id=1, source_target_pairs={{0,24},{4,28},{8,16},{12,20},{16,8},{20,12},{24,0},{28,4},{1,25},{... | collective-permute-start | bytes 61448 | tf_op jit(solution)/shard_map/ppermute | solution.py:175
  17.2 0.0 collective-permute-start.5
  17.2 1.6 %collective-permute-start.4 = (bf16[80,128]{1,0:T(8,128)(2,1)S(1)}, bf16[80,128]{1,0:T(8,128)(2,1)S(1)}, u32[]{:S(2)}, u32[]{:S(2)}) collective-permute-start(bf16[80,128]{1,0:T(8,128)(2,1)S(1)} %last.1.refs_0_), channel_id=1, source_target_pairs={{0,8},{4,12},{8,0},{12,4},{16,24},{20,28},{24,16},{28,20},{1,9},{5... | collective-permute-start | bytes 61448 | tf_op jit(solution)/shard_map/ppermute | solution.py:175
  18.8 1.2 %collective-permute-done.6.refs_3_ = bf16[80,128]{1,0:T(8,128)(2,1)S(1)} collective-permute-done((bf16[80,128]{1,0:T(8,128)(2,1)S(1)}, bf16[80,128]{1,0:T(8,128)(2,1)S(1)}, u32[]{:S(2)}, u32[]{:S(2)}) %collective-permute-start.6) | collective-permute-done | bytes 20512 | tf_op jit(solution)/shard_map/ppermute | solution.py:175
  20.0 1.8 %collective-permute-done.5.refs_2_ = bf16[80,128]{1,0:T(8,128)(2,1)S(1)} collective-permute-done((bf16[80,128]{1,0:T(8,128)(2,1)S(1)}, bf16[80,128]{1,0:T(8,128)(2,1)S(1)}, u32[]{:S(2)}, u32[]{:S(2)}) %collective-permute-start.5) | collective-permute-done | bytes 20512 | tf_op jit(solution)/shard_map/ppermute | solution.py:175
  21.9 0.0 collective-permute-done.4.refs_1_
  21.9 0.6 %collective-permute-start.7 = (bf16[272,128]{1,0:T(8,128)(2,1)S(1)}, bf16[272,128]{1,0:T(8,128)(2,1)S(1)}, u32[]{:S(2)}, u32[]{:S(2)}) collective-permute-start(bf16[272,128]{1,0:T(8,128)(2,1)S(1)} %load.1.own_ref), channel_id=1, source_target_pairs={{0,4},{4,0},{8,12},{12,8},{16,20},{20,16},{24,28},{28,24},{1,5},{5... | collective-permute-start | bytes 208904 | tf_op jit(solution)/shard_map/ppermute | solution.py:175
  22.5 3.8 %collective-permute-done.7.mate_ref = bf16[272,128]{1,0:T(8,128)(2,1)S(1)} collective-permute-done((bf16[272,128]{1,0:T(8,128)(2,1)S(1)}, bf16[272,128]{1,0:T(8,128)(2,1)S(1)}, u32[]{:S(2)}, u32[]{:S(2)}) %collective-permute-start.7) | collective-permute-done | bytes 69664 | tf_op jit(solution)/shard_map/ppermute | solution.py:175
  26.3 1.4 %bank.1 = (bf16[7,128,512]{2,1,0:T(8,128)(2,1)}, bf16[64,128]{1,0:T(8,128)(2,1)}) custom-call(bf16[7,128,128]{2,1,0:T(8,128)(2,1)S(1)} %get-tuple-element.9.refs_0_.own_ref.query_ref, bf16[272,128]{1,0:T(8,128)(2,1)S(1)} %load.1.own_ref, bf16[272,128]{1,0:T(8,128)(2,1)S(1)} %collective-permute-done.7.mate_ref, bf16[512,32]{1,0:T(8,128)(2,1)S(1)} %get-tuple-element.13.pick_ref), custom_call_target="tpu_custom_call" | custom-call | tf_op jit(solution)/shard_map/bank/pallas_call | solution.py:238
  (9 shorter events, 0.0 us)
Async XLA Ops:
  0.6 7.4 %copy-start.3 = (s32[8]{0:T(128)S(1)}, s32[8]{0:T(128)}, u32[]{:S(2)}) copy-start(s32[8]{0:T(128)} %start_ref.1) | copy-start | bytes 100
  0.6 7.4 %copy-start.4 = (s32[8]{0:T(128)S(1)}, s32[8]{0:T(128)}, u32[]{:S(2)}) copy-start(s32[8]{0:T(128)} %slot_ref.1) | copy-start | bytes 100
  0.7 11.4 %collective-permute-start.2 = (bf16[7,128,128]{2,1,0:T(8,128)(2,1)}, bf16[7,128,128]{2,1,0:T(8,128)(2,1)S(1)}, u32[]{:S(2)}, u32[]{:S(2)}) collective-permute-start(bf16[7,128,128]{2,1,0:T(8,128)(2,1)} %bitcast.5), channel_id=1, source_target_pairs={{0,4},{4,0},{8,12},{12,8},{16,20},{20,16},{24,28},{28,24},{1,5},{5... | collective-permute-start | bytes 688136 | tf_op jit(solution)/shard_map/ppermute | solution.py:175
  3.7 7.5 %collective-permute-start = (bf16[128,128]{1,0:T(8,128)(2,1)}, bf16[128,128]{1,0:T(8,128)(2,1)S(1)}, u32[]{:S(2)}, u32[]{:S(2)}) collective-permute-start(bf16[128,128]{1,0:T(8,128)(2,1)} %bitcast.7), channel_id=1, source_target_pairs={{0,16},{4,20},{8,24},{12,28},{16,0},{20,4},{24,8},{28,12},{1,17},{... | collective-permute-start | bytes 98312 | tf_op jit(solution)/shard_map/ppermute | solution.py:175
  6.3 5.4 %collective-permute-start.1 = (bf16[128,128]{1,0:T(8,128)(2,1)}, bf16[128,128]{1,0:T(8,128)(2,1)S(1)}, u32[]{:S(2)}, u32[]{:S(2)}) collective-permute-start(bf16[128,128]{1,0:T(8,128)(2,1)} %bitcast.8), channel_id=1, source_target_pairs={{0,8},{4,12},{8,0},{12,4},{16,24},{20,28},{24,16},{28,20},{1,9},{5... | collective-permute-start | bytes 98312 | tf_op jit(solution)/shard_map/ppermute | solution.py:175
  7.8 5.9 %collective-permute-start.3 = (bf16[128,128]{1,0:T(8,128)(2,1)}, bf16[128,128]{1,0:T(8,128)(2,1)S(1)}, u32[]{:S(2)}, u32[]{:S(2)}) collective-permute-start(bf16[128,128]{1,0:T(8,128)(2,1)} %bitcast.9), channel_id=1, source_target_pairs={{0,24},{4,28},{8,16},{12,20},{16,8},{20,12},{24,0},{28,4},{1,25},{... | collective-permute-start | bytes 98312 | tf_op jit(solution)/shard_map/ppermute | solution.py:175
  8.1 0.9 %copy-start = (bf16[128,7,128]{2,0,1:T(8,128)(2,1)S(1)}, bf16[128,7,128]{2,0,1:T(8,128)(2,1)}, u32[]{:S(2)}) copy-start(bf16[128,7,128]{2,0,1:T(8,128)(2,1)} %param.5) | copy-start | bytes 688132
  9.0 0.8 %copy-start.1 = (bf16[128,1,128]{2,0,1:T(8,128)(2,1)S(1)}, bf16[128,1,128]{2,0,1:T(8,128)(2,1)}, u32[]{:S(2)}) copy-start(bf16[128,1,128]{2,0,1:T(8,128)(2,1)} %param.6) | copy-start | bytes 98308
  12.1 1.7 %copy-start.2 = (bf16[64,1,128]{2,0,1:T(8,128)(2,1)S(1)}, bf16[64,1,128]{2,0,1:T(8,128)(2,1)}, u32[]{:S(2)}) copy-start(bf16[64,1,128]{2,0,1:T(8,128)(2,1)} %param.7) | copy-start | bytes 49156
  14.4 5.6 %collective-permute-start.6 = (bf16[80,128]{1,0:T(8,128)(2,1)S(1)}, bf16[80,128]{1,0:T(8,128)(2,1)S(1)}, u32[]{:S(2)}, u32[]{:S(2)}) collective-permute-start(bf16[80,128]{1,0:T(8,128)(2,1)S(1)} %last.1.refs_0_), channel_id=1, source_target_pairs={{0,24},{4,28},{8,16},{12,20},{16,8},{20,12},{24,0},{28,4},{1,25},{... | collective-permute-start | bytes 61448 | tf_op jit(solution)/shard_map/ppermute | solution.py:175
  17.2 4.7 %collective-permute-start.5 = (bf16[80,128]{1,0:T(8,128)(2,1)S(1)}, bf16[80,128]{1,0:T(8,128)(2,1)S(1)}, u32[]{:S(2)}, u32[]{:S(2)}) collective-permute-start(bf16[80,128]{1,0:T(8,128)(2,1)S(1)} %last.1.refs_0_), channel_id=1, source_target_pairs={{0,16},{4,20},{8,24},{12,28},{16,0},{20,4},{24,8},{28,12},{1,17},{... | collective-permute-start | bytes 61448 | tf_op jit(solution)/shard_map/ppermute | solution.py:175
  17.2 4.7 %collective-permute-start.4 = (bf16[80,128]{1,0:T(8,128)(2,1)S(1)}, bf16[80,128]{1,0:T(8,128)(2,1)S(1)}, u32[]{:S(2)}, u32[]{:S(2)}) collective-permute-start(bf16[80,128]{1,0:T(8,128)(2,1)S(1)} %last.1.refs_0_), channel_id=1, source_target_pairs={{0,8},{4,12},{8,0},{12,4},{16,24},{20,28},{24,16},{28,20},{1,9},{5... | collective-permute-start | bytes 61448 | tf_op jit(solution)/shard_map/ppermute | solution.py:175
  21.9 4.4 %collective-permute-start.7 = (bf16[272,128]{1,0:T(8,128)(2,1)S(1)}, bf16[272,128]{1,0:T(8,128)(2,1)S(1)}, u32[]{:S(2)}, u32[]{:S(2)}) collective-permute-start(bf16[272,128]{1,0:T(8,128)(2,1)S(1)} %load.1.own_ref), channel_id=1, source_target_pairs={{0,4},{4,0},{8,12},{12,8},{16,20},{20,16},{24,28},{28,24},{1,5},{5... | collective-permute-start | bytes 208904 | tf_op jit(solution)/shard_map/ppermute | solution.py:175

commit v4 on v3

--- a/solution.py
+++ b/solution.py
@@ -14,7 +14,6 @@
 MIB = 1 << 20
 
 VMEM = pl.BlockSpec(memory_space=pltpu.VMEM)
-SMEM = pl.BlockSpec(memory_space=pltpu.SMEM)
 HBM = pl.BlockSpec(memory_space=pltpu.HBM)
 
 
@@ -36,41 +35,44 @@
     return padded(3 * parts, PACK)
 
 
-def column_sums(scale, query_ref, inside, keys):
+def column_sums(scale, query_ref, keys):
     group, tok, _ = query_ref.shape
 
     def one_head(head, total):
         scores = nt_dot(keys, query_ref[head])
         top = jnp.max(scores, axis=0, keepdims=True)
         grown = jnp.exp2((scores - top) * scale)
-        return total + grown * (inside / jnp.sum(grown, axis=0, keepdims=True))
+        return total + grown * (1.0 / jnp.sum(grown, axis=0, keepdims=True))
 
     total = jnp.zeros((BLK, tok), jnp.float32)
     return lax.fori_loop(0, group, one_head, total, unroll=True)
 
 
-def partial_rep(scale, query_refs, mask_refs, keys):
+def partial_rep(scale, query_refs, insides, keys):
     total = 0.0
-    for query_ref, inside in zip(query_refs, mask_refs):
-        total += column_sums(scale, query_ref, inside, keys)
+    for query_ref, inside in zip(query_refs, insides):
+        total += column_sums(scale, query_ref, keys) * inside
     column = jnp.sum(total, axis=1, keepdims=True)
     return jnp.sum(column * keys.astype(jnp.float32), axis=0, keepdims=True)
 
 
-def first_kernel(parts, scale, start_ref, slot_ref, query_hbm, key_hbm, rep_ref, mask_ref, pick_ref, query_ref, key_ref, sems):
-    tok = query_ref.shape[1]
-    copies = [
-        pltpu.make_async_copy(key_hbm, key_ref, sems.at[0]),
-        pltpu.make_async_copy(query_hbm, query_ref, sems.at[1]),
-    ]
+def first_kernel(
+    parts, scale, start_hbm, slot_hbm, query_hbm, key_hbm,
+    rep_ref, mask_ref, pick_ref, query_ref, key_ref, start_ref, slot_ref, sems,
+):
+    pairs = ((start_hbm, start_ref), (slot_hbm, slot_ref), (key_hbm, key_ref), (query_hbm, query_ref))
+    copies = [pltpu.make_async_copy(*pair, sems.at[i]) for i, pair in enumerate(pairs)]
     for copy in copies:
         copy.start()
+    tok = query_ref.shape[1]
     me = lax.axis_index("seq")
     here, lane = me // 2, me % 2
     lead = lead_rows(parts)
     token = lax.broadcasted_iota(jnp.int32, (1, tok), 1)
     column = lax.broadcasted_iota(jnp.int32, (1, 2 * lead), 1)
     slots = jnp.full((1, 2 * lead), -1, jnp.int32)
+    for copy in copies[:2]:
+        copy.wait()
     for part in range(parts):
         for side in range(2):
             where = (me ^ side) * tok + token - start_ref[2 * part + lane]
@@ -81,7 +83,7 @@
     row = lax.broadcasted_iota(jnp.int32, pick_ref.shape, 0)
     pick_ref[...] = (row == slots).astype(jnp.float32).astype(jnp.bfloat16)
     rep_ref[...] = jnp.zeros_like(rep_ref)
-    for copy in copies:
+    for copy in copies[2:]:
         copy.wait()
     inside = mask_ref[0, pl.ds(here, 1), :]
     rep_ref[pl.ds(here, 1), :] = partial_rep(scale, [query_ref], [inside], key_ref[...])
@@ -97,8 +99,10 @@
         rep_ref[pl.ds(slot, 1), :] += partial_rep(scale, query_refs, inside, key_ref[...])
 
 
-def last_kernel(parts, scale, mask_ref, prior_ref, own_ref, mate_ref, key_ref, cache_ref, sum_ref, rep_ref):
-    slot = (lax.axis_index("seq") // 2) ^ (parts - 1)
+def last_kernel(
+    parts, part, scale, mask_ref, prior_ref, own_ref, mate_ref, key_ref, cache_ref, sum_ref, rep_ref
+):
+    slot = (lax.axis_index("seq") // 2) ^ part
     rep_ref[...] = prior_ref[...]
     inside = [mask_ref[side, pl.ds(slot, 1), :] for side in range(2)]
     rep_ref[pl.ds(slot, 1), :] += partial_rep(scale, [own_ref, mate_ref], inside, key_ref[...])
@@ -193,12 +197,16 @@
             jax.ShapeDtypeStruct(asked.shape, jnp.bfloat16),
             jax.ShapeDtypeStruct(keys.shape, jnp.bfloat16),
         ),
-        in_specs=[SMEM, SMEM, HBM, HBM],
+        in_specs=[HBM] * 4,
         out_specs=(VMEM,) * 5,
-        scratch_shapes=[pltpu.SemaphoreType.DMA((2,))],
+        scratch_shapes=[
+            pltpu.SMEM(window_start.shape, jnp.int32),
+            pltpu.SMEM(owner_slot.shape, jnp.int32),
+            pltpu.SemaphoreType.DMA((4,)),
+        ],
         compiler_params=params,
         name="first",
-    )(window_start, owner_slot, asked, keys)
+    )(*[pltpu.with_memory_space_constraint(x, pltpu.HBM) for x in (window_start, owner_slot, asked, keys)])
     pieces[0] = held
 
     def step(partial, sides, members, label):
@@ -212,18 +220,19 @@
             name=label,
         )(inside, partial, *asking, *[pieces[part] for part in members])
 
-    for part in reversed(range(1, parts - 1)):
+    *middle, tail = reversed(range(1, parts))
+    for part in middle:
         partial = step(partial, (0,), (part,), "own_step")
-    partial = step(partial, (1,), tuple(range(parts - 1)), "mate_step")
+    partial = step(partial, (1,), (0, *middle), "mate_step")
     partial = pl.pallas_call(
-        functools.partial(last_kernel, parts, exp_scale),
+        functools.partial(last_kernel, parts, tail, exp_scale),
         out_shape=shape(term_rows(parts) + rows, jnp.bfloat16),
         in_specs=[VMEM] * 6,
         out_specs=VMEM,
         scratch_shapes=[pltpu.VMEM(sums.shape, sums.dtype)],
         compiler_params=params,
         name="last",
-    )(inside, partial, own, mate, pieces[-1], cache_keys[:, 0, :])
+    )(inside, partial, own, mate, pieces[tail], cache_keys[:, 0, :])
 
     load = pl.pallas_call(
         functools.partial(load_kernel, parts, 1.0 / (group * WIN)),

time: 27.9 us -> 26.4 us (0.946)
  local copies, waits for them, and re-layouts: 1.71 us -> 0.01 us
    unnamed x10 -> x2, local copies, waits for them, and re-layouts: 1.71 us -> 0.01 us
  transfers between devices with their start and end apart: 8 -> 8, of which waited for: 4 -> 6; matrix products, arithmetic and copies ran while one was open for 0% -> 0% of each run, Pallas kernels for 11% -> 12%
where the time goes in v4:
time: 26.4 us; the launch traced here: 26.3 us
  starting transfers between devices  12.6 us (48%)
  waiting for transfers between devices  7.88 us (30%)
  Pallas kernels  5.1 us (19%)
  between operations  0.7 us (3%)
    ppermute x8, starting transfers between devices, swap(): return lax.ppermute(value, 'seq', [(i, i ^ mask) for i in range(count)])  12.6 us
    ppermute x8, waiting for transfers between devices, swap(): return lax.ppermute(value, 'seq', [(i, i ^ mask) for i in range(count)])  7.88 us
    pallas_call x3, Pallas kernels, step(): pl.pallas_call(functools.partial(step_kernel, sides, members, exp_scale),...  1.66 us
    pallas_call x1, Pallas kernels, per_device(): pl.pallas_call(functools.partial(first_kernel, parts, exp_scale), out_sha...  1.44 us
    pallas_call x1, Pallas kernels, per_device(): pl.pallas_call(functools.partial(bank_kernel, parts, score_scale), out_sh...  1.36 us
    pallas_call x1, Pallas kernels, per_device(): pl.pallas_call(functools.partial(last_kernel, parts, tail, exp_scale), ou...  0.62 us
  transfers between devices with their start and end apart: 8, of which 6 were waited for; matrix products, arithmetic and copies ran while one was open for 0% of the time, Pallas kernels for 12%

profile of v4, /device:TPU:0, one launch (start us, length us, event | category | flops | bytes accessed | tf_op | source)
XLA Modules:
  0.0 26.3 jit_solution(1035078180999839475)
XLA Ops:
  0.6 3.0 %collective-permute-start.2 = (bf16[7,128,128]{2,1,0:T(8,128)(2,1)}, bf16[7,128,128]{2,1,0:T(8,128)(2,1)S(1)}, u32[]{:S(2)}, u32[]{:S(2)}) collective-permute-start(bf16[7,128,128]{2,1,0:T(8,128)(2,1)} %bitcast.6), channel_id=1, source_target_pairs={{0,4},{4,0},{8,12},{12,8},{16,20},{20,16},{24,28},{28,24},{1,5},{5... | collective-permute-start | bytes 688136 | tf_op jit(solution)/shard_map/ppermute | solution.py:179
  3.7 3.6 %collective-permute-start = (bf16[128,128]{1,0:T(8,128)(2,1)}, bf16[128,128]{1,0:T(8,128)(2,1)S(1)}, u32[]{:S(2)}, u32[]{:S(2)}) collective-permute-start(bf16[128,128]{1,0:T(8,128)(2,1)} %bitcast.8), channel_id=1, source_target_pairs={{0,24},{4,28},{8,16},{12,20},{16,8},{20,12},{24,0},{28,4},{1,25},{... | collective-permute-start | bytes 98312 | tf_op jit(solution)/shard_map/ppermute | solution.py:179
  7.3 0.0 collective-permute-start.1
  7.3 0.8 %collective-permute-start.3 = (bf16[128,128]{1,0:T(8,128)(2,1)}, bf16[128,128]{1,0:T(8,128)(2,1)S(1)}, u32[]{:S(2)}, u32[]{:S(2)}) collective-permute-start(bf16[128,128]{1,0:T(8,128)(2,1)} %bitcast.10), channel_id=1, source_target_pairs={{0,8},{4,12},{8,0},{12,4},{16,24},{20,28},{24,16},{28,20},{1,9},{5... | collective-permute-start | bytes 98312 | tf_op jit(solution)/shard_map/ppermute | solution.py:179
  8.1 1.4 %first.1 = (f32[8,128]{1,0:T(8,128)S(1)}, f32[2,4,128]{2,1,0:T(4,128)S(1)}, bf16[512,32]{1,0:T(8,128)(2,1)S(1)}, bf16[7,128,128]{2,1,0:T(8,128)(2,1)S(1)}, bf16[128,128]{1,0:T(8,128)(2,1)S(1)}) custom-call(s32[8]{0:T(128)} %start_hbm.1, s32[8]{0:T(128)} %slot_hbm.1, bf16[7,128,128]{2,1,0:T(8,128)(2,1)} %bitcast.7, bf16[128,128]{1,0:T(8,128)(2,1)} %bitcast.11), custom_call_target="tpu_custom_call" | custom-call | tf_op jit(solution)/shard_map/first/pallas_call | solution.py:191
  9.5 0.4 %collective-permute-done.refs_1_.refs_2_ = bf16[128,128]{1,0:T(8,128)(2,1)S(1)} collective-permute-done((bf16[128,128]{1,0:T(8,128)(2,1)}, bf16[128,128]{1,0:T(8,128)(2,1)S(1)}, u32[]{:S(2)}, u32[]{:S(2)}) %collective-permute-start) | collective-permute-done | bytes 32800 | tf_op jit(solution)/shard_map/ppermute | solution.py:179
  9.9 0.4 %own_step.2.prior_ref = f32[8,128]{1,0:T(8,128)S(1)} custom-call(f32[2,4,128]{2,1,0:T(4,128)S(1)} %get-tuple-element.10.mask_ref, f32[8,128]{1,0:T(8,128)S(1)} %get-tuple-element.11.prior_ref, bf16[7,128,128]{2,1,0:T(8,128)(2,1)S(1)} %get-tuple-element.9.refs_0_.own_ref.query_ref, bf16[128,128]{1,0:T(8,128)(2,1)S(1)} %collective-permute-done.refs_1_.refs_2_), custom_call_target="tpu_custom_call" | custom-call | tf_op jit(solution)/shard_map/own_step/pallas_call | solution.py:214
  10.4 1.9 %collective-permute-done.1.refs_1_.refs_3_ = bf16[128,128]{1,0:T(8,128)(2,1)S(1)} collective-permute-done((bf16[128,128]{1,0:T(8,128)(2,1)}, bf16[128,128]{1,0:T(8,128)(2,1)S(1)}, u32[]{:S(2)}, u32[]{:S(2)}) %collective-permute-start.1) | collective-permute-done | bytes 32800 | tf_op jit(solution)/shard_map/ppermute | solution.py:179
  12.3 0.4 %own_step.3.prior_ref = f32[8,128]{1,0:T(8,128)S(1)} custom-call(f32[2,4,128]{2,1,0:T(4,128)S(1)} %get-tuple-element.10.mask_ref, f32[8,128]{1,0:T(8,128)S(1)} %own_step.2.prior_ref, bf16[7,128,128]{2,1,0:T(8,128)(2,1)S(1)} %get-tuple-element.9.refs_0_.own_ref.query_ref, bf16[128,128]{1,0:T(8,128)(2,1)S(1)} %collective-permute-done.1.refs_1_.refs_3_), custom_call_target="tpu_custom_call" | custom-call | tf_op jit(solution)/shard_map/own_step/pallas_call | solution.py:214
  12.7 0.0 collective-permute-done.2.refs_0_.mate_ref
  12.7 0.0 copy-start
  12.8 0.8 %mate_step.1.prior_ref = f32[8,128]{1,0:T(8,128)S(1)} custom-call(f32[2,4,128]{2,1,0:T(4,128)S(1)} %get-tuple-element.10.mask_ref, f32[8,128]{1,0:T(8,128)S(1)} %own_step.3.prior_ref, bf16[7,128,128]{2,1,0:T(8,128)(2,1)S(1)} %collective-permute-done.2.refs_0_.mate_ref, bf16[128,128]{1,0:T(8,128)(2,1)S(1)} %get-tuple-element.12.refs_1_, ...), custom_call_target="tpu_custom_call" | custom-call | tf_op jit(solution)/shard_map/mate_step/pallas_call | solution.py:214
  13.5 0.0 collective-permute-done.3.key_ref
  13.6 0.0 copy-done
  13.6 0.6 %last.1.refs_0_ = bf16[80,128]{1,0:T(8,128)(2,1)S(1)} custom-call(f32[2,4,128]{2,1,0:T(4,128)S(1)} %get-tuple-element.10.mask_ref, f32[8,128]{1,0:T(8,128)S(1)} %mate_step.1.prior_ref, bf16[7,128,128]{2,1,0:T(8,128)(2,1)S(1)} %get-tuple-element.9.refs_0_.own_ref.query_ref, bf16[7,128,128]{2,1,0:T(8,128)(2,1)S(1)} %collective-permute-done.2.refs_0_.mate_ref, ...), custom_call_target="tpu_custom_call" | custom-call | tf_op jit(solution)/shard_map/last/pallas_call | solution.py:227
  14.2 1.4 %collective-permute-start.6 = (bf16[80,128]{1,0:T(8,128)(2,1)S(1)}, bf16[80,128]{1,0:T(8,128)(2,1)S(1)}, u32[]{:S(2)}, u32[]{:S(2)}) collective-permute-start(bf16[80,128]{1,0:T(8,128)(2,1)S(1)} %last.1.refs_0_), channel_id=1, source_target_pairs={{0,24},{4,28},{8,16},{12,20},{16,8},{20,12},{24,0},{28,4},{1,25},{... | collective-permute-start | bytes 61448 | tf_op jit(solution)/shard_map/ppermute | solution.py:179
  15.6 0.0 collective-permute-start.5
  15.6 3.0 %collective-permute-start.4 = (bf16[80,128]{1,0:T(8,128)(2,1)S(1)}, bf16[80,128]{1,0:T(8,128)(2,1)S(1)}, u32[]{:S(2)}, u32[]{:S(2)}) collective-permute-start(bf16[80,128]{1,0:T(8,128)(2,1)S(1)} %last.1.refs_0_), channel_id=1, source_target_pairs={{0,8},{4,12},{8,0},{12,4},{16,24},{20,28},{24,16},{28,20},{1,9},{5... | collective-permute-start | bytes 61448 | tf_op jit(solution)/shard_map/ppermute | solution.py:179
  18.6 1.2 %collective-permute-done.6.refs_3_ = bf16[80,128]{1,0:T(8,128)(2,1)S(1)} collective-permute-done((bf16[80,128]{1,0:T(8,128)(2,1)S(1)}, bf16[80,128]{1,0:T(8,128)(2,1)S(1)}, u32[]{:S(2)}, u32[]{:S(2)}) %collective-permute-start.6) | collective-permute-done | bytes 20512 | tf_op jit(solution)/shard_map/ppermute | solution.py:179
  19.8 0.5 %collective-permute-done.5.refs_2_ = bf16[80,128]{1,0:T(8,128)(2,1)S(1)} collective-permute-done((bf16[80,128]{1,0:T(8,128)(2,1)S(1)}, bf16[80,128]{1,0:T(8,128)(2,1)S(1)}, u32[]{:S(2)}, u32[]{:S(2)}) %collective-permute-start.5) | collective-permute-done | bytes 20512 | tf_op jit(solution)/shard_map/ppermute | solution.py:179
  20.3 0.2 collective-permute-done.4.refs_1_
  20.5 0.7 %collective-permute-start.7 = (bf16[272,128]{1,0:T(8,128)(2,1)S(1)}, bf16[272,128]{1,0:T(8,128)(2,1)S(1)}, u32[]{:S(2)}, u32[]{:S(2)}) collective-permute-start(bf16[272,128]{1,0:T(8,128)(2,1)S(1)} %load.1.own_ref), channel_id=1, source_target_pairs={{0,4},{4,0},{8,12},{12,8},{16,20},{20,16},{24,28},{28,24},{1,5},{5... | collective-permute-start | bytes 208904 | tf_op jit(solution)/shard_map/ppermute | solution.py:179
  21.2 3.7 %collective-permute-done.7.mate_ref = bf16[272,128]{1,0:T(8,128)(2,1)S(1)} collective-permute-done((bf16[272,128]{1,0:T(8,128)(2,1)S(1)}, bf16[272,128]{1,0:T(8,128)(2,1)S(1)}, u32[]{:S(2)}, u32[]{:S(2)}) %collective-permute-start.7) | collective-permute-done | bytes 69664 | tf_op jit(solution)/shard_map/ppermute | solution.py:179
  24.9 1.4 %bank.1 = (bf16[7,128,512]{2,1,0:T(8,128)(2,1)}, bf16[64,128]{1,0:T(8,128)(2,1)}) custom-call(bf16[7,128,128]{2,1,0:T(8,128)(2,1)S(1)} %get-tuple-element.9.refs_0_.own_ref.query_ref, bf16[272,128]{1,0:T(8,128)(2,1)S(1)} %load.1.own_ref, bf16[272,128]{1,0:T(8,128)(2,1)S(1)} %collective-permute-done.7.mate_ref, bf16[512,32]{1,0:T(8,128)(2,1)S(1)} %get-tuple-element.13.pick_ref), custom_call_target="tpu_custom_call" | custom-call | tf_op jit(solution)/shard_map/bank/pallas_call | solution.py:247
  (1 shorter events, 0.0 us)
Async XLA Ops:
  0.6 12.1 %collective-permute-start.2 = (bf16[7,128,128]{2,1,0:T(8,128)(2,1)}, bf16[7,128,128]{2,1,0:T(8,128)(2,1)S(1)}, u32[]{:S(2)}, u32[]{:S(2)}) collective-permute-start(bf16[7,128,128]{2,1,0:T(8,128)(2,1)} %bitcast.6), channel_id=1, source_target_pairs={{0,4},{4,0},{8,12},{12,8},{16,20},{20,16},{24,28},{28,24},{1,5},{5... | collective-permute-start | bytes 688136 | tf_op jit(solution)/shard_map/ppermute | solution.py:179
  3.7 6.3 %collective-permute-start = (bf16[128,128]{1,0:T(8,128)(2,1)}, bf16[128,128]{1,0:T(8,128)(2,1)S(1)}, u32[]{:S(2)}, u32[]{:S(2)}) collective-permute-start(bf16[128,128]{1,0:T(8,128)(2,1)} %bitcast.8), channel_id=1, source_target_pairs={{0,24},{4,28},{8,16},{12,20},{16,8},{20,12},{24,0},{28,4},{1,25},{... | collective-permute-start | bytes 98312 | tf_op jit(solution)/shard_map/ppermute | solution.py:179
  7.3 5.0 %collective-permute-start.1 = (bf16[128,128]{1,0:T(8,128)(2,1)}, bf16[128,128]{1,0:T(8,128)(2,1)S(1)}, u32[]{:S(2)}, u32[]{:S(2)}) collective-permute-start(bf16[128,128]{1,0:T(8,128)(2,1)} %bitcast.9), channel_id=1, source_target_pairs={{0,16},{4,20},{8,24},{12,28},{16,0},{20,4},{24,8},{28,12},{1,17},{... | collective-permute-start | bytes 98312 | tf_op jit(solution)/shard_map/ppermute | solution.py:179
  7.3 6.3 %collective-permute-start.3 = (bf16[128,128]{1,0:T(8,128)(2,1)}, bf16[128,128]{1,0:T(8,128)(2,1)S(1)}, u32[]{:S(2)}, u32[]{:S(2)}) collective-permute-start(bf16[128,128]{1,0:T(8,128)(2,1)} %bitcast.10), channel_id=1, source_target_pairs={{0,8},{4,12},{8,0},{12,4},{16,24},{20,28},{24,16},{28,20},{1,9},{5... | collective-permute-start | bytes 98312 | tf_op jit(solution)/shard_map/ppermute | solution.py:179
  12.7 0.8 %copy-start = (bf16[64,1,128]{2,0,1:T(8,128)(2,1)S(1)}, bf16[64,1,128]{2,0,1:T(8,128)(2,1)}, u32[]{:S(2)}) copy-start(bf16[64,1,128]{2,0,1:T(8,128)(2,1)} %param.7) | copy-start | bytes 49156
  14.2 5.6 %collective-permute-start.6 = (bf16[80,128]{1,0:T(8,128)(2,1)S(1)}, bf16[80,128]{1,0:T(8,128)(2,1)S(1)}, u32[]{:S(2)}, u32[]{:S(2)}) collective-permute-start(bf16[80,128]{1,0:T(8,128)(2,1)S(1)} %last.1.refs_0_), channel_id=1, source_target_pairs={{0,24},{4,28},{8,16},{12,20},{16,8},{20,12},{24,0},{28,4},{1,25},{... | collective-permute-start | bytes 61448 | tf_op jit(solution)/shard_map/ppermute | solution.py:179
  15.6 4.7 %collective-permute-start.5 = (bf16[80,128]{1,0:T(8,128)(2,1)S(1)}, bf16[80,128]{1,0:T(8,128)(2,1)S(1)}, u32[]{:S(2)}, u32[]{:S(2)}) collective-permute-start(bf16[80,128]{1,0:T(8,128)(2,1)S(1)} %last.1.refs_0_), channel_id=1, source_target_pairs={{0,16},{4,20},{8,24},{12,28},{16,0},{20,4},{24,8},{28,12},{1,17},{... | collective-permute-start | bytes 61448 | tf_op jit(solution)/shard_map/ppermute | solution.py:179
  15.6 4.9 %collective-permute-start.4 = (bf16[80,128]{1,0:T(8,128)(2,1)S(1)}, bf16[80,128]{1,0:T(8,128)(2,1)S(1)}, u32[]{:S(2)}, u32[]{:S(2)}) collective-permute-start(bf16[80,128]{1,0:T(8,128)(2,1)S(1)} %last.1.refs_0_), channel_id=1, source_target_pairs={{0,8},{4,12},{8,0},{12,4},{16,24},{20,28},{24,16},{28,20},{1,9},{5... | collective-permute-start | bytes 61448 | tf_op jit(solution)/shard_map/ppermute | solution.py:179
  20.5 4.4 %collective-permute-start.7 = (bf16[272,128]{1,0:T(8,128)(2,1)S(1)}, bf16[272,128]{1,0:T(8,128)(2,1)S(1)}, u32[]{:S(2)}, u32[]{:S(2)}) collective-permute-start(bf16[272,128]{1,0:T(8,128)(2,1)S(1)} %load.1.own_ref), channel_id=1, source_target_pairs={{0,4},{4,0},{8,12},{12,8},{16,20},{20,16},{24,28},{28,24},{1,5},{5... | collective-permute-start | bytes 208904 | tf_op jit(solution)/shard_map/ppermute | solution.py:179

commit v5 on v4

v5 whole, which is shorter than its diff:
```python
import functools
import math

import jax
import jax.numpy as jnp
from jax import lax
from jax.experimental import pallas as pl
from jax.experimental.pallas import tpu as pltpu
from jax.sharding import PartitionSpec as P

BLK = 128
WIN = 512
PACK = 16
MIB = 1 << 20

VMEM = pl.BlockSpec(memory_space=pltpu.VMEM)
HBM = pl.BlockSpec(memory_space=pltpu.HBM)


def nt_dot(left, right):
    return lax.dot_general(
        left, right, (((1,), (1,)), ((), ())), preferred_element_type=jnp.float32
    )


def padded(rows, unit):
    return unit * pl.cdiv(rows, unit)


def key_order(parts):
    return sorted(range(1, parts), key=lambda k: (k % 2 == 0, k))


def lead_rows(parts):
    return padded(parts, PACK)


def term_rows(parts):
    return padded(3 * parts, PACK)


def unit(scale, query, keys):
    scores = nt_dot(keys, query)
    top = jnp.max(scores, axis=0, keepdims=True)
    grown = jnp.exp2((scores - top) * scale)
    return grown * (1.0 / jnp.sum(grown, axis=0, keepdims=True))


def column_sums(scale, query_ref, keys, inside):
    total = unit(scale, query_ref[0], keys)
    for head in range(1, query_ref.shape[0]):
        total += unit(scale, query_ref[head], keys)
    return total * inside


def representative(total, keys):
    column = jnp.sum(total, axis=1, keepdims=True)
    return jnp.sum(column * keys.astype(jnp.float32), axis=0, keepdims=True)


def first_kernel(
    parts, scale, start_hbm, slot_hbm, query_hbm, key_hbm,
    total_ref, mask_ref, pick_ref, query_ref, key_ref, start_ref, slot_ref, sems,
):
    tok = query_ref.shape[1]
    pairs = [(key_hbm, key_ref), (start_hbm, start_ref), (slot_hbm, slot_ref)]
    pairs.append((query_hbm, query_ref))
    copies = [pltpu.make_async_copy(*pair, sems.at[i]) for i, pair in enumerate(pairs)]
    for copy in copies:
        copy.start()
    me = lax.axis_index("seq")
    here, lane = me // 2, me % 2
    lead = lead_rows(parts)
    token = lax.broadcasted_iota(jnp.int32, (1, tok), 1)
    column = lax.broadcasted_iota(jnp.int32, (1, 2 * lead), 1)
    slots = jnp.full((1, 2 * lead), -1, jnp.int32)
    for copy in copies[:3]:
        copy.wait()
    for part in range(parts):
        for side in range(2):
            where = (me ^ side) * tok + token - start_ref[2 * part + lane]
            mask_ref[side, pl.ds(part, 1), :] = ((where >= 0) & (where < WIN)).astype(jnp.float32)
            slots = jnp.where(column == side * lead + part, slot_ref[2 * part + side], slots)
    row = lax.broadcasted_iota(jnp.int32, pick_ref.shape, 0)
    pick_ref[...] = (row == slots).astype(jnp.float32).astype(jnp.bfloat16)
    copies[3].wait()
    total_ref[...] = column_sums(scale, query_ref, key_ref[...], mask_ref[0, pl.ds(here, 1), :])


def own_kernel(part, scale, mask_ref, query_ref, key_ref, total_ref, pass_ref):
    pass_ref[...] = mask_ref[...]
    slot = (lax.axis_index("seq") // 2) ^ part
    inside = mask_ref[0, pl.ds(slot, 1), :]
    total_ref[...] = column_sums(scale, query_ref, key_ref[...], inside)


def mate_kernel(members, scale, mask_ref, query_ref, *refs):
    total_refs, key_refs, rep_ref = refs[: len(members)], refs[len(members) : -1], refs[-1]
    here = lax.axis_index("seq") // 2
    rep_ref[...] = jnp.zeros_like(rep_ref)
    for part, total_ref, key_ref in zip(members, total_refs, key_refs):
        slot = here ^ part
        keys = key_ref[...]
        total = column_sums(scale, query_ref, keys, mask_ref[1, pl.ds(slot, 1), :])
        rep_ref[pl.ds(slot, 1), :] = representative(total + total_ref[...], keys)


def last_kernel(
    parts, part, scale, mask_ref, prior_ref, own_ref, mate_ref, key_ref, sum_ref, rep_ref
):
    slot = (lax.axis_index("seq") // 2) ^ part
    keys = key_ref[...]
    rep_ref[...] = prior_ref[...]
    total = column_sums(scale, own_ref, keys, mask_ref[0, pl.ds(slot, 1), :])
    total += column_sums(scale, mate_ref, keys, mask_ref[1, pl.ds(slot, 1), :])
    rep_ref[pl.ds(slot, 1), :] = representative(total, keys)
    rest = rep_ref[pl.ds(0, parts), :]
    terms = []
    for _ in range(3):
        terms.append(rest.astype(jnp.bfloat16).astype(jnp.float32))
        rest = rest - terms[-1]
    spare = term_rows(parts) - 3 * parts
    if spare:
        terms.append(jnp.zeros((spare, rest.shape[1]), jnp.float32))
    sum_ref[...] = jnp.concatenate(terms, axis=0).astype(jnp.bfloat16)


def pair_kernel(own_ref, mate_ref, near_ref, far_ref, pair_ref):
    terms, rows = own_ref.shape[0], near_ref.shape[0]
    lane = lax.axis_index("seq") % 2
    for side, (sum_ref, cache_ref) in enumerate(((own_ref, near_ref), (mate_ref, far_ref))):
        start = pl.multiple_of((lane ^ side) * (terms + rows), PACK)
        pair_ref[pl.ds(start, terms), :] = sum_ref[...]
        pair_ref[pl.ds(pl.multiple_of(start + terms, PACK), rows), :] = cache_ref[...]


def bank_kernel(parts, share, scale, query_ref, pick_ref, *refs):
    pair_refs = refs[:parts]
    rel_ref, bank_ref, base_ref, rel_work, bank_work, sems = refs[parts:]
    group = query_ref.shape[0]
    rows = bank_ref.shape[0]
    lead, terms = lead_rows(parts), term_rows(parts)
    me = lax.axis_index("seq")
    fresh = []
    for side in range(2):
        first = side * (terms + rows)
        sums = []
        for part, ref in enumerate(pair_refs):
            wide = ref[pl.ds(first, terms), :].astype(jnp.float32)
            sums.append(wide[:parts] + (wide[parts : 2 * parts] + wide[2 * parts : 3 * parts]))
            start = pl.multiple_of((2 * ((me // 2) ^ part) + side) * rows, PACK)
            base_ref[pl.ds(start, rows), :] = ref[pl.ds(first + terms, rows), :]
        while len(sums) > 1:
            sums = [left + right for left, right in zip(sums[::2], sums[1::2])]
        fresh.append(sums[0] * share)
        if lead > parts:
            fresh.append(jnp.zeros((lead - parts, fresh[0].shape[1]), jnp.float32))
    fresh = jnp.concatenate(fresh, axis=0).astype(jnp.bfloat16)
    pick = pick_ref[...]
    placed = jnp.dot(pick, fresh, preferred_element_type=jnp.float32)
    taken = jnp.dot(pick, jnp.ones_like(fresh), preferred_element_type=jnp.float32)
    bank = jnp.where(taken > 0.5, placed, base_ref[...].astype(jnp.float32)).astype(jnp.bfloat16)
    base_ref[...] = bank
    bank_work[...] = base_ref[pl.ds(pl.multiple_of(me * rows, PACK), rows), :]
    copies = [pltpu.make_async_copy(bank_work, bank_ref, sems.at[group])]
    copies[0].start()
    for head in range(group):
        rel_work[head] = (nt_dot(query_ref[head], bank) * scale).astype(jnp.bfloat16)
        copies.append(pltpu.make_async_copy(rel_work.at[head], rel_ref.at[head], sems.at[head]))
        copies[-1].start()
    for copy in copies:
        copy.wait()


def per_device(count, queries, new_keys, cache_keys, window_start, owner_slot):
    tok, group, head_dim = queries.shape
    rows = cache_keys.shape[0]
    parts = count // 2
    lead = lead_rows(parts)
    assert tok == BLK and count == 1 << (count.bit_length() - 1) and count > 2
    score_scale = 1.0 / math.sqrt(head_dim)
    exp_scale = score_scale * math.log2(math.e)

    def swap(value, mask):
        return lax.ppermute(value, "seq", [(i, i ^ mask) for i in range(count)])

    def shape(rows_of, dtype):
        return jax.ShapeDtypeStruct((rows_of, head_dim), dtype)

    params = pltpu.CompilerParams(vmem_limit_bytes=(8 + parts) * MIB)
    asked = queries.transpose(1, 0, 2)
    keys = new_keys[:, 0, :]
    far = key_order(parts)
    mate = swap(asked, 1)
    pieces = {}
    for k in far:
        pieces[k] = swap(keys, 2 * k)

    cache = cache_keys[:, 0, :]
    far_cache = swap(cache, 1)
    square = jax.ShapeDtypeStruct((BLK, tok), jnp.float32)
    totals = {}
    totals[0], inside, pick, own, pieces[0] = pl.pallas_call(
        functools.partial(first_kernel, parts, exp_scale),
        out_shape=(
            square,
            jax.ShapeDtypeStruct((2, parts, tok), jnp.float32),
            jax.ShapeDtypeStruct((count * rows, 2 * lead), jnp.bfloat16),
            jax.ShapeDtypeStruct(asked.shape, jnp.bfloat16),
            jax.ShapeDtypeStruct(keys.shape, jnp.bfloat16),
        ),
        in_specs=[HBM] * 4,
        out_specs=(VMEM,) * 5,
        scratch_shapes=[
            pltpu.SMEM(window_start.shape, jnp.int32),
            pltpu.SMEM(owner_slot.shape, jnp.int32),
            pltpu.SemaphoreType.DMA((4,)),
        ],
        compiler_params=params,
        name="first",
    )(*[pltpu.with_memory_space_constraint(x, pltpu.HBM) for x in (window_start, owner_slot, asked, keys)])

    *middle, tail = far
    for k in middle:
        totals[k], inside = pl.pallas_call(
            functools.partial(own_kernel, k, exp_scale),
            out_shape=(square, inside),
            in_specs=[VMEM] * 3,
            out_specs=(VMEM, VMEM),
            compiler_params=params,
            name="own_step",
        )(inside, own, pieces[k])
    members = [0, *middle]
    partial = pl.pallas_call(
        functools.partial(mate_kernel, members, exp_scale),
        out_shape=shape(padded(parts, 8), jnp.float32),
        in_specs=[VMEM] * (2 + 2 * len(members)),
        out_specs=VMEM,
        compiler_params=params,
        name="mate_step",
    )(inside, mate, *[totals[k] for k in members], *[pieces[k] for k in members])
    partial = pl.pallas_call(
        functools.partial(last_kernel, parts, tail, exp_scale),
        out_shape=shape(term_rows(parts), jnp.bfloat16),
        in_specs=[VMEM] * 5,
        out_specs=VMEM,
        scratch_shapes=[pltpu.VMEM((padded(parts, 8), head_dim), jnp.float32)],
        compiler_params=params,
        name="last",
    )(inside, partial, own, mate, pieces[tail])

    other = swap(partial, 1)
    pair = pl.pallas_call(
        pair_kernel,
        out_shape=shape(2 * (partial.shape[0] + rows), jnp.bfloat16),
        in_specs=[VMEM] * 4,
        out_specs=VMEM,
        compiler_params=params,
        name="pair",
    )(partial, other, cache, far_cache)
    pairs = [pair]
    for k in range(1, parts):
        pairs.append(swap(pair, 2 * k))

    relevance, bank = pl.pallas_call(
        functools.partial(bank_kernel, parts, 1.0 / (group * WIN), score_scale),
        out_shape=(
            jax.ShapeDtypeStruct((group, tok, count * rows), jnp.bfloat16),
            jax.ShapeDtypeStruct((rows, head_dim), jnp.bfloat16),
        ),
        in_specs=[VMEM] * (2 + parts),
        out_specs=(HBM, HBM),
        scratch_shapes=[
            pltpu.VMEM((count * rows, head_dim), jnp.bfloat16),
            pltpu.VMEM((group, tok, count * rows), jnp.bfloat16),
            pltpu.VMEM((rows, head_dim), jnp.bfloat16),
            pltpu.SemaphoreType.DMA((group + 1,)),
        ],
        compiler_params=params,
        name="bank",
    )(own, pick, *pairs)
    return (relevance.transpose(1, 0, 2), bank[:, None, :])


def solution(mesh):
    count = mesh.shape["seq"]

    def body(*args):
        return per_device(count, *args)

    return jax.shard_map(
        body,
        mesh=mesh,
        in_specs=(P("seq", "kvh", None), P("seq", "kvh", None), P("seq", "kvh", None), P(), P()),
        out_specs=(P("seq", "kvh", None), P("seq", "kvh", None)),
        check_vma=False,
    )
```

time: 26.4 us -> 25.8 us (0.977)
  waiting for transfers between devices: 7.88 us -> 7.29 us
    ppermute x8 -> x9, waiting for transfers between devices: 7.88 us -> 7.29 us  [swap(): return lax.ppermute(value, 'seq', [(i, i ^ mask) for i in range(count)])]
    ppermute x8 -> x9, starting transfers between devices: 12.6 us -> 12.8 us  [swap(): return lax.ppermute(value, 'seq', [(i, i ^ mask) for i in range(count)])]
  transfers between devices with their start and end apart: 8 -> 9, of which waited for: 6 -> 5; matrix products, arithmetic and copies ran while one was open for 0% -> 0% of each run, Pallas kernels for 12% -> 14%
where the time goes in v5:
time: 25.8 us; the launch traced here: 25.6 us
  starting transfers between devices  12.8 us (50%)
  waiting for transfers between devices  7.29 us (28%)
  Pallas kernels  4.86 us (19%)
  between operations  0.69 us (3%)
    ppermute x9, starting transfers between devices, swap(): return lax.ppermute(value, 'seq', [(i, i ^ mask) for i in range(count)])  12.8 us
    ppermute x9, waiting for transfers between devices, swap(): return lax.ppermute(value, 'seq', [(i, i ^ mask) for i in range(count)])  7.29 us
    pallas_call x1, Pallas kernels, per_device(): pl.pallas_call(functools.partial(bank_kernel, parts, 1.0 / (group * WIN),...  1.36 us
    pallas_call x1, Pallas kernels, per_device(): pl.pallas_call(functools.partial(first_kernel, parts, exp_scale), out_sha...  1.36 us
    pallas_call x1, Pallas kernels, per_device(): pl.pallas_call(functools.partial(mate_kernel, members, exp_scale), out_sh...  0.79 us
    pallas_call x2, Pallas kernels, per_device(): pl.pallas_call(functools.partial(own_kernel, k, exp_scale), out_shape=(sq...  0.72 us
    pallas_call x1, Pallas kernels, per_device(): pl.pallas_call(functools.partial(last_kernel, parts, tail, exp_scale), ou...  0.62 us
  transfers between devices with their start and end apart: 9, of which 5 were waited for; matrix products, arithmetic and copies ran while one was open for 0% of the time, Pallas kernels for 14%

profile of v5, /device:TPU:0, one launch (start us, length us, event | category | flops | bytes accessed | tf_op | source)
XLA Modules:
  0.0 25.6 jit_solution(10378084658212134664)
XLA Ops:
  0.6 3.0 %collective-permute-start.2 = (bf16[7,128,128]{2,1,0:T(8,128)(2,1)}, bf16[7,128,128]{2,1,0:T(8,128)(2,1)S(1)}, u32[]{:S(2)}, u32[]{:S(2)}) collective-permute-start(bf16[7,128,128]{2,1,0:T(8,128)(2,1)} %bitcast.7), channel_id=1, source_target_pairs={{0,4},{4,0},{8,12},{12,8},{16,20},{20,16},{24,28},{28,24},{1,5},{5... | collective-permute-start | bytes 688136 | tf_op jit(solution)/shard_map/ppermute | solution.py:185
  3.7 1.6 %collective-permute-start = (bf16[128,128]{1,0:T(8,128)(2,1)}, bf16[128,128]{1,0:T(8,128)(2,1)S(1)}, u32[]{:S(2)}, u32[]{:S(2)}) collective-permute-start(bf16[128,128]{1,0:T(8,128)(2,1)} %bitcast.9), channel_id=1, source_target_pairs={{0,8},{4,12},{8,0},{12,4},{16,24},{20,28},{24,16},{28,20},{1,9},{5... | collective-permute-start | bytes 98312 | tf_op jit(solution)/shard_map/ppermute | solution.py:185
  5.2 2.5 %collective-permute-start.1 = (bf16[128,128]{1,0:T(8,128)(2,1)}, bf16[128,128]{1,0:T(8,128)(2,1)S(1)}, u32[]{:S(2)}, u32[]{:S(2)}) collective-permute-start(bf16[128,128]{1,0:T(8,128)(2,1)} %bitcast.10), channel_id=1, source_target_pairs={{0,24},{4,28},{8,16},{12,20},{16,8},{20,12},{24,0},{28,4},{1,25},{... | collective-permute-start | bytes 98312 | tf_op jit(solution)/shard_map/ppermute | solution.py:185
  7.7 0.1 collective-permute-start.3
  7.8 0.5 %collective-permute-start.5 = (bf16[64,128]{1,0:T(8,128)(2,1)}, bf16[64,128]{1,0:T(8,128)(2,1)S(1)}, u32[]{:S(2)}, u32[]{:S(2)}) collective-permute-start(bf16[64,128]{1,0:T(8,128)(2,1)} %bitcast.5), channel_id=1, source_target_pairs={{0,4},{4,0},{8,12},{12,8},{16,20},{20,16},{24,28},{28,24},{1,5},{5... | collective-permute-start | bytes 49160 | tf_op jit(solution)/shard_map/ppermute | solution.py:185
  8.4 1.4 %first.1 = (f32[128,128]{1,0:T(8,128)S(1)}, f32[2,4,128]{2,1,0:T(4,128)S(1)}, bf16[512,32]{1,0:T(8,128)(2,1)S(1)}, bf16[7,128,128]{2,1,0:T(8,128)(2,1)S(1)}, bf16[128,128]{1,0:T(8,128)(2,1)S(1)}) custom-call(s32[8]{0:T(128)} %start_hbm.1, s32[8]{0:T(128)} %slot_hbm.1, bf16[7,128,128]{2,1,0:T(8,128)(2,1)} %bitcast.8, bf16[128,128]{1,0:T(8,128)(2,1)} %bitcast.12), custom_call_target="tpu_custom_call" | custom-call | tf_op jit(solution)/shard_map/first/pallas_call | solution.py:203
  9.7 0.4 %own_step.2 = (f32[128,128]{1,0:T(8,128)S(1)}, f32[2,4,128]{2,1,0:T(4,128)S(1)}) custom-call(f32[2,4,128]{2,1,0:T(4,128)S(1)} %get-tuple-element.15.mask_ref, bf16[7,128,128]{2,1,0:T(8,128)(2,1)S(1)} %get-tuple-element.13.query_ref.own_ref, bf16[128,128]{1,0:T(8,128)(2,1)S(1)} %collective-permute-done.key_ref.refs_4_), custom_call_target="tpu_custom_call" | custom-call | tf_op jit(solution)/shard_map/own_step/pallas_call | solution.py:225
  10.1 1.2 %collective-permute-done.1.key_ref.refs_5_ = bf16[128,128]{1,0:T(8,128)(2,1)S(1)} collective-permute-done((bf16[128,128]{1,0:T(8,128)(2,1)}, bf16[128,128]{1,0:T(8,128)(2,1)S(1)}, u32[]{:S(2)}, u32[]{:S(2)}) %collective-permute-start.1) | collective-permute-done | bytes 32800 | tf_op jit(solution)/shard_map/ppermute | solution.py:185
  11.3 0.4 %own_step.3 = (f32[128,128]{1,0:T(8,128)S(1)}, f32[2,4,128]{2,1,0:T(4,128)S(1)}) custom-call(f32[2,4,128]{2,1,0:T(4,128)S(1)} %get-tuple-element.16.mask_ref, bf16[7,128,128]{2,1,0:T(8,128)(2,1)S(1)} %get-tuple-element.13.query_ref.own_ref, bf16[128,128]{1,0:T(8,128)(2,1)S(1)} %collective-permute-done.1.key_ref.refs_5_), custom_call_target="tpu_custom_call" | custom-call | tf_op jit(solution)/shard_map/own_step/pallas_call | solution.py:225
  11.7 0.0 collective-permute-done.2.query_ref.mate_ref
  11.7 0.8 %mate_step.1.prior_ref = f32[8,128]{1,0:T(8,128)S(1)} custom-call(f32[2,4,128]{2,1,0:T(4,128)S(1)} %get-tuple-element.17.mask_ref, bf16[7,128,128]{2,1,0:T(8,128)(2,1)S(1)} %collective-permute-done.2.query_ref.mate_ref, f32[128,128]{1,0:T(8,128)S(1)} %get-tuple-element.18.refs_0_, f32[128,128]{1,0:T(8,128)S(1)} %get-tuple-element.19.refs_1_, ...), custom_call_target="tpu_custom_call" | custom-call | tf_op jit(solution)/shard_map/mate_step/pallas_call | solution.py:234
  12.5 0.0 copy-start
  12.5 0.6 %collective-permute-done.3.key_ref = bf16[128,128]{1,0:T(8,128)(2,1)S(1)} collective-permute-done((bf16[128,128]{1,0:T(8,128)(2,1)}, bf16[128,128]{1,0:T(8,128)(2,1)S(1)}, u32[]{:S(2)}, u32[]{:S(2)}) %collective-permute-start.3) | collective-permute-done | bytes 32800 | tf_op jit(solution)/shard_map/ppermute | solution.py:185
  13.1 0.6 %last.1.own_ref = bf16[16,128]{1,0:T(8,128)(2,1)S(1)} custom-call(f32[2,4,128]{2,1,0:T(4,128)S(1)} %get-tuple-element.17.mask_ref, f32[8,128]{1,0:T(8,128)S(1)} %mate_step.1.prior_ref, bf16[7,128,128]{2,1,0:T(8,128)(2,1)S(1)} %get-tuple-element.13.query_ref.own_ref, bf16[7,128,128]{2,1,0:T(8,128)(2,1)S(1)} %collective-permute-done.2.query_ref.mate_ref, ...), custom_call_target="tpu_custom_call" | custom-call | tf_op jit(solution)/shard_map/last/pallas_call | solution.py:242
  13.7 0.6 %collective-permute-start.4 = (bf16[16,128]{1,0:T(8,128)(2,1)S(1)}, bf16[16,128]{1,0:T(8,128)(2,1)S(1)}, u32[]{:S(2)}, u32[]{:S(2)}) collective-permute-start(bf16[16,128]{1,0:T(8,128)(2,1)S(1)} %last.1.own_ref), channel_id=1, source_target_pairs={{0,4},{4,0},{8,12},{12,8},{16,20},{20,16},{24,28},{28,24},{1,5},{5... | collective-permute-start | bytes 12296 | tf_op jit(solution)/shard_map/ppermute | solution.py:185
  14.3 0.0 collective-permute-done.5.far_ref
  14.3 3.1 %collective-permute-done.4.mate_ref = bf16[16,128]{1,0:T(8,128)(2,1)S(1)} collective-permute-done((bf16[16,128]{1,0:T(8,128)(2,1)S(1)}, bf16[16,128]{1,0:T(8,128)(2,1)S(1)}, u32[]{:S(2)}, u32[]{:S(2)}) %collective-permute-start.4) | collective-permute-done | bytes 4128 | tf_op jit(solution)/shard_map/ppermute | solution.py:185
  17.4 1.8 %collective-permute-start.8 = (bf16[160,128]{1,0:T(8,128)(2,1)S(1)}, bf16[160,128]{1,0:T(8,128)(2,1)S(1)}, u32[]{:S(2)}, u32[]{:S(2)}) collective-permute-start(bf16[160,128]{1,0:T(8,128)(2,1)S(1)} %pair.1.refs_0_), channel_id=1, source_target_pairs={{0,24},{4,28},{8,16},{12,20},{16,8},{20,12},{24,0},{28,4},{1,25},{... | collective-permute-start | bytes 122888 | tf_op jit(solution)/shard_map/ppermute | solution.py:185
  19.2 0.1 collective-permute-start.7
  19.3 2.5 %collective-permute-start.6 = (bf16[160,128]{1,0:T(8,128)(2,1)S(1)}, bf16[160,128]{1,0:T(8,128)(2,1)S(1)}, u32[]{:S(2)}, u32[]{:S(2)}) collective-permute-start(bf16[160,128]{1,0:T(8,128)(2,1)S(1)} %pair.1.refs_0_), channel_id=1, source_target_pairs={{0,8},{4,12},{8,0},{12,4},{16,24},{20,28},{24,16},{28,20},{1,9},{5... | collective-permute-start | bytes 122888 | tf_op jit(solution)/shard_map/ppermute | solution.py:185
  21.8 1.4 %collective-permute-done.8.refs_3_ = bf16[160,128]{1,0:T(8,128)(2,1)S(1)} collective-permute-done((bf16[160,128]{1,0:T(8,128)(2,1)S(1)}, bf16[160,128]{1,0:T(8,128)(2,1)S(1)}, u32[]{:S(2)}, u32[]{:S(2)}) %collective-permute-start.8) | collective-permute-done | bytes 40992 | tf_op jit(solution)/shard_map/ppermute | solution.py:185
  23.3 1.0 %collective-permute-done.7.refs_2_ = bf16[160,128]{1,0:T(8,128)(2,1)S(1)} collective-permute-done((bf16[160,128]{1,0:T(8,128)(2,1)S(1)}, bf16[160,128]{1,0:T(8,128)(2,1)S(1)}, u32[]{:S(2)}, u32[]{:S(2)}) %collective-permute-start.7) | collective-permute-done | bytes 40992 | tf_op jit(solution)/shard_map/ppermute | solution.py:185
  24.2 0.0 collective-permute-done.6.refs_1_
  24.3 1.4 %bank.1 = (bf16[7,128,512]{2,1,0:T(8,128)(2,1)}, bf16[64,128]{1,0:T(8,128)(2,1)}) custom-call(bf16[7,128,128]{2,1,0:T(8,128)(2,1)S(1)} %get-tuple-element.13.query_ref.own_ref, bf16[512,32]{1,0:T(8,128)(2,1)S(1)} %get-tuple-element.14.pick_ref, bf16[160,128]{1,0:T(8,128)(2,1)S(1)} %pair.1.refs_0_, bf16[160,128]{1,0:T(8,128)(2,1)S(1)} %collective-permute-done.6.refs_1_, ...), custom_call_target="tpu_custom_call" | custom-call | tf_op jit(solution)/shard_map/bank/pallas_call | solution.py:265
  (3 shorter events, 0.0 us)
Async XLA Ops:
  0.6 11.1 %collective-permute-start.2 = (bf16[7,128,128]{2,1,0:T(8,128)(2,1)}, bf16[7,128,128]{2,1,0:T(8,128)(2,1)S(1)}, u32[]{:S(2)}, u32[]{:S(2)}) collective-permute-start(bf16[7,128,128]{2,1,0:T(8,128)(2,1)} %bitcast.7), channel_id=1, source_target_pairs={{0,4},{4,0},{8,12},{12,8},{16,20},{20,16},{24,28},{28,24},{1,5},{5... | collective-permute-start | bytes 688136 | tf_op jit(solution)/shard_map/ppermute | solution.py:185
  3.7 6.1 %collective-permute-start = (bf16[128,128]{1,0:T(8,128)(2,1)}, bf16[128,128]{1,0:T(8,128)(2,1)S(1)}, u32[]{:S(2)}, u32[]{:S(2)}) collective-permute-start(bf16[128,128]{1,0:T(8,128)(2,1)} %bitcast.9), channel_id=1, source_target_pairs={{0,8},{4,12},{8,0},{12,4},{16,24},{20,28},{24,16},{28,20},{1,9},{5... | collective-permute-start | bytes 98312 | tf_op jit(solution)/shard_map/ppermute | solution.py:185
  5.2 6.1 %collective-permute-start.1 = (bf16[128,128]{1,0:T(8,128)(2,1)}, bf16[128,128]{1,0:T(8,128)(2,1)S(1)}, u32[]{:S(2)}, u32[]{:S(2)}) collective-permute-start(bf16[128,128]{1,0:T(8,128)(2,1)} %bitcast.10), channel_id=1, source_target_pairs={{0,24},{4,28},{8,16},{12,20},{16,8},{20,12},{24,0},{28,4},{1,25},{... | collective-permute-start | bytes 98312 | tf_op jit(solution)/shard_map/ppermute | solution.py:185
  7.7 5.4 %collective-permute-start.3 = (bf16[128,128]{1,0:T(8,128)(2,1)}, bf16[128,128]{1,0:T(8,128)(2,1)S(1)}, u32[]{:S(2)}, u32[]{:S(2)}) collective-permute-start(bf16[128,128]{1,0:T(8,128)(2,1)} %bitcast.11), channel_id=1, source_target_pairs={{0,16},{4,20},{8,24},{12,28},{16,0},{20,4},{24,8},{28,12},{1,17},{... | collective-permute-start | bytes 98312 | tf_op jit(solution)/shard_map/ppermute | solution.py:185
  7.8 6.5 %collective-permute-start.5 = (bf16[64,128]{1,0:T(8,128)(2,1)}, bf16[64,128]{1,0:T(8,128)(2,1)S(1)}, u32[]{:S(2)}, u32[]{:S(2)}) collective-permute-start(bf16[64,128]{1,0:T(8,128)(2,1)} %bitcast.5), channel_id=1, source_target_pairs={{0,4},{4,0},{8,12},{12,8},{16,20},{20,16},{24,28},{28,24},{1,5},{5... | collective-permute-start | bytes 49160 | tf_op jit(solution)/shard_map/ppermute | solution.py:185
  12.5 4.9 %copy-start = (bf16[64,1,128]{2,0,1:T(8,128)(2,1)S(1)}, bf16[64,1,128]{2,0,1:T(8,128)(2,1)}, u32[]{:S(2)}) copy-start(bf16[64,1,128]{2,0,1:T(8,128)(2,1)} %param.7) | copy-start | bytes 49156
  13.7 3.7 %collective-permute-start.4 = (bf16[16,128]{1,0:T(8,128)(2,1)S(1)}, bf16[16,128]{1,0:T(8,128)(2,1)S(1)}, u32[]{:S(2)}, u32[]{:S(2)}) collective-permute-start(bf16[16,128]{1,0:T(8,128)(2,1)S(1)} %last.1.own_ref), channel_id=1, source_target_pairs={{0,4},{4,0},{8,12},{12,8},{16,20},{20,16},{24,28},{28,24},{1,5},{5... | collective-permute-start | bytes 12296 | tf_op jit(solution)/shard_map/ppermute | solution.py:185
  17.4 5.9 %collective-permute-start.8 = (bf16[160,128]{1,0:T(8,128)(2,1)S(1)}, bf16[160,128]{1,0:T(8,128)(2,1)S(1)}, u32[]{:S(2)}, u32[]{:S(2)}) collective-permute-start(bf16[160,128]{1,0:T(8,128)(2,1)S(1)} %pair.1.refs_0_), channel_id=1, source_target_pairs={{0,24},{4,28},{8,16},{12,20},{16,8},{20,12},{24,0},{28,4},{1,25},{... | collective-permute-start | bytes 122888 | tf_op jit(solution)/shard_map/ppermute | solution.py:185
  19.2 5.0 %collective-permute-start.7 = (bf16[160,128]{1,0:T(8,128)(2,1)S(1)}, bf16[160,128]{1,0:T(8,128)(2,1)S(1)}, u32[]{:S(2)}, u32[]{:S(2)}) collective-permute-start(bf16[160,128]{1,0:T(8,128)(2,1)S(1)} %pair.1.refs_0_), channel_id=1, source_target_pairs={{0,16},{4,20},{8,24},{12,28},{16,0},{20,4},{24,8},{28,12},{1,17},{... | collective-permute-start | bytes 122888 | tf_op jit(solution)/shard_map/ppermute | solution.py:185
  19.3 4.9 %collective-permute-start.6 = (bf16[160,128]{1,0:T(8,128)(2,1)S(1)}, bf16[160,128]{1,0:T(8,128)(2,1)S(1)}, u32[]{:S(2)}, u32[]{:S(2)}) collective-permute-start(bf16[160,128]{1,0:T(8,128)(2,1)S(1)} %pair.1.refs_0_), channel_id=1, source_target_pairs={{0,8},{4,12},{8,0},{12,4},{16,24},{20,28},{24,16},{28,20},{1,9},{5... | collective-permute-start | bytes 122888 | tf_op jit(solution)/shard_map/ppermute | solution.py:185

commit v6 on v5

--- a/solution.py
+++ b/solution.py
@@ -64,7 +64,7 @@
 ):
     tok = query_ref.shape[1]
     pairs = [(key_hbm, key_ref), (start_hbm, start_ref), (slot_hbm, slot_ref)]
-    pairs.append((query_hbm, query_ref))
+    pairs += [(query_hbm.at[head], query_ref.at[head]) for head in range(query_ref.shape[0])]
     copies = [pltpu.make_async_copy(*pair, sems.at[i]) for i, pair in enumerate(pairs)]
     for copy in copies:
         copy.start()
@@ -83,7 +83,8 @@
             slots = jnp.where(column == side * lead + part, slot_ref[2 * part + side], slots)
     row = lax.broadcasted_iota(jnp.int32, pick_ref.shape, 0)
     pick_ref[...] = (row == slots).astype(jnp.float32).astype(jnp.bfloat16)
-    copies[3].wait()
+    for copy in copies[3:]:
+        copy.wait()
     total_ref[...] = column_sums(scale, query_ref, key_ref[...], mask_ref[0, pl.ds(here, 1), :])
 
 
@@ -214,7 +215,7 @@
         scratch_shapes=[
             pltpu.SMEM(window_start.shape, jnp.int32),
             pltpu.SMEM(owner_slot.shape, jnp.int32),
-            pltpu.SemaphoreType.DMA((4,)),
+            pltpu.SemaphoreType.DMA((3 + group,)),
         ],
         compiler_params=params,
         name="first",

time: 25.8 us -> 25.8 us (level)
  transfers between devices with their start and end apart: 9 -> 9, of which waited for: 5 -> 5; matrix products, arithmetic and copies ran while one was open for 0% -> 0% of each run, Pallas kernels for 14% -> 13%
where the time goes in v6:
time: 25.8 us; the launch traced here: 25.6 us
  starting transfers between devices  12.8 us (50%)
  waiting for transfers between devices  7.33 us (28%)
  Pallas kernels  4.82 us (19%)
  between operations  0.69 us (3%)
    ppermute x9, starting transfers between devices, swap(): return lax.ppermute(value, 'seq', [(i, i ^ mask) for i in range(count)])  12.8 us
    ppermute x9, waiting for transfers between devices, swap(): return lax.ppermute(value, 'seq', [(i, i ^ mask) for i in range(count)])  7.33 us
    pallas_call x1, Pallas kernels, per_device(): pl.pallas_call(functools.partial(bank_kernel, parts, 1.0 / (group * WIN),...  1.36 us
    pallas_call x1, Pallas kernels, per_device(): pl.pallas_call(functools.partial(first_kernel, parts, exp_scale), out_sha...  1.32 us
    pallas_call x1, Pallas kernels, per_device(): pl.pallas_call(functools.partial(mate_kernel, members, exp_scale), out_sh...  0.79 us
    pallas_call x2, Pallas kernels, per_device(): pl.pallas_call(functools.partial(own_kernel, k, exp_scale), out_shape=(sq...  0.72 us
    pallas_call x1, Pallas kernels, per_device(): pl.pallas_call(functools.partial(last_kernel, parts, tail, exp_scale), ou...  0.62 us
  transfers between devices with their start and end apart: 9, of which 5 were waited for; matrix products, arithmetic and copies ran while one was open for 0% of the time, Pallas kernels for 13%

profile of v6, /device:TPU:0, one launch (start us, length us, event | category | flops | bytes accessed | tf_op | source)
XLA Modules:
  0.0 25.6 jit_solution(2099927120131458376)
XLA Ops:
  0.6 3.0 %collective-permute-start.2 = (bf16[7,128,128]{2,1,0:T(8,128)(2,1)}, bf16[7,128,128]{2,1,0:T(8,128)(2,1)S(1)}, u32[]{:S(2)}, u32[]{:S(2)}) collective-permute-start(bf16[7,128,128]{2,1,0:T(8,128)(2,1)} %bitcast.7), channel_id=1, source_target_pairs={{0,4},{4,0},{8,12},{12,8},{16,20},{20,16},{24,28},{28,24},{1,5},{5... | collective-permute-start | bytes 688136 | tf_op jit(solution)/shard_map/ppermute | solution.py:186
  3.7 1.6 %collective-permute-start = (bf16[128,128]{1,0:T(8,128)(2,1)}, bf16[128,128]{1,0:T(8,128)(2,1)S(1)}, u32[]{:S(2)}, u32[]{:S(2)}) collective-permute-start(bf16[128,128]{1,0:T(8,128)(2,1)} %bitcast.9), channel_id=1, source_target_pairs={{0,8},{4,12},{8,0},{12,4},{16,24},{20,28},{24,16},{28,20},{1,9},{5... | collective-permute-start | bytes 98312 | tf_op jit(solution)/shard_map/ppermute | solution.py:186
  5.2 2.5 %collective-permute-start.1 = (bf16[128,128]{1,0:T(8,128)(2,1)}, bf16[128,128]{1,0:T(8,128)(2,1)S(1)}, u32[]{:S(2)}, u32[]{:S(2)}) collective-permute-start(bf16[128,128]{1,0:T(8,128)(2,1)} %bitcast.10), channel_id=1, source_target_pairs={{0,24},{4,28},{8,16},{12,20},{16,8},{20,12},{24,0},{28,4},{1,25},{... | collective-permute-start | bytes 98312 | tf_op jit(solution)/shard_map/ppermute | solution.py:186
  7.7 0.1 collective-permute-start.3
  7.8 0.5 %collective-permute-start.5 = (bf16[64,128]{1,0:T(8,128)(2,1)}, bf16[64,128]{1,0:T(8,128)(2,1)S(1)}, u32[]{:S(2)}, u32[]{:S(2)}) collective-permute-start(bf16[64,128]{1,0:T(8,128)(2,1)} %bitcast.5), channel_id=1, source_target_pairs={{0,4},{4,0},{8,12},{12,8},{16,20},{20,16},{24,28},{28,24},{1,5},{5... | collective-permute-start | bytes 49160 | tf_op jit(solution)/shard_map/ppermute | solution.py:186
  8.4 1.3 %first.1 = (f32[128,128]{1,0:T(8,128)S(1)}, f32[2,4,128]{2,1,0:T(4,128)S(1)}, bf16[512,32]{1,0:T(8,128)(2,1)S(1)}, bf16[7,128,128]{2,1,0:T(8,128)(2,1)S(1)}, bf16[128,128]{1,0:T(8,128)(2,1)S(1)}) custom-call(s32[8]{0:T(128)} %start_hbm.1, s32[8]{0:T(128)} %slot_hbm.1, bf16[7,128,128]{2,1,0:T(8,128)(2,1)} %bitcast.8, bf16[128,128]{1,0:T(8,128)(2,1)} %bitcast.12), custom_call_target="tpu_custom_call" | custom-call | tf_op jit(solution)/shard_map/first/pallas_call | solution.py:204
  9.7 0.0 collective-permute-done.key_ref.refs_4_
  9.7 0.4 %own_step.2 = (f32[128,128]{1,0:T(8,128)S(1)}, f32[2,4,128]{2,1,0:T(4,128)S(1)}) custom-call(f32[2,4,128]{2,1,0:T(4,128)S(1)} %get-tuple-element.15.mask_ref, bf16[7,128,128]{2,1,0:T(8,128)(2,1)S(1)} %get-tuple-element.13.query_ref.own_ref, bf16[128,128]{1,0:T(8,128)(2,1)S(1)} %collective-permute-done.key_ref.refs_4_), custom_call_target="tpu_custom_call" | custom-call | tf_op jit(solution)/shard_map/own_step/pallas_call | solution.py:226
  10.1 1.3 %collective-permute-done.1.key_ref.refs_5_ = bf16[128,128]{1,0:T(8,128)(2,1)S(1)} collective-permute-done((bf16[128,128]{1,0:T(8,128)(2,1)}, bf16[128,128]{1,0:T(8,128)(2,1)S(1)}, u32[]{:S(2)}, u32[]{:S(2)}) %collective-permute-start.1) | collective-permute-done | bytes 32800 | tf_op jit(solution)/shard_map/ppermute | solution.py:186
  11.3 0.4 %own_step.3 = (f32[128,128]{1,0:T(8,128)S(1)}, f32[2,4,128]{2,1,0:T(4,128)S(1)}) custom-call(f32[2,4,128]{2,1,0:T(4,128)S(1)} %get-tuple-element.16.mask_ref, bf16[7,128,128]{2,1,0:T(8,128)(2,1)S(1)} %get-tuple-element.13.query_ref.own_ref, bf16[128,128]{1,0:T(8,128)(2,1)S(1)} %collective-permute-done.1.key_ref.refs_5_), custom_call_target="tpu_custom_call" | custom-call | tf_op jit(solution)/shard_map/own_step/pallas_call | solution.py:226
  11.7 0.0 collective-permute-done.2.query_ref.mate_ref
  11.7 0.8 %mate_step.1.prior_ref = f32[8,128]{1,0:T(8,128)S(1)} custom-call(f32[2,4,128]{2,1,0:T(4,128)S(1)} %get-tuple-element.17.mask_ref, bf16[7,128,128]{2,1,0:T(8,128)(2,1)S(1)} %collective-permute-done.2.query_ref.mate_ref, f32[128,128]{1,0:T(8,128)S(1)} %get-tuple-element.18.refs_0_, f32[128,128]{1,0:T(8,128)S(1)} %get-tuple-element.19.refs_1_, ...), custom_call_target="tpu_custom_call" | custom-call | tf_op jit(solution)/shard_map/mate_step/pallas_call | solution.py:235
  12.5 0.0 copy-start
  12.5 0.6 %collective-permute-done.3.key_ref = bf16[128,128]{1,0:T(8,128)(2,1)S(1)} collective-permute-done((bf16[128,128]{1,0:T(8,128)(2,1)}, bf16[128,128]{1,0:T(8,128)(2,1)S(1)}, u32[]{:S(2)}, u32[]{:S(2)}) %collective-permute-start.3) | collective-permute-done | bytes 32800 | tf_op jit(solution)/shard_map/ppermute | solution.py:186
  13.1 0.6 %last.1.own_ref = bf16[16,128]{1,0:T(8,128)(2,1)S(1)} custom-call(f32[2,4,128]{2,1,0:T(4,128)S(1)} %get-tuple-element.17.mask_ref, f32[8,128]{1,0:T(8,128)S(1)} %mate_step.1.prior_ref, bf16[7,128,128]{2,1,0:T(8,128)(2,1)S(1)} %get-tuple-element.13.query_ref.own_ref, bf16[7,128,128]{2,1,0:T(8,128)(2,1)S(1)} %collective-permute-done.2.query_ref.mate_ref, ...), custom_call_target="tpu_custom_call" | custom-call | tf_op jit(solution)/shard_map/last/pallas_call | solution.py:243
  13.7 0.6 %collective-permute-start.4 = (bf16[16,128]{1,0:T(8,128)(2,1)S(1)}, bf16[16,128]{1,0:T(8,128)(2,1)S(1)}, u32[]{:S(2)}, u32[]{:S(2)}) collective-permute-start(bf16[16,128]{1,0:T(8,128)(2,1)S(1)} %last.1.own_ref), channel_id=1, source_target_pairs={{0,4},{4,0},{8,12},{12,8},{16,20},{20,16},{24,28},{28,24},{1,5},{5... | collective-permute-start | bytes 12296 | tf_op jit(solution)/shard_map/ppermute | solution.py:186
  14.3 3.1 %collective-permute-done.4.mate_ref = bf16[16,128]{1,0:T(8,128)(2,1)S(1)} collective-permute-done((bf16[16,128]{1,0:T(8,128)(2,1)S(1)}, bf16[16,128]{1,0:T(8,128)(2,1)S(1)}, u32[]{:S(2)}, u32[]{:S(2)}) %collective-permute-start.4) | collective-permute-done | bytes 4128 | tf_op jit(solution)/shard_map/ppermute | solution.py:186
  17.4 1.8 %collective-permute-start.8 = (bf16[160,128]{1,0:T(8,128)(2,1)S(1)}, bf16[160,128]{1,0:T(8,128)(2,1)S(1)}, u32[]{:S(2)}, u32[]{:S(2)}) collective-permute-start(bf16[160,128]{1,0:T(8,128)(2,1)S(1)} %pair.1.refs_0_), channel_id=1, source_target_pairs={{0,24},{4,28},{8,16},{12,20},{16,8},{20,12},{24,0},{28,4},{1,25},{... | collective-permute-start | bytes 122888 | tf_op jit(solution)/shard_map/ppermute | solution.py:186
  19.2 0.1 collective-permute-start.7
  19.3 2.5 %collective-permute-start.6 = (bf16[160,128]{1,0:T(8,128)(2,1)S(1)}, bf16[160,128]{1,0:T(8,128)(2,1)S(1)}, u32[]{:S(2)}, u32[]{:S(2)}) collective-permute-start(bf16[160,128]{1,0:T(8,128)(2,1)S(1)} %pair.1.refs_0_), channel_id=1, source_target_pairs={{0,8},{4,12},{8,0},{12,4},{16,24},{20,28},{24,16},{28,20},{1,9},{5... | collective-permute-start | bytes 122888 | tf_op jit(solution)/shard_map/ppermute | solution.py:186
  21.8 1.4 %collective-permute-done.8.refs_3_ = bf16[160,128]{1,0:T(8,128)(2,1)S(1)} collective-permute-done((bf16[160,128]{1,0:T(8,128)(2,1)S(1)}, bf16[160,128]{1,0:T(8,128)(2,1)S(1)}, u32[]{:S(2)}, u32[]{:S(2)}) %collective-permute-start.8) | collective-permute-done | bytes 40992 | tf_op jit(solution)/shard_map/ppermute | solution.py:186
  23.3 1.0 %collective-permute-done.7.refs_2_ = bf16[160,128]{1,0:T(8,128)(2,1)S(1)} collective-permute-done((bf16[160,128]{1,0:T(8,128)(2,1)S(1)}, bf16[160,128]{1,0:T(8,128)(2,1)S(1)}, u32[]{:S(2)}, u32[]{:S(2)}) %collective-permute-start.7) | collective-permute-done | bytes 40992 | tf_op jit(solution)/shard_map/ppermute | solution.py:186
  24.2 0.0 collective-permute-done.6.refs_1_
  24.3 1.4 %bank.1 = (bf16[7,128,512]{2,1,0:T(8,128)(2,1)}, bf16[64,128]{1,0:T(8,128)(2,1)}) custom-call(bf16[7,128,128]{2,1,0:T(8,128)(2,1)S(1)} %get-tuple-element.13.query_ref.own_ref, bf16[512,32]{1,0:T(8,128)(2,1)S(1)} %get-tuple-element.14.pick_ref, bf16[160,128]{1,0:T(8,128)(2,1)S(1)} %pair.1.refs_0_, bf16[160,128]{1,0:T(8,128)(2,1)S(1)} %collective-permute-done.6.refs_1_, ...), custom_call_target="tpu_custom_call" | custom-call | tf_op jit(solution)/shard_map/bank/pallas_call | solution.py:266
  (3 shorter events, 0.0 us)
Async XLA Ops:
  0.6 11.1 %collective-permute-start.2 = (bf16[7,128,128]{2,1,0:T(8,128)(2,1)}, bf16[7,128,128]{2,1,0:T(8,128)(2,1)S(1)}, u32[]{:S(2)}, u32[]{:S(2)}) collective-permute-start(bf16[7,128,128]{2,1,0:T(8,128)(2,1)} %bitcast.7), channel_id=1, source_target_pairs={{0,4},{4,0},{8,12},{12,8},{16,20},{20,16},{24,28},{28,24},{1,5},{5... | collective-permute-start | bytes 688136 | tf_op jit(solution)/shard_map/ppermute | solution.py:186
  3.7 6.0 %collective-permute-start = (bf16[128,128]{1,0:T(8,128)(2,1)}, bf16[128,128]{1,0:T(8,128)(2,1)S(1)}, u32[]{:S(2)}, u32[]{:S(2)}) collective-permute-start(bf16[128,128]{1,0:T(8,128)(2,1)} %bitcast.9), channel_id=1, source_target_pairs={{0,8},{4,12},{8,0},{12,4},{16,24},{20,28},{24,16},{28,20},{1,9},{5... | collective-permute-start | bytes 98312 | tf_op jit(solution)/shard_map/ppermute | solution.py:186
  5.2 6.1 %collective-permute-start.1 = (bf16[128,128]{1,0:T(8,128)(2,1)}, bf16[128,128]{1,0:T(8,128)(2,1)S(1)}, u32[]{:S(2)}, u32[]{:S(2)}) collective-permute-start(bf16[128,128]{1,0:T(8,128)(2,1)} %bitcast.10), channel_id=1, source_target_pairs={{0,24},{4,28},{8,16},{12,20},{16,8},{20,12},{24,0},{28,4},{1,25},{... | collective-permute-start | bytes 98312 | tf_op jit(solution)/shard_map/ppermute | solution.py:186
  7.7 5.4 %collective-permute-start.3 = (bf16[128,128]{1,0:T(8,128)(2,1)}, bf16[128,128]{1,0:T(8,128)(2,1)S(1)}, u32[]{:S(2)}, u32[]{:S(2)}) collective-permute-start(bf16[128,128]{1,0:T(8,128)(2,1)} %bitcast.11), channel_id=1, source_target_pairs={{0,16},{4,20},{8,24},{12,28},{16,0},{20,4},{24,8},{28,12},{1,17},{... | collective-permute-start | bytes 98312 | tf_op jit(solution)/shard_map/ppermute | solution.py:186
  7.8 6.5 %collective-permute-start.5 = (bf16[64,128]{1,0:T(8,128)(2,1)}, bf16[64,128]{1,0:T(8,128)(2,1)S(1)}, u32[]{:S(2)}, u32[]{:S(2)}) collective-permute-start(bf16[64,128]{1,0:T(8,128)(2,1)} %bitcast.5), channel_id=1, source_target_pairs={{0,4},{4,0},{8,12},{12,8},{16,20},{20,16},{24,28},{28,24},{1,5},{5... | collective-permute-start | bytes 49160 | tf_op jit(solution)/shard_map/ppermute | solution.py:186
  12.5 4.9 %copy-start = (bf16[64,1,128]{2,0,1:T(8,128)(2,1)S(1)}, bf16[64,1,128]{2,0,1:T(8,128)(2,1)}, u32[]{:S(2)}) copy-start(bf16[64,1,128]{2,0,1:T(8,128)(2,1)} %param.7) | copy-start | bytes 49156
  13.7 3.7 %collective-permute-start.4 = (bf16[16,128]{1,0:T(8,128)(2,1)S(1)}, bf16[16,128]{1,0:T(8,128)(2,1)S(1)}, u32[]{:S(2)}, u32[]{:S(2)}) collective-permute-start(bf16[16,128]{1,0:T(8,128)(2,1)S(1)} %last.1.own_ref), channel_id=1, source_target_pairs={{0,4},{4,0},{8,12},{12,8},{16,20},{20,16},{24,28},{28,24},{1,5},{5... | collective-permute-start | bytes 12296 | tf_op jit(solution)/shard_map/ppermute | solution.py:186
  17.4 5.9 %collective-permute-start.8 = (bf16[160,128]{1,0:T(8,128)(2,1)S(1)}, bf16[160,128]{1,0:T(8,128)(2,1)S(1)}, u32[]{:S(2)}, u32[]{:S(2)}) collective-permute-start(bf16[160,128]{1,0:T(8,128)(2,1)S(1)} %pair.1.refs_0_), channel_id=1, source_target_pairs={{0,24},{4,28},{8,16},{12,20},{16,8},{20,12},{24,0},{28,4},{1,25},{... | collective-permute-start | bytes 122888 | tf_op jit(solution)/shard_map/ppermute | solution.py:186
  19.2 5.0 %collective-permute-start.7 = (bf16[160,128]{1,0:T(8,128)(2,1)S(1)}, bf16[160,128]{1,0:T(8,128)(2,1)S(1)}, u32[]{:S(2)}, u32[]{:S(2)}) collective-permute-start(bf16[160,128]{1,0:T(8,128)(2,1)S(1)} %pair.1.refs_0_), channel_id=1, source_target_pairs={{0,16},{4,20},{8,24},{12,28},{16,0},{20,4},{24,8},{28,12},{1,17},{... | collective-permute-start | bytes 122888 | tf_op jit(solution)/shard_map/ppermute | solution.py:186
  19.3 4.9 %collective-permute-start.6 = (bf16[160,128]{1,0:T(8,128)(2,1)S(1)}, bf16[160,128]{1,0:T(8,128)(2,1)S(1)}, u32[]{:S(2)}, u32[]{:S(2)}) collective-permute-start(bf16[160,128]{1,0:T(8,128)(2,1)S(1)} %pair.1.refs_0_), channel_id=1, source_target_pairs={{0,8},{4,12},{8,0},{12,4},{16,24},{20,28},{24,16},{28,20},{1,9},{5... | collective-permute-start | bytes 122888 | tf_op jit(solution)/shard_map/ppermute | solution.py:186

commit v7 on v6

--- a/solution.py
+++ b/solution.py
@@ -29,6 +29,10 @@
 
 def key_order(parts):
     return sorted(range(1, parts), key=lambda k: (k % 2 == 0, k))
+
+
+def sum_order(parts):
+    return sorted(range(1, parts), key=lambda k: (k % 2 == 0, -k))
 
 
 def lead_rows(parts):
@@ -135,32 +139,65 @@
         pair_ref[pl.ds(pl.multiple_of(start + terms, PACK), rows), :] = cache_ref[...]
 
 
-def bank_kernel(parts, share, scale, query_ref, pick_ref, *refs):
-    pair_refs = refs[:parts]
-    rel_ref, bank_ref, base_ref, rel_work, bank_work, sems = refs[parts:]
+def pair_sums(parts, ref):
+    terms = term_rows(parts)
+    half = ref.shape[0] // 2
+    sums = []
+    for side in range(2):
+        wide = ref[pl.ds(side * half, terms), :].astype(jnp.float32)
+        sums.append(wide[:parts] + (wide[parts : 2 * parts] + wide[2 * parts : 3 * parts]))
+    return sums
+
+
+def pair_rows(parts, ref):
+    terms, half = term_rows(parts), ref.shape[0] // 2
+    return jnp.concatenate(
+        [ref[pl.ds(terms, half - terms), :], ref[pl.ds(half + terms, half - terms), :]], axis=0
+    )
+
+
+def prep_kernel(parts, members, pick_ref, *refs):
+    pair_refs = refs[: len(members)]
+    base_ref, keep_ref, sum_ref = refs[len(members) :]
+    here = lax.axis_index("seq") // 2
+    pick = pick_ref[...]
+    ones = jnp.ones((pick.shape[1], base_ref.shape[1]), jnp.bfloat16)
+    taken = jnp.dot(pick, ones, preferred_element_type=jnp.float32)
+    keep_ref[...] = (1.0 - taken).astype(jnp.bfloat16)
+    base_ref[...] = jnp.zeros_like(base_ref)
+    for index, (part, ref) in enumerate(zip(members, pair_refs)):
+        rows = pair_rows(parts, ref)
+        span = pl.ds(pl.multiple_of((here ^ part) * rows.shape[0], PACK), rows.shape[0])
+        base_ref[span, :] = rows * keep_ref[span, :]
+        for side, value in enumerate(pair_sums(parts, ref)):
+            sum_ref[index, side, pl.ds(0, parts), :] = value
+
+
+def bank_kernel(
+    parts, members, late, share, scale, query_ref, pick_ref, ready_ref, keep_ref, sum_ref, pair_ref,
+    rel_ref, bank_ref, base_ref, rel_work, bank_work, sems,
+):
     group = query_ref.shape[0]
     rows = bank_ref.shape[0]
-    lead, terms = lead_rows(parts), term_rows(parts)
+    lead = lead_rows(parts)
     me = lax.axis_index("seq")
+    base_ref[...] = ready_ref[...]
+    span = pl.ds(pl.multiple_of(((me // 2) ^ late) * 2 * rows, PACK), 2 * rows)
+    base_ref[span, :] = pair_rows(parts, pair_ref) * keep_ref[span, :]
     fresh = []
-    for side in range(2):
-        first = side * (terms + rows)
-        sums = []
-        for part, ref in enumerate(pair_refs):
-            wide = ref[pl.ds(first, terms), :].astype(jnp.float32)
-            sums.append(wide[:parts] + (wide[parts : 2 * parts] + wide[2 * parts : 3 * parts]))
-            start = pl.multiple_of((2 * ((me // 2) ^ part) + side) * rows, PACK)
-            base_ref[pl.ds(start, rows), :] = ref[pl.ds(first + terms, rows), :]
+    for side, last in enumerate(pair_sums(parts, pair_ref)):
+        sums = {late: last}
+        for index, part in enumerate(members):
+            sums[part] = sum_ref[index, side, pl.ds(0, parts), :]
+        sums = [sums[part] for part in range(parts)]
         while len(sums) > 1:
             sums = [left + right for left, right in zip(sums[::2], sums[1::2])]
         fresh.append(sums[0] * share)
         if lead > parts:
             fresh.append(jnp.zeros((lead - parts, fresh[0].shape[1]), jnp.float32))
     fresh = jnp.concatenate(fresh, axis=0).astype(jnp.bfloat16)
-    pick = pick_ref[...]
-    placed = jnp.dot(pick, fresh, preferred_element_type=jnp.float32)
-    taken = jnp.dot(pick, jnp.ones_like(fresh), preferred_element_type=jnp.float32)
-    bank = jnp.where(taken > 0.5, placed, base_ref[...].astype(jnp.float32)).astype(jnp.bfloat16)
+    placed = jnp.dot(pick_ref[...], fresh, preferred_element_type=jnp.float32)
+    bank = base_ref[...] + placed.astype(jnp.bfloat16)
     base_ref[...] = bank
     bank_work[...] = base_ref[pl.ds(pl.multiple_of(me * rows, PACK), rows), :]
     copies = [pltpu.make_async_copy(bank_work, bank_ref, sems.at[group])]
@@ -263,13 +300,27 @@
     for k in range(1, parts):
         pairs.append(swap(pair, 2 * k))
 
+    *members, late = [0, *sum_order(parts)]
+    ready, keep, sums = pl.pallas_call(
+        functools.partial(prep_kernel, parts, members),
+        out_shape=(
+            shape(count * rows, jnp.bfloat16),
+            shape(count * rows, jnp.bfloat16),
+            jax.ShapeDtypeStruct((len(members), 2, padded(parts, 8), head_dim), jnp.float32),
+        ),
+        in_specs=[VMEM] * (1 + len(members)),
+        out_specs=(VMEM,) * 3,
+        compiler_params=params,
+        name="prep",
+    )(pick, *[pairs[part] for part in members])
+
     relevance, bank = pl.pallas_call(
-        functools.partial(bank_kernel, parts, 1.0 / (group * WIN), score_scale),
+        functools.partial(bank_kernel, parts, members, late, 1.0 / (group * WIN), score_scale),
         out_shape=(
             jax.ShapeDtypeStruct((group, tok, count * rows), jnp.bfloat16),
             jax.ShapeDtypeStruct((rows, head_dim), jnp.bfloat16),
         ),
-        in_specs=[VMEM] * (2 + parts),
+        in_specs=[VMEM] * 6,
         out_specs=(HBM, HBM),
         scratch_shapes=[
             pltpu.VMEM((count * rows, head_dim), jnp.bfloat16),
@@ -279,7 +330,7 @@
         ],
         compiler_params=params,
         name="bank",
-    )(own, pick, *pairs)
+    )(own, pick, ready, keep, sums, pairs[late])
     return (relevance.transpose(1, 0, 2), bank[:, None, :])
 
 

time: 25.8 us -> 26.6 us (1.031)
  waiting for transfers between devices: 7.33 us -> 8.87 us
  starting transfers between devices: 12.8 us -> 11.9 us
    ppermute x9, waiting for transfers between devices: 7.33 us -> 8.87 us  [swap(): return lax.ppermute(value, 'seq', [(i, i ^ mask) for i in range(count)])]
    ppermute x9, starting transfers between devices: 12.8 us -> 11.9 us  [swap(): return lax.ppermute(value, 'seq', [(i, i ^ mask) for i in range(count)])]
    pallas_call x1 -> x2, Pallas kernels: 1.36 us -> 1.55 us  [the longest x1 1.37 us: per_device(): pl.pallas_call(functools.partial(bank_kernel, parts, members, late, 1.0 /...]
  transfers between devices with their start and end apart: 9 -> 9, of which waited for: 5 -> 6; matrix products, arithmetic and copies ran while one was open for 0% -> 0% of each run, Pallas kernels for 13% -> 14%
where the time goes in v7:
time: 26.6 us; the launch traced here: 26.5 us
  starting transfers between devices  11.9 us (45%)
  waiting for transfers between devices  8.87 us (33%)
  Pallas kernels  4.99 us (19%)
  between operations  0.7 us (3%)
    ppermute x9, starting transfers between devices, swap(): return lax.ppermute(value, 'seq', [(i, i ^ mask) for i in range(count)])  11.9 us
    ppermute x9, waiting for transfers between devices, swap(): return lax.ppermute(value, 'seq', [(i, i ^ mask) for i in range(count)])  8.87 us
    pallas_call x1, Pallas kernels, per_device(): pl.pallas_call(functools.partial(bank_kernel, parts, members, late, 1.0 /...  1.37 us
    pallas_call x1, Pallas kernels, per_device(): pl.pallas_call(functools.partial(first_kernel, parts, exp_scale), out_sha...  1.32 us
    pallas_call x1, Pallas kernels, per_device(): pl.pallas_call(functools.partial(mate_kernel, members, exp_scale), out_sh...  0.78 us
    pallas_call x2, Pallas kernels, per_device(): pl.pallas_call(functools.partial(own_kernel, k, exp_scale), out_shape=(sq...  0.72 us
    pallas_call x1, Pallas kernels, per_device(): pl.pallas_call(functools.partial(last_kernel, parts, tail, exp_scale), ou...  0.62 us
  transfers between devices with their start and end apart: 9, of which 6 were waited for; matrix products, arithmetic and copies ran while one was open for 0% of the time, Pallas kernels for 14%

profile of v7, /device:TPU:0, one launch (start us, length us, event | category | flops | bytes accessed | tf_op | source)
XLA Modules:
  0.0 26.5 jit_solution(637391495449248317)
XLA Ops:
  0.6 3.0 %collective-permute-start.2 = (bf16[7,128,128]{2,1,0:T(8,128)(2,1)}, bf16[7,128,128]{2,1,0:T(8,128)(2,1)S(1)}, u32[]{:S(2)}, u32[]{:S(2)}) collective-permute-start(bf16[7,128,128]{2,1,0:T(8,128)(2,1)} %bitcast.7), channel_id=1, source_target_pairs={{0,4},{4,0},{8,12},{12,8},{16,20},{20,16},{24,28},{28,24},{1,5},{5... | collective-permute-start | bytes 688136 | tf_op jit(solution)/shard_map/ppermute | solution.py:223
  3.7 1.6 %collective-permute-start = (bf16[128,128]{1,0:T(8,128)(2,1)}, bf16[128,128]{1,0:T(8,128)(2,1)S(1)}, u32[]{:S(2)}, u32[]{:S(2)}) collective-permute-start(bf16[128,128]{1,0:T(8,128)(2,1)} %bitcast.9), channel_id=1, source_target_pairs={{0,8},{4,12},{8,0},{12,4},{16,24},{20,28},{24,16},{28,20},{1,9},{5... | collective-permute-start | bytes 98312 | tf_op jit(solution)/shard_map/ppermute | solution.py:223
  5.2 2.5 %collective-permute-start.1 = (bf16[128,128]{1,0:T(8,128)(2,1)}, bf16[128,128]{1,0:T(8,128)(2,1)S(1)}, u32[]{:S(2)}, u32[]{:S(2)}) collective-permute-start(bf16[128,128]{1,0:T(8,128)(2,1)} %bitcast.10), channel_id=1, source_target_pairs={{0,24},{4,28},{8,16},{12,20},{16,8},{20,12},{24,0},{28,4},{1,25},{... | collective-permute-start | bytes 98312 | tf_op jit(solution)/shard_map/ppermute | solution.py:223
  7.7 0.1 collective-permute-start.3
  7.8 0.5 %collective-permute-start.5 = (bf16[64,128]{1,0:T(8,128)(2,1)}, bf16[64,128]{1,0:T(8,128)(2,1)S(1)}, u32[]{:S(2)}, u32[]{:S(2)}) collective-permute-start(bf16[64,128]{1,0:T(8,128)(2,1)} %bitcast.5), channel_id=1, source_target_pairs={{0,4},{4,0},{8,12},{12,8},{16,20},{20,16},{24,28},{28,24},{1,5},{5... | collective-permute-start | bytes 49160 | tf_op jit(solution)/shard_map/ppermute | solution.py:223
  8.4 1.3 %first.1 = (f32[128,128]{1,0:T(8,128)S(1)}, f32[2,4,128]{2,1,0:T(4,128)S(1)}, bf16[512,32]{1,0:T(8,128)(2,1)S(1)}, bf16[7,128,128]{2,1,0:T(8,128)(2,1)S(1)}, bf16[128,128]{1,0:T(8,128)(2,1)S(1)}) custom-call(s32[8]{0:T(128)} %start_hbm.1, s32[8]{0:T(128)} %slot_hbm.1, bf16[7,128,128]{2,1,0:T(8,128)(2,1)} %bitcast.8, bf16[128,128]{1,0:T(8,128)(2,1)} %bitcast.12), custom_call_target="tpu_custom_call" | custom-call | tf_op jit(solution)/shard_map/first/pallas_call | solution.py:241
  9.7 0.4 %own_step.2 = (f32[128,128]{1,0:T(8,128)S(1)}, f32[2,4,128]{2,1,0:T(4,128)S(1)}) custom-call(f32[2,4,128]{2,1,0:T(4,128)S(1)} %get-tuple-element.18.mask_ref, bf16[7,128,128]{2,1,0:T(8,128)(2,1)S(1)} %get-tuple-element.16.query_ref.own_ref, bf16[128,128]{1,0:T(8,128)(2,1)S(1)} %collective-permute-done.key_ref.refs_4_), custom_call_target="tpu_custom_call" | custom-call | tf_op jit(solution)/shard_map/own_step/pallas_call | solution.py:263
  10.1 1.3 %collective-permute-done.1.key_ref.refs_5_ = bf16[128,128]{1,0:T(8,128)(2,1)S(1)} collective-permute-done((bf16[128,128]{1,0:T(8,128)(2,1)}, bf16[128,128]{1,0:T(8,128)(2,1)S(1)}, u32[]{:S(2)}, u32[]{:S(2)}) %collective-permute-start.1) | collective-permute-done | bytes 32800 | tf_op jit(solution)/shard_map/ppermute | solution.py:223
  11.3 0.4 %own_step.3 = (f32[128,128]{1,0:T(8,128)S(1)}, f32[2,4,128]{2,1,0:T(4,128)S(1)}) custom-call(f32[2,4,128]{2,1,0:T(4,128)S(1)} %get-tuple-element.19.mask_ref, bf16[7,128,128]{2,1,0:T(8,128)(2,1)S(1)} %get-tuple-element.16.query_ref.own_ref, bf16[128,128]{1,0:T(8,128)(2,1)S(1)} %collective-permute-done.1.key_ref.refs_5_), custom_call_target="tpu_custom_call" | custom-call | tf_op jit(solution)/shard_map/own_step/pallas_call | solution.py:263
  11.7 0.8 %mate_step.1.prior_ref = f32[8,128]{1,0:T(8,128)S(1)} custom-call(f32[2,4,128]{2,1,0:T(4,128)S(1)} %get-tuple-element.20.mask_ref, bf16[7,128,128]{2,1,0:T(8,128)(2,1)S(1)} %collective-permute-done.2.query_ref.mate_ref, f32[128,128]{1,0:T(8,128)S(1)} %get-tuple-element.21.refs_0_, f32[128,128]{1,0:T(8,128)S(1)} %get-tuple-element.22.refs_1_, ...), custom_call_target="tpu_custom_call" | custom-call | tf_op jit(solution)/shard_map/mate_step/pallas_call | solution.py:272
  12.5 0.0 copy-start
  12.5 0.6 %collective-permute-done.3.key_ref = bf16[128,128]{1,0:T(8,128)(2,1)S(1)} collective-permute-done((bf16[128,128]{1,0:T(8,128)(2,1)}, bf16[128,128]{1,0:T(8,128)(2,1)S(1)}, u32[]{:S(2)}, u32[]{:S(2)}) %collective-permute-start.3) | collective-permute-done | bytes 32800 | tf_op jit(solution)/shard_map/ppermute | solution.py:223
  13.1 0.6 %last.1.own_ref = bf16[16,128]{1,0:T(8,128)(2,1)S(1)} custom-call(f32[2,4,128]{2,1,0:T(4,128)S(1)} %get-tuple-element.20.mask_ref, f32[8,128]{1,0:T(8,128)S(1)} %mate_step.1.prior_ref, bf16[7,128,128]{2,1,0:T(8,128)(2,1)S(1)} %get-tuple-element.16.query_ref.own_ref, bf16[7,128,128]{2,1,0:T(8,128)(2,1)S(1)} %collective-permute-done.2.query_ref.mate_ref, ...), custom_call_target="tpu_custom_call" | custom-call | tf_op jit(solution)/shard_map/last/pallas_call | solution.py:280
  13.7 0.6 %collective-permute-start.4 = (bf16[16,128]{1,0:T(8,128)(2,1)S(1)}, bf16[16,128]{1,0:T(8,128)(2,1)S(1)}, u32[]{:S(2)}, u32[]{:S(2)}) collective-permute-start(bf16[16,128]{1,0:T(8,128)(2,1)S(1)} %last.1.own_ref), channel_id=1, source_target_pairs={{0,4},{4,0},{8,12},{12,8},{16,20},{20,16},{24,28},{28,24},{1,5},{5... | collective-permute-start | bytes 12296 | tf_op jit(solution)/shard_map/ppermute | solution.py:223
  14.3 0.0 collective-permute-done.5.far_ref
  14.3 3.1 %collective-permute-done.4.mate_ref = bf16[16,128]{1,0:T(8,128)(2,1)S(1)} collective-permute-done((bf16[16,128]{1,0:T(8,128)(2,1)S(1)}, bf16[16,128]{1,0:T(8,128)(2,1)S(1)}, u32[]{:S(2)}, u32[]{:S(2)}) %collective-permute-start.4) | collective-permute-done | bytes 4128 | tf_op jit(solution)/shard_map/ppermute | solution.py:223
  17.4 0.5 %collective-permute-start.7 = (bf16[160,128]{1,0:T(8,128)(2,1)S(1)}, bf16[160,128]{1,0:T(8,128)(2,1)S(1)}, u32[]{:S(2)}, u32[]{:S(2)}) collective-permute-start(bf16[160,128]{1,0:T(8,128)(2,1)S(1)} %pair.1.refs_0_), channel_id=1, source_target_pairs={{0,8},{4,12},{8,0},{12,4},{16,24},{20,28},{24,16},{28,20},{1,9},{5... | collective-permute-start | bytes 122888 | tf_op jit(solution)/shard_map/ppermute | solution.py:223
  17.9 2.0 %collective-permute-start.6 = (bf16[160,128]{1,0:T(8,128)(2,1)S(1)}, bf16[160,128]{1,0:T(8,128)(2,1)S(1)}, u32[]{:S(2)}, u32[]{:S(2)}) collective-permute-start(bf16[160,128]{1,0:T(8,128)(2,1)S(1)} %pair.1.refs_0_), channel_id=1, source_target_pairs={{0,24},{4,28},{8,16},{12,20},{16,8},{20,12},{24,0},{28,4},{1,25},{... | collective-permute-start | bytes 122888 | tf_op jit(solution)/shard_map/ppermute | solution.py:223
  19.9 1.0 %collective-permute-start.8 = (bf16[160,128]{1,0:T(8,128)(2,1)S(1)}, bf16[160,128]{1,0:T(8,128)(2,1)S(1)}, u32[]{:S(2)}, u32[]{:S(2)}) collective-permute-start(bf16[160,128]{1,0:T(8,128)(2,1)S(1)} %pair.1.refs_0_), channel_id=1, source_target_pairs={{0,16},{4,20},{8,24},{12,28},{16,0},{20,4},{24,8},{28,12},{1,17},{... | collective-permute-start | bytes 122888 | tf_op jit(solution)/shard_map/ppermute | solution.py:223
  20.9 0.5 %collective-permute-done.7.refs_2_ = bf16[160,128]{1,0:T(8,128)(2,1)S(1)} collective-permute-done((bf16[160,128]{1,0:T(8,128)(2,1)S(1)}, bf16[160,128]{1,0:T(8,128)(2,1)S(1)}, u32[]{:S(2)}, u32[]{:S(2)}) %collective-permute-start.7) | collective-permute-done | bytes 40992 | tf_op jit(solution)/shard_map/ppermute | solution.py:223
  21.5 2.2 %collective-permute-done.6.refs_1_ = bf16[160,128]{1,0:T(8,128)(2,1)S(1)} collective-permute-done((bf16[160,128]{1,0:T(8,128)(2,1)S(1)}, bf16[160,128]{1,0:T(8,128)(2,1)S(1)}, u32[]{:S(2)}, u32[]{:S(2)}) %collective-permute-start.6) | collective-permute-done | bytes 40992 | tf_op jit(solution)/shard_map/ppermute | solution.py:223
  23.7 0.2 prep.1
  23.9 1.2 %collective-permute-done.8.pair_ref = bf16[160,128]{1,0:T(8,128)(2,1)S(1)} collective-permute-done((bf16[160,128]{1,0:T(8,128)(2,1)S(1)}, bf16[160,128]{1,0:T(8,128)(2,1)S(1)}, u32[]{:S(2)}, u32[]{:S(2)}) %collective-permute-start.8) | collective-permute-done | bytes 40992 | tf_op jit(solution)/shard_map/ppermute | solution.py:223
  25.1 1.4 %bank.1 = (bf16[7,128,512]{2,1,0:T(8,128)(2,1)}, bf16[64,128]{1,0:T(8,128)(2,1)}) custom-call(bf16[7,128,128]{2,1,0:T(8,128)(2,1)S(1)} %get-tuple-element.16.query_ref.own_ref, bf16[512,32]{1,0:T(8,128)(2,1)S(1)} %get-tuple-element.17.pick_ref, bf16[512,128]{1,0:T(8,128)(2,1)S(1)} %get-tuple-element.25.ready_ref, ...), custom_call_target="tpu_custom_call" | custom-call | tf_op jit(solution)/shard_map/bank/pallas_call | solution.py:317
  (4 shorter events, 0.0 us)
Async XLA Ops:
  0.6 11.1 %collective-permute-start.2 = (bf16[7,128,128]{2,1,0:T(8,128)(2,1)}, bf16[7,128,128]{2,1,0:T(8,128)(2,1)S(1)}, u32[]{:S(2)}, u32[]{:S(2)}) collective-permute-start(bf16[7,128,128]{2,1,0:T(8,128)(2,1)} %bitcast.7), channel_id=1, source_target_pairs={{0,4},{4,0},{8,12},{12,8},{16,20},{20,16},{24,28},{28,24},{1,5},{5... | collective-permute-start | bytes 688136 | tf_op jit(solution)/shard_map/ppermute | solution.py:223
  3.7 6.0 %collective-permute-start = (bf16[128,128]{1,0:T(8,128)(2,1)}, bf16[128,128]{1,0:T(8,128)(2,1)S(1)}, u32[]{:S(2)}, u32[]{:S(2)}) collective-permute-start(bf16[128,128]{1,0:T(8,128)(2,1)} %bitcast.9), channel_id=1, source_target_pairs={{0,8},{4,12},{8,0},{12,4},{16,24},{20,28},{24,16},{28,20},{1,9},{5... | collective-permute-start | bytes 98312 | tf_op jit(solution)/shard_map/ppermute | solution.py:223
  5.2 6.1 %collective-permute-start.1 = (bf16[128,128]{1,0:T(8,128)(2,1)}, bf16[128,128]{1,0:T(8,128)(2,1)S(1)}, u32[]{:S(2)}, u32[]{:S(2)}) collective-permute-start(bf16[128,128]{1,0:T(8,128)(2,1)} %bitcast.10), channel_id=1, source_target_pairs={{0,24},{4,28},{8,16},{12,20},{16,8},{20,12},{24,0},{28,4},{1,25},{... | collective-permute-start | bytes 98312 | tf_op jit(solution)/shard_map/ppermute | solution.py:223
  7.7 5.4 %collective-permute-start.3 = (bf16[128,128]{1,0:T(8,128)(2,1)}, bf16[128,128]{1,0:T(8,128)(2,1)S(1)}, u32[]{:S(2)}, u32[]{:S(2)}) collective-permute-start(bf16[128,128]{1,0:T(8,128)(2,1)} %bitcast.11), channel_id=1, source_target_pairs={{0,16},{4,20},{8,24},{12,28},{16,0},{20,4},{24,8},{28,12},{1,17},{... | collective-permute-start | bytes 98312 | tf_op jit(solution)/shard_map/ppermute | solution.py:223
  7.8 6.5 %collective-permute-start.5 = (bf16[64,128]{1,0:T(8,128)(2,1)}, bf16[64,128]{1,0:T(8,128)(2,1)S(1)}, u32[]{:S(2)}, u32[]{:S(2)}) collective-permute-start(bf16[64,128]{1,0:T(8,128)(2,1)} %bitcast.5), channel_id=1, source_target_pairs={{0,4},{4,0},{8,12},{12,8},{16,20},{20,16},{24,28},{28,24},{1,5},{5... | collective-permute-start | bytes 49160 | tf_op jit(solution)/shard_map/ppermute | solution.py:223
  12.5 4.9 %copy-start = (bf16[64,1,128]{2,0,1:T(8,128)(2,1)S(1)}, bf16[64,1,128]{2,0,1:T(8,128)(2,1)}, u32[]{:S(2)}) copy-start(bf16[64,1,128]{2,0,1:T(8,128)(2,1)} %param.7) | copy-start | bytes 49156
  13.7 3.7 %collective-permute-start.4 = (bf16[16,128]{1,0:T(8,128)(2,1)S(1)}, bf16[16,128]{1,0:T(8,128)(2,1)S(1)}, u32[]{:S(2)}, u32[]{:S(2)}) collective-permute-start(bf16[16,128]{1,0:T(8,128)(2,1)S(1)} %last.1.own_ref), channel_id=1, source_target_pairs={{0,4},{4,0},{8,12},{12,8},{16,20},{20,16},{24,28},{28,24},{1,5},{5... | collective-permute-start | bytes 12296 | tf_op jit(solution)/shard_map/ppermute | solution.py:223
  17.4 4.1 %collective-permute-start.7 = (bf16[160,128]{1,0:T(8,128)(2,1)S(1)}, bf16[160,128]{1,0:T(8,128)(2,1)S(1)}, u32[]{:S(2)}, u32[]{:S(2)}) collective-permute-start(bf16[160,128]{1,0:T(8,128)(2,1)S(1)} %pair.1.refs_0_), channel_id=1, source_target_pairs={{0,8},{4,12},{8,0},{12,4},{16,24},{20,28},{24,16},{28,20},{1,9},{5... | collective-permute-start | bytes 122888 | tf_op jit(solution)/shard_map/ppermute | solution.py:223
  17.9 5.8 %collective-permute-start.6 = (bf16[160,128]{1,0:T(8,128)(2,1)S(1)}, bf16[160,128]{1,0:T(8,128)(2,1)S(1)}, u32[]{:S(2)}, u32[]{:S(2)}) collective-permute-start(bf16[160,128]{1,0:T(8,128)(2,1)S(1)} %pair.1.refs_0_), channel_id=1, source_target_pairs={{0,24},{4,28},{8,16},{12,20},{16,8},{20,12},{24,0},{28,4},{1,25},{... | collective-permute-start | bytes 122888 | tf_op jit(solution)/shard_map/ppermute | solution.py:223
  19.9 5.2 %collective-permute-start.8 = (bf16[160,128]{1,0:T(8,128)(2,1)S(1)}, bf16[160,128]{1,0:T(8,128)(2,1)S(1)}, u32[]{:S(2)}, u32[]{:S(2)}) collective-permute-start(bf16[160,128]{1,0:T(8,128)(2,1)S(1)} %pair.1.refs_0_), channel_id=1, source_target_pairs={{0,16},{4,20},{8,24},{12,28},{16,0},{20,4},{24,8},{28,12},{1,17},{... | collective-permute-start | bytes 122888 | tf_op jit(solution)/shard_map/ppermute | solution.py:223

commit v8 on v7

--- a/solution.py
+++ b/solution.py
@@ -92,8 +92,7 @@
     total_ref[...] = column_sums(scale, query_ref, key_ref[...], mask_ref[0, pl.ds(here, 1), :])
 
 
-def own_kernel(part, scale, mask_ref, query_ref, key_ref, total_ref, pass_ref):
-    pass_ref[...] = mask_ref[...]
+def own_kernel(part, scale, mask_ref, query_ref, key_ref, total_ref):
     slot = (lax.axis_index("seq") // 2) ^ part
     inside = mask_ref[0, pl.ds(slot, 1), :]
     total_ref[...] = column_sums(scale, query_ref, key_ref[...], inside)
@@ -260,13 +259,12 @@
 
     *middle, tail = far
     for k in middle:
-        totals[k], inside = pl.pallas_call(
+        totals[k] = pl.pallas_call(
             functools.partial(own_kernel, k, exp_scale),
-            out_shape=(square, inside),
+            out_shape=square,
             in_specs=[VMEM] * 3,
-            out_specs=(VMEM, VMEM),
+            out_specs=VMEM,
             compiler_params=params,
-            name="own_step",
         )(inside, own, pieces[k])
     members = [0, *middle]
     partial = pl.pallas_call(

time: 26.6 us -> 26.9 us (1.011)
  transfers between devices with their start and end apart: 9 -> 9, of which waited for: 6 -> 5; matrix products, arithmetic and copies ran while one was open for 0% -> 0% of each run, Pallas kernels for 14% -> 14%
where the time goes in v8:
time: 26.9 us; the launch traced here: 26.7 us
  starting transfers between devices  11.9 us (44%)
  waiting for transfers between devices  9.08 us (34%)
  Pallas kernels  5 us (19%)
  between operations  0.71 us (3%)
    ppermute x9, starting transfers between devices, swap(): return lax.ppermute(value, 'seq', [(i, i ^ mask) for i in range(count)])  11.9 us
    ppermute x9, waiting for transfers between devices, swap(): return lax.ppermute(value, 'seq', [(i, i ^ mask) for i in range(count)])  9.08 us
    pallas_call x1, Pallas kernels, per_device(): pl.pallas_call(functools.partial(bank_kernel, parts, members, late, 1.0 /...  1.37 us
    pallas_call x1, Pallas kernels, per_device(): pl.pallas_call(functools.partial(first_kernel, parts, exp_scale), out_sha...  1.32 us
    pallas_call x1, Pallas kernels, per_device(): pl.pallas_call(functools.partial(mate_kernel, members, exp_scale), out_sh...  0.78 us
    pallas_call x2, Pallas kernels, per_device(): pl.pallas_call(functools.partial(own_kernel, k, exp_scale), out_shape=squ...  0.72 us
    pallas_call x1, Pallas kernels, per_device(): pl.pallas_call(functools.partial(last_kernel, parts, tail, exp_scale), ou...  0.62 us
  transfers between devices with their start and end apart: 9, of which 5 were waited for; matrix products, arithmetic and copies ran while one was open for 0% of the time, Pallas kernels for 14%

profile of v8, /device:TPU:0, one launch (start us, length us, event | category | flops | bytes accessed | tf_op | source)
XLA Modules:
  0.0 26.7 jit_solution(4412775801781134278)
XLA Ops:
  0.6 3.0 %collective-permute-start = (bf16[7,128,128]{2,1,0:T(8,128)(2,1)}, bf16[7,128,128]{2,1,0:T(8,128)(2,1)S(1)}, u32[]{:S(2)}, u32[]{:S(2)}) collective-permute-start(bf16[7,128,128]{2,1,0:T(8,128)(2,1)} %bitcast.7), channel_id=1, source_target_pairs={{0,4},{4,0},{8,12},{12,8},{16,20},{20,16},{24,28},{28,24},{1,5},{5... | collective-permute-start | bytes 688136 | tf_op jit(solution)/shard_map/ppermute | solution.py:222
  3.7 3.6 %collective-permute-start.2 = (bf16[128,128]{1,0:T(8,128)(2,1)}, bf16[128,128]{1,0:T(8,128)(2,1)S(1)}, u32[]{:S(2)}, u32[]{:S(2)}) collective-permute-start(bf16[128,128]{1,0:T(8,128)(2,1)} %bitcast.9), channel_id=1, source_target_pairs={{0,24},{4,28},{8,16},{12,20},{16,8},{20,12},{24,0},{28,4},{1,25},{... | collective-permute-start | bytes 98312 | tf_op jit(solution)/shard_map/ppermute | solution.py:222
  7.3 0.0 collective-permute-start.1
  7.3 0.8 %collective-permute-start.3 = (bf16[128,128]{1,0:T(8,128)(2,1)}, bf16[128,128]{1,0:T(8,128)(2,1)S(1)}, u32[]{:S(2)}, u32[]{:S(2)}) collective-permute-start(bf16[128,128]{1,0:T(8,128)(2,1)} %bitcast.11), channel_id=1, source_target_pairs={{0,16},{4,20},{8,24},{12,28},{16,0},{20,4},{24,8},{28,12},{1,17},{... | collective-permute-start | bytes 98312 | tf_op jit(solution)/shard_map/ppermute | solution.py:222
  8.1 0.3 %collective-permute-start.5 = (bf16[64,128]{1,0:T(8,128)(2,1)}, bf16[64,128]{1,0:T(8,128)(2,1)S(1)}, u32[]{:S(2)}, u32[]{:S(2)}) collective-permute-start(bf16[64,128]{1,0:T(8,128)(2,1)} %bitcast.5), channel_id=1, source_target_pairs={{0,4},{4,0},{8,12},{12,8},{16,20},{20,16},{24,28},{28,24},{1,5},{5... | collective-permute-start | bytes 49160 | tf_op jit(solution)/shard_map/ppermute | solution.py:222
  8.4 1.3 %first.1 = (f32[128,128]{1,0:T(8,128)S(1)}, f32[2,4,128]{2,1,0:T(4,128)S(1)}, bf16[512,32]{1,0:T(8,128)(2,1)S(1)}, bf16[7,128,128]{2,1,0:T(8,128)(2,1)S(1)}, bf16[128,128]{1,0:T(8,128)(2,1)S(1)}) custom-call(s32[8]{0:T(128)} %start_hbm.1, s32[8]{0:T(128)} %slot_hbm.1, bf16[7,128,128]{2,1,0:T(8,128)(2,1)} %bitcast.8, bf16[128,128]{1,0:T(8,128)(2,1)} %bitcast.12), custom_call_target="tpu_custom_call" | custom-call | tf_op jit(solution)/shard_map/first/pallas_call | solution.py:240
  9.7 0.4 %shard_map.69.refs_2_ = f32[128,128]{1,0:T(8,128)S(1)} custom-call(f32[2,4,128]{2,1,0:T(4,128)S(1)} %get-tuple-element.14.mask_ref, bf16[7,128,128]{2,1,0:T(8,128)(2,1)S(1)} %get-tuple-element.12.query_ref.own_ref, bf16[128,128]{1,0:T(8,128)(2,1)S(1)} %collective-permute-done.2.key_ref.refs_5_), custom_call_target="tpu_custom_call" | custom-call | tf_op jit(solution)/shard_map/pallas_call | solution.py:262
  10.1 1.3 %collective-permute-done.1.key_ref.refs_4_ = bf16[128,128]{1,0:T(8,128)(2,1)S(1)} collective-permute-done((bf16[128,128]{1,0:T(8,128)(2,1)}, bf16[128,128]{1,0:T(8,128)(2,1)S(1)}, u32[]{:S(2)}, u32[]{:S(2)}) %collective-permute-start.1) | collective-permute-done | bytes 32800 | tf_op jit(solution)/shard_map/ppermute | solution.py:222
  11.4 0.4 %shard_map.68.refs_1_ = f32[128,128]{1,0:T(8,128)S(1)} custom-call(f32[2,4,128]{2,1,0:T(4,128)S(1)} %get-tuple-element.14.mask_ref, bf16[7,128,128]{2,1,0:T(8,128)(2,1)S(1)} %get-tuple-element.12.query_ref.own_ref, bf16[128,128]{1,0:T(8,128)(2,1)S(1)} %collective-permute-done.1.key_ref.refs_4_), custom_call_target="tpu_custom_call" | custom-call | tf_op jit(solution)/shard_map/pallas_call | solution.py:262
  11.8 0.0 collective-permute-done.query_ref.mate_ref
  11.8 0.8 %mate_step.1.prior_ref = f32[8,128]{1,0:T(8,128)S(1)} custom-call(f32[2,4,128]{2,1,0:T(4,128)S(1)} %get-tuple-element.14.mask_ref, bf16[7,128,128]{2,1,0:T(8,128)(2,1)S(1)} %collective-permute-done.query_ref.mate_ref, f32[128,128]{1,0:T(8,128)S(1)} %get-tuple-element.15.refs_0_, f32[128,128]{1,0:T(8,128)S(1)} %shard_map.68.refs_1_, ...), custom_call_target="tpu_custom_call" | custom-call | tf_op jit(solution)/shard_map/mate_step/pallas_call | solution.py:270
  12.6 0.0 copy-start
  12.6 0.0 collective-permute-done.3.key_ref
  12.6 0.6 %last.1.own_ref = bf16[16,128]{1,0:T(8,128)(2,1)S(1)} custom-call(f32[2,4,128]{2,1,0:T(4,128)S(1)} %get-tuple-element.14.mask_ref, f32[8,128]{1,0:T(8,128)S(1)} %mate_step.1.prior_ref, bf16[7,128,128]{2,1,0:T(8,128)(2,1)S(1)} %get-tuple-element.12.query_ref.own_ref, bf16[7,128,128]{2,1,0:T(8,128)(2,1)S(1)} %collective-permute-done.query_ref.mate_ref, ...), custom_call_target="tpu_custom_call" | custom-call | tf_op jit(solution)/shard_map/last/pallas_call | solution.py:278
  13.2 0.6 %collective-permute-start.4 = (bf16[16,128]{1,0:T(8,128)(2,1)S(1)}, bf16[16,128]{1,0:T(8,128)(2,1)S(1)}, u32[]{:S(2)}, u32[]{:S(2)}) collective-permute-start(bf16[16,128]{1,0:T(8,128)(2,1)S(1)} %last.1.own_ref), channel_id=1, source_target_pairs={{0,4},{4,0},{8,12},{12,8},{16,20},{20,16},{24,28},{28,24},{1,5},{5... | collective-permute-start | bytes 12296 | tf_op jit(solution)/shard_map/ppermute | solution.py:222
  13.8 3.1 %collective-permute-done.4.mate_ref = bf16[16,128]{1,0:T(8,128)(2,1)S(1)} collective-permute-done((bf16[16,128]{1,0:T(8,128)(2,1)S(1)}, bf16[16,128]{1,0:T(8,128)(2,1)S(1)}, u32[]{:S(2)}, u32[]{:S(2)}) %collective-permute-start.4) | collective-permute-done | bytes 4128 | tf_op jit(solution)/shard_map/ppermute | solution.py:222
  16.9 1.8 %collective-permute-start.7 = (bf16[160,128]{1,0:T(8,128)(2,1)S(1)}, bf16[160,128]{1,0:T(8,128)(2,1)S(1)}, u32[]{:S(2)}, u32[]{:S(2)}) collective-permute-start(bf16[160,128]{1,0:T(8,128)(2,1)S(1)} %pair.1.refs_0_), channel_id=1, source_target_pairs={{0,8},{4,12},{8,0},{12,4},{16,24},{20,28},{24,16},{28,20},{1,9},{5... | collective-permute-start | bytes 122888 | tf_op jit(solution)/shard_map/ppermute | solution.py:222
  18.7 0.8 %collective-permute-start.6 = (bf16[160,128]{1,0:T(8,128)(2,1)S(1)}, bf16[160,128]{1,0:T(8,128)(2,1)S(1)}, u32[]{:S(2)}, u32[]{:S(2)}) collective-permute-start(bf16[160,128]{1,0:T(8,128)(2,1)S(1)} %pair.1.refs_0_), channel_id=1, source_target_pairs={{0,24},{4,28},{8,16},{12,20},{16,8},{20,12},{24,0},{28,4},{1,25},{... | collective-permute-start | bytes 122888 | tf_op jit(solution)/shard_map/ppermute | solution.py:222
  19.5 0.9 %collective-permute-start.8 = (bf16[160,128]{1,0:T(8,128)(2,1)S(1)}, bf16[160,128]{1,0:T(8,128)(2,1)S(1)}, u32[]{:S(2)}, u32[]{:S(2)}) collective-permute-start(bf16[160,128]{1,0:T(8,128)(2,1)S(1)} %pair.1.refs_0_), channel_id=1, source_target_pairs={{0,16},{4,20},{8,24},{12,28},{16,0},{20,4},{24,8},{28,12},{1,17},{... | collective-permute-start | bytes 122888 | tf_op jit(solution)/shard_map/ppermute | solution.py:222
  20.4 0.6 %collective-permute-done.7.refs_2_ = bf16[160,128]{1,0:T(8,128)(2,1)S(1)} collective-permute-done((bf16[160,128]{1,0:T(8,128)(2,1)S(1)}, bf16[160,128]{1,0:T(8,128)(2,1)S(1)}, u32[]{:S(2)}, u32[]{:S(2)}) %collective-permute-start.7) | collective-permute-done | bytes 40992 | tf_op jit(solution)/shard_map/ppermute | solution.py:222
  21.1 3.5 %collective-permute-done.6.refs_1_ = bf16[160,128]{1,0:T(8,128)(2,1)S(1)} collective-permute-done((bf16[160,128]{1,0:T(8,128)(2,1)S(1)}, bf16[160,128]{1,0:T(8,128)(2,1)S(1)}, u32[]{:S(2)}, u32[]{:S(2)}) %collective-permute-start.6) | collective-permute-done | bytes 40992 | tf_op jit(solution)/shard_map/ppermute | solution.py:222
  24.6 0.2 prep.1
  24.8 0.5 %collective-permute-done.8.pair_ref = bf16[160,128]{1,0:T(8,128)(2,1)S(1)} collective-permute-done((bf16[160,128]{1,0:T(8,128)(2,1)S(1)}, bf16[160,128]{1,0:T(8,128)(2,1)S(1)}, u32[]{:S(2)}, u32[]{:S(2)}) %collective-permute-start.8) | collective-permute-done | bytes 40992 | tf_op jit(solution)/shard_map/ppermute | solution.py:222
  25.3 1.4 %bank.1 = (bf16[7,128,512]{2,1,0:T(8,128)(2,1)}, bf16[64,128]{1,0:T(8,128)(2,1)}) custom-call(bf16[7,128,128]{2,1,0:T(8,128)(2,1)S(1)} %get-tuple-element.12.query_ref.own_ref, bf16[512,32]{1,0:T(8,128)(2,1)S(1)} %get-tuple-element.13.pick_ref, bf16[512,128]{1,0:T(8,128)(2,1)S(1)} %get-tuple-element.17.ready_ref, ...), custom_call_target="tpu_custom_call" | custom-call | tf_op jit(solution)/shard_map/bank/pallas_call | solution.py:315
  (4 shorter events, 0.0 us)
Async XLA Ops:
  0.6 11.1 %collective-permute-start = (bf16[7,128,128]{2,1,0:T(8,128)(2,1)}, bf16[7,128,128]{2,1,0:T(8,128)(2,1)S(1)}, u32[]{:S(2)}, u32[]{:S(2)}) collective-permute-start(bf16[7,128,128]{2,1,0:T(8,128)(2,1)} %bitcast.7), channel_id=1, source_target_pairs={{0,4},{4,0},{8,12},{12,8},{16,20},{20,16},{24,28},{28,24},{1,5},{5... | collective-permute-start | bytes 688136 | tf_op jit(solution)/shard_map/ppermute | solution.py:222
  3.7 6.0 %collective-permute-start.2 = (bf16[128,128]{1,0:T(8,128)(2,1)}, bf16[128,128]{1,0:T(8,128)(2,1)S(1)}, u32[]{:S(2)}, u32[]{:S(2)}) collective-permute-start(bf16[128,128]{1,0:T(8,128)(2,1)} %bitcast.9), channel_id=1, source_target_pairs={{0,24},{4,28},{8,16},{12,20},{16,8},{20,12},{24,0},{28,4},{1,25},{... | collective-permute-start | bytes 98312 | tf_op jit(solution)/shard_map/ppermute | solution.py:222
  7.3 4.1 %collective-permute-start.1 = (bf16[128,128]{1,0:T(8,128)(2,1)}, bf16[128,128]{1,0:T(8,128)(2,1)S(1)}, u32[]{:S(2)}, u32[]{:S(2)}) collective-permute-start(bf16[128,128]{1,0:T(8,128)(2,1)} %bitcast.10), channel_id=1, source_target_pairs={{0,8},{4,12},{8,0},{12,4},{16,24},{20,28},{24,16},{28,20},{1,9},{5... | collective-permute-start | bytes 98312 | tf_op jit(solution)/shard_map/ppermute | solution.py:222
  7.3 5.3 %collective-permute-start.3 = (bf16[128,128]{1,0:T(8,128)(2,1)}, bf16[128,128]{1,0:T(8,128)(2,1)S(1)}, u32[]{:S(2)}, u32[]{:S(2)}) collective-permute-start(bf16[128,128]{1,0:T(8,128)(2,1)} %bitcast.11), channel_id=1, source_target_pairs={{0,16},{4,20},{8,24},{12,28},{16,0},{20,4},{24,8},{28,12},{1,17},{... | collective-permute-start | bytes 98312 | tf_op jit(solution)/shard_map/ppermute | solution.py:222
  8.1 5.7 %collective-permute-start.5 = (bf16[64,128]{1,0:T(8,128)(2,1)}, bf16[64,128]{1,0:T(8,128)(2,1)S(1)}, u32[]{:S(2)}, u32[]{:S(2)}) collective-permute-start(bf16[64,128]{1,0:T(8,128)(2,1)} %bitcast.5), channel_id=1, source_target_pairs={{0,4},{4,0},{8,12},{12,8},{16,20},{20,16},{24,28},{28,24},{1,5},{5... | collective-permute-start | bytes 49160 | tf_op jit(solution)/shard_map/ppermute | solution.py:222
  12.6 4.3 %copy-start = (bf16[64,1,128]{2,0,1:T(8,128)(2,1)S(1)}, bf16[64,1,128]{2,0,1:T(8,128)(2,1)}, u32[]{:S(2)}) copy-start(bf16[64,1,128]{2,0,1:T(8,128)(2,1)} %param.7) | copy-start | bytes 49156
  13.2 3.7 %collective-permute-start.4 = (bf16[16,128]{1,0:T(8,128)(2,1)S(1)}, bf16[16,128]{1,0:T(8,128)(2,1)S(1)}, u32[]{:S(2)}, u32[]{:S(2)}) collective-permute-start(bf16[16,128]{1,0:T(8,128)(2,1)S(1)} %last.1.own_ref), channel_id=1, source_target_pairs={{0,4},{4,0},{8,12},{12,8},{16,20},{20,16},{24,28},{28,24},{1,5},{5... | collective-permute-start | bytes 12296 | tf_op jit(solution)/shard_map/ppermute | solution.py:222
  16.9 4.2 %collective-permute-start.7 = (bf16[160,128]{1,0:T(8,128)(2,1)S(1)}, bf16[160,128]{1,0:T(8,128)(2,1)S(1)}, u32[]{:S(2)}, u32[]{:S(2)}) collective-permute-start(bf16[160,128]{1,0:T(8,128)(2,1)S(1)} %pair.1.refs_0_), channel_id=1, source_target_pairs={{0,8},{4,12},{8,0},{12,4},{16,24},{20,28},{24,16},{28,20},{1,9},{5... | collective-permute-start | bytes 122888 | tf_op jit(solution)/shard_map/ppermute | solution.py:222
  18.7 5.9 %collective-permute-start.6 = (bf16[160,128]{1,0:T(8,128)(2,1)S(1)}, bf16[160,128]{1,0:T(8,128)(2,1)S(1)}, u32[]{:S(2)}, u32[]{:S(2)}) collective-permute-start(bf16[160,128]{1,0:T(8,128)(2,1)S(1)} %pair.1.refs_0_), channel_id=1, source_target_pairs={{0,24},{4,28},{8,16},{12,20},{16,8},{20,12},{24,0},{28,4},{1,25},{... | collective-permute-start | bytes 122888 | tf_op jit(solution)/shard_map/ppermute | solution.py:222
  19.5 5.8 %collective-permute-start.8 = (bf16[160,128]{1,0:T(8,128)(2,1)S(1)}, bf16[160,128]{1,0:T(8,128)(2,1)S(1)}, u32[]{:S(2)}, u32[]{:S(2)}) collective-permute-start(bf16[160,128]{1,0:T(8,128)(2,1)S(1)} %pair.1.refs_0_), channel_id=1, source_target_pairs={{0,16},{4,20},{8,24},{12,28},{16,0},{20,4},{24,8},{28,12},{1,17},{... | collective-permute-start | bytes 122888 | tf_op jit(solution)/shard_map/ppermute | solution.py:222
